TPU v7x, 256 devices: a whole 4x4x8 slice. The times are simulated.
256 devices in a mesh: rows: 32 (over y, x, core), feat: 8 (over z).
Axes of the slice: x: 4, y: 4, z: 8, core: 2. Of those that a mesh axis runs over, the one named last changes fastest.
Arguments:
- features: bfloat16 [32768, 2048], P('rows', 'feat'), may hold values from -6 to 6
- grad_out: bfloat16 [32768, 2048], P('rows', 'feat'), may hold values from -6 to 6
- eigvecs: float32 [2048, 2048], P('feat', 'rows'), may hold values from -1 to 1, as said below
- eigvals: float32 [2048], replicated, may hold values from 0.1 to 1, as said below
- whiten: bfloat16 [2048, 2048], P(None, 'feat'), may hold values from -0.125 to 0.125
Outputs:
- grad_in: bfloat16 [32768, 2048], P('rows', 'feat')
Inputs may be any that keep to these rules, and one draw needn't show every extreme that they name: `eigvecs`: the columns are orthonormal. `eigvals`: any two entries differ by at least 0.45 / 2048.
All inputs are finite; a program needn't handle non-finite values.
Results may differ from a plain program's by a relative error of at most 0.0074.
Values may be sent and summed in bfloat16 or wider, within the bound.
No kernel may reach another device: no remote copies, remote signals or barrier semaphores. Data moves between devices by JAX's collectives and lax.ppermute only.
A program may use at most 128 MiB of HBM per device.

v0:
```python
import jax
import jax.numpy as jnp
from jax import lax
from jax.sharding import PartitionSpec as P


def side_by_side(arrays, axis, dim, along):
    ends, at = ([], 0)
    for a in arrays[:-1]:
        at += a.shape[along]
        ends.append(at)
    both = jnp.concatenate(arrays, axis=along)
    return tuple(jnp.split(lax.all_gather(both, axis, axis=dim, tiled=True), ends, axis=along))


def copy_for_each(shard, axis):
    copies = jnp.broadcast_to(shard, (lax.axis_size(axis), *shard.shape))
    return lax.all_to_all(copies, axis, split_axis=0, concat_axis=0, tiled=True)


def laid_out(parts, dim):
    parts = jnp.moveaxis(parts, 0, dim)
    lengths = parts.shape
    return parts.reshape(*lengths[:dim], lengths[dim] * lengths[dim + 1], *lengths[dim + 2 :])


def collect(shard, axis, dim):
    parts = copy_for_each(shard, axis)
    return laid_out(parts, dim)


def of_everyone(shard, axis):
    everything = copy_for_each(shard, axis)
    return jnp.sum(everything.astype(jnp.float32), axis=0)


def split_up(shard, dim, peers):
    before, after = (shard.shape[:dim], shard.shape[dim + 1 :])
    return jnp.moveaxis(shard.reshape(*before, peers, -1, *after), dim, 0)


def summed_on_arrival(shard, axis, dim):
    peers = lax.axis_size(axis)
    parts = lax.all_to_all(split_up(shard, dim, peers), axis, 0, 0, tiled=True)
    return jnp.sum(parts.astype(jnp.float32), axis=0)


def divided(lam_row, lam_col, first_col):
    on_diag = (
        jnp.arange(lam_row.shape[0], dtype=jnp.int32)[:, None]
        == (first_col + jnp.arange(lam_col.shape[0], dtype=jnp.int32))[None, :]
    )
    root_row = lam_row ** (-0.5)
    root_col = lam_col ** (-0.5)
    gaps_lam = lam_row[:, None] - lam_col[None, :]
    safe_gap = jnp.where(on_diag, jnp.ones_like(gaps_lam), gaps_lam)
    off_diag = (root_row[:, None] - root_col[None, :]) / safe_gap
    diag_vals = -0.5 * lam_row[:, None] ** (-1.5) + jnp.zeros_like(gaps_lam)
    return jnp.where(on_diag, diag_vals, off_diag)


def local(features, grad_out, eigvecs, eigvals, whiten):
    highest = lax.Precision.HIGHEST
    tok_rows, own_cols = features.shape
    row_count = tok_rows * lax.axis_size("rows")
    contract_rows = (((0,), (0,)), ((), ()))
    contract_last = (((1,), (1,)), ((), ()))
    piece_x, piece_g = side_by_side((features, grad_out), "feat", 1, 0)
    left_part = lax.dot_general(
        features, piece_g, contract_rows, preferred_element_type=jnp.float32
    )
    right_part = lax.dot_general(
        grad_out, piece_x, contract_rows, preferred_element_type=jnp.float32
    )
    cross_one = left_part
    cross_two = right_part
    sum_x = jnp.sum(piece_x, axis=0, dtype=jnp.float32)
    sum_g = jnp.sum(piece_g, axis=0, dtype=jnp.float32)
    cross_one, cross_two, sum_x, sum_g = (cross_one, cross_two, sum_x, sum_g)
    cross_one, cross_two, sum_x, sum_g = lax.psum((cross_one, cross_two, sum_x, sum_g), "rows")
    both_cross = cross_one + cross_two
    col_mean = sum_x / row_count
    grad_mean = sum_g / row_count
    offset = lax.axis_index("feat") * own_cols
    mean_part = lax.dynamic_slice_in_dim(col_mean, offset, own_cols)
    grad_part = lax.dynamic_slice_in_dim(grad_mean, offset, own_cols)
    sym_gram = 0.5 * (
        both_cross
        - row_count
        * (mean_part[:, None] * grad_mean[None, :] + grad_part[:, None] * col_mean[None, :])
    )
    basis_cols = collect(eigvecs, "feat", 0)
    basis_block = collect(eigvecs, "rows", 1)
    narrow = basis_cols.shape[1]
    inner_prod = jnp.dot(sym_gram, basis_cols, precision=highest)
    partial_value = lax.dot_general(basis_block, inner_prod, contract_rows, precision=highest)
    rotated = of_everyone(partial_value.astype(jnp.bfloat16), "feat").astype(jnp.float32)
    first_col = lax.axis_index("rows") * narrow
    lam_col = lax.dynamic_slice_in_dim(eigvals, first_col, narrow)
    scaled = divided(eigvals, lam_col, first_col) * rotated
    back_rot = jnp.dot(basis_block, scaled, precision=highest)
    sens_own = summed_on_arrival(
        lax.dot_general(back_rot, basis_cols, contract_last, precision=highest).astype(
            jnp.bfloat16
        ),
        "rows",
        0,
    )
    scaled_own = (2.0 / row_count * sens_own).astype(jnp.bfloat16)
    sens_scaled = collect(scaled_own, "rows", 0)
    piece_x, piece_g = side_by_side((features, grad_out), "feat", 1, 0)
    shifted = (piece_g.astype(jnp.float32) - grad_mean).astype(jnp.bfloat16)
    centered = (piece_x.astype(jnp.float32) - col_mean).astype(jnp.bfloat16)
    running = jnp.dot(shifted, whiten, preferred_element_type=jnp.float32)
    grad_in = running + lax.dot_general(
        centered, sens_scaled, contract_last, preferred_element_type=jnp.float32
    )
    return grad_in.astype(jnp.bfloat16)


def solution(mesh):
    in_specs = (P("rows", "feat"), P("rows", "feat"), P("feat", "rows"), P(), P(None, "feat"))
    out_specs = P("rows", "feat")
    return jax.shard_map(local, mesh=mesh, in_specs=in_specs, out_specs=out_specs, check_vma=False)
```

profile of v0, /device:TPU:1, one launch (start us, length us, event | category | flops | bytes accessed | tf_op | source)
XLA Modules:
  0.0 375.5 jit_solution(18292856345036790117)
XLA Ops:
  6.5 2.4 pad_maximum_fusion
  8.9 0.0 all-gather.2.cloned.1.call-update
  9.0 27.7 %all_to_all.25 = f32[8,256,64]{1,2,0:T(8,128)} all-to-all(f32[8,256,64]{1,2,0:T(8,128)S(1)} %broadcast_in_dim.11), channel_id=1, replica_groups=mesh['rows'=32,'feat'=8] {'feat'}, dimensions={0} | all-to-all | bytes 1048576 | tf_op jit(solution)/shard_map/all_to_all | solution.py:18
  36.7 1.6 broadcast_in_dim.12
  38.3 10.4 %all-to-all-start.1 = ((f32[32,256,64]{1,2,0:T(8,128)}), f32[32,256,64]{1,2,0:T(8,128)S(1)}, u32[]{:S(2)}, u32[]{:S(2)}) async-start(f32[32,256,64]{1,2,0:T(8,128)} %broadcast_in_dim.12), calls=%async_computation.1 | async-start | bytes 4194304 | tf_op jit(solution)/shard_map/all_to_all | solution.py:18
  48.7 0.0 all-reduce.3.cloned.1.call-start
  48.8 66.8 %all-gather.2.cloned.1.call-done = bf16[2048,2048]{1,0:T(8,128)(2,1)} async-done(((bf16[2048,256]{1,0:T(8,128)(2,1)}), bf16[2048,2048]{1,0:T(8,128)(2,1)}) %all-gather.2.cloned.1.call-update) | async-done | bytes 8388624 | tf_op jit(solution)/shard_map/all_gather | solution.py:13
  115.6 3.8 %fusion.9 = f32[2048,256]{1,0:T(8,128)S(1)} fusion(bf16[1024,256]{1,0:T(8,128)(2,1)} %param.6, bf16[2048,2048]{1,0:T(8,128)(2,1)} %all-gather.2.cloned.1.call-done), kind=kOutput, calls=%fused_computation.12 | convolution fusion | flops 1073741824 | bytes 6815744 | tf_op jit(solution)/shard_map/dot_general | solution.py:72
  119.4 1.0 copy-done.1
  120.4 0.0 copy-done.5
  120.4 2.7 fusion.17
  123.2 1.9 copy.13
  125.1 4.3 %convert_reduce_fusion.1 = (f32[2048]{0:T(1024)S(1)}, f32[2048]{0:T(1024)S(1)}) fusion(bf16[2048,2048]{1,0:T(8,128)(2,1)} %all-gather.2.cloned.1.call-done), kind=kLoop, calls=%fused_computation.3 | loop fusion | flops 8384512 | bytes 8404992 | tf_op jit(solution)/shard_map/reduce_sum | solution.py:78
  129.3 123.8 %all-reduce = (f32[2048]{0:T(1024)S(1)}, f32[2048]{0:T(1024)S(1)}) all-reduce(f32[2048]{0:T(1024)S(1)} %get-tuple-element.6, f32[2048]{0:T(1024)S(1)} %get-tuple-element.5), channel_id=1, replica_groups=mesh['rows'=32,'feat'=8] {'rows'}, use_global_device_ids=true, to_apply=%region_3.0 | all-reduce | flops 4096 | bytes 32768 | tf_op jit(solution)/shard_map/psum | solution.py:80
  253.2 0.1 dynamic_slice.10
  253.3 0.1 dynamic_slice.11
  253.3 3.5 fusion.22
  256.9 2.1 fusion.21
  259.0 1.6 broadcast_in_dim.13
  260.6 3.7 all-to-all-start.2
  264.4 0.1 broadcast_power_fusion.1
  264.5 47.3 %all-to-all-done.2 = bf16[8,2048,64]{1,2,0:T(8,128)(2,1)S(1)} async-done(((bf16[8,2048,64]{1,2,0:T(8,128)(2,1)}), bf16[8,2048,64]{1,2,0:T(8,128)(2,1)S(1)}, u32[]{:S(2)}, u32[]{:S(2)}) %all-to-all-start.2) | async-done | bytes 2097184 | tf_op jit(solution)/shard_map/all_to_all | solution.py:18
  311.8 0.3 convert_reduce_fusion.2
  312.1 1.2 copy-done.3
  313.3 1.2 fusion.42
  314.6 1.8 fusion.20
  316.4 25.3 %all_to_all.26 = bf16[32,8,2048]{2,1,0:T(8,128)(2,1)S(1)} all-to-all(bf16[32,8,2048]{2,1,0:T(8,128)(2,1)S(1)} %fusion.20), channel_id=1, replica_groups=mesh['rows'=32,'feat'=8] {'rows'}, dimensions={0} | all-to-all | bytes 2097152 | tf_op jit(solution)/shard_map/all_to_all | solution.py:44
  341.7 0.2 convert_reduce_fusion.3
  341.9 0.1 broadcast_in_dim.14
  342.0 20.9 %all_to_all.27 = bf16[32,8,2048]{2,1,0:T(8,128)(2,1)S(1)} all-to-all(bf16[32,8,2048]{2,1,0:T(8,128)(2,1)S(1)} %broadcast_in_dim.14), channel_id=1, replica_groups=mesh['rows'=32,'feat'=8] {'rows'}, dimensions={0} | all-to-all | bytes 2097152 | tf_op jit(solution)/shard_map/all_to_all | solution.py:18
  363.0 3.6 fusion.2
  366.6 2.1 fusion.32
  (28 shorter events, 0.1 us)
Async XLA Ops:
  6.5 360.1 %copy-start = (bf16[2048,256]{1,0:T(8,128)(2,1)S(1)}, bf16[2048,256]{1,0:T(8,128)(2,1)}, u32[]{:S(2)}) copy-start(bf16[2048,256]{1,0:T(8,128)(2,1)} %param.9) | copy-start | bytes 3145732
  6.5 2.4 copy-start.6
  6.5 109.0 %all-gather.2.cloned.1.call-start = ((), (), s32[]{:S(2)}) async-start(), calls=%async_computation.5 | async-start | bytes 9437184 | tf_op jit(solution)/shard_map/all_gather | solution.py:13
  38.3 218.6 %all-to-all-start.1 = ((f32[32,256,64]{1,2,0:T(8,128)}), f32[32,256,64]{1,2,0:T(8,128)S(1)}, u32[]{:S(2)}, u32[]{:S(2)}) async-start(f32[32,256,64]{1,2,0:T(8,128)} %broadcast_in_dim.12), calls=%async_computation.1 | async-start | bytes 4194304 | tf_op jit(solution)/shard_map/all_to_all | solution.py:18
  48.7 204.6 %all-reduce.3.cloned.1.call-start = ((), (), s32[]{:S(2)}) async-start(), calls=%async_computation.6 | async-start | bytes 4194304 | tf_op jit(solution)/shard_map/psum | solution.py:80
  115.6 4.8 %copy-start.1 = (bf16[2048,2048]{1,0:T(8,128)(2,1)S(1)}, bf16[2048,2048]{1,0:T(8,128)(2,1)}, u32[]{:S(2)}) copy-start(bf16[2048,2048]{1,0:T(8,128)(2,1)} %all-gather.2.cloned.1.call-done) | copy-start | bytes 25165828
  115.6 4.8 %copy-start.5 = (bf16[1024,256]{1,0:T(8,128)(2,1)S(1)}, bf16[1024,256]{1,0:T(8,128)(2,1)}, u32[]{:S(2)}) copy-start(bf16[1024,256]{1,0:T(8,128)(2,1)} %param.5) | copy-start | bytes 1572868
  256.9 3.7 copy-start.2
  260.6 3.8 %copy-start.7 = (f32[2048]{0:T(1024)S(1)}, f32[2048]{0:T(1024)}, u32[]{:S(2)}) copy-start(f32[2048]{0:T(1024)} %param.8) | copy-start | bytes 24580
  260.6 51.1 %all-to-all-start.2 = ((bf16[8,2048,64]{1,2,0:T(8,128)(2,1)}), bf16[8,2048,64]{1,2,0:T(8,128)(2,1)S(1)}, u32[]{:S(2)}, u32[]{:S(2)}) async-start(bf16[8,2048,64]{1,2,0:T(8,128)(2,1)} %broadcast_in_dim.13), calls=%async_computation.2 | async-start | bytes 4194304 | tf_op jit(solution)/shard_map/all_to_all | solution.py:18
  311.8 1.6 copy-start.3
  312.1 2.4 copy-start.4
  342.0 24.6 %slice-start = ((s8[8388608]{0:T(1024)(128)(4,1)}), s8[4194304]{0:T(1024)(128)(4,1)S(1)}, s32[]{:S(2)}) async-start(s8[8388608]{0:T(1024)(128)(4,1)} %bitcast.23), calls=%async_computation.7 | async-start | bytes 8388608
  363.0 3.7 slice-start.1
Sparse Core Ops, SparseCore 0:
  9.0 106.4 all-gather.1
  123.3 119.2 all-reduce.2
where the time goes:
time: 376 us
  blocking collectives  198 us (53%)
  waiting for transfers between devices  114 us (30%)
  matrix products  20.9 us (6%)
  starting transfers between devices  14.2 us (4%)
  between operations  13.6 us (4%)
  local copies, waits for them, and re-layouts  7.75 us (2%)
  other arithmetic  7.15 us (2%)
    psum x1, blocking collectives, local(): lax.psum((cross_one, cross_two, sum_x, sum_g), 'rows')  124 us
    all_gather x1, waiting for transfers between devices, side_by_side(): lax.all_gather(both, axis, axis=dim, tiled=True)  66.8 us
    all_to_all x2, blocking collectives, copy_for_each(): return lax.all_to_all(copies, axis, split_axis=0, concat_axis=0, tiled=True)  48.6 us
    all_to_all x2, waiting for transfers between devices, copy_for_each(): return lax.all_to_all(copies, axis, split_axis=0, concat_axis=0, tiled=True)  47.3 us
    all_to_all x1, blocking collectives, summed_on_arrival(): parts = lax.all_to_all(split_up(shard, dim, peers), axis, 0, 0, tiled=True)  25.3 us
    all_to_all x2, starting transfers between devices, copy_for_each(): return lax.all_to_all(copies, axis, split_axis=0, concat_axis=0, tiled=True)  14.2 us
  transfers between devices with their start and end apart: 4, of which 2 were waited for; matrix products, arithmetic and copies ran while one was open for 5% of the time, Pallas kernels for 0%

commit v1 on v0

v1 whole, which is shorter than its diff:
```python
import jax
import jax.numpy as jnp
from jax import lax
from jax.sharding import PartitionSpec as P

F32 = jnp.float32
BF16 = jnp.bfloat16
CHUNKS = 2


def copy_for_each(shard, axis):
    copies = jnp.broadcast_to(shard, (lax.axis_size(axis), *shard.shape))
    return lax.all_to_all(copies, axis, split_axis=0, concat_axis=0, tiled=True)


def exchange(parts, axis):
    return lax.all_to_all(parts, axis, split_axis=0, concat_axis=0, tiled=True)


def contract_first(a, b):
    return lax.dot_general(a, b, (((0,), (0,)), ((), ())), preferred_element_type=F32)


def three_parts(x):
    a = lax.reduce_precision(x, 8, 7)
    b = lax.reduce_precision(x - a, 8, 7)
    c = x - a - b
    return [part.astype(BF16) for part in (a, b, c)]


def divided(lam_row, lam_col, first_col):
    on_diag = (
        jnp.arange(lam_row.shape[0], dtype=jnp.int32)[:, None]
        == (first_col + jnp.arange(lam_col.shape[0], dtype=jnp.int32))[None, :]
    )
    root_row = lam_row ** (-0.5)
    root_col = lam_col ** (-0.5)
    gaps_lam = lam_row[:, None] - lam_col[None, :]
    safe_gap = jnp.where(on_diag, jnp.ones_like(gaps_lam), gaps_lam)
    off_diag = (root_row[:, None] - root_col[None, :]) / safe_gap
    diag_vals = -0.5 * lam_row[:, None] ** (-1.5) + jnp.zeros_like(gaps_lam)
    return jnp.where(on_diag, diag_vals, off_diag)


def local(features, grad_out, eigvecs, eigvals, whiten):
    n, width = features.shape
    groups, planes = lax.axis_size("rows"), lax.axis_size("feat")
    total = n * groups
    dim = width * planes
    narrow = eigvecs.shape[1]
    half = planes // 2
    r, f = lax.axis_index("rows"), lax.axis_index("feat")
    way = jnp.where(r % 2 == 0, -1, 1)
    ring = [
        (a * planes + b, a * planes + (b + (1 if a % 2 == 0 else -1)) % planes)
        for a in range(groups)
        for b in range(planes)
    ]

    step = n // CHUNKS
    cut = lambda a, k: a[k * step : (k + 1) * step]
    own = [jnp.concatenate([cut(features, k), cut(grad_out, k)]) for k in range(CHUNKS)]
    blocks = [[jnp.concatenate([cut(grad_out, k), cut(features, k)]) for k in range(CHUNKS)]]
    for _ in range(planes - 1):
        blocks.append([lax.ppermute(b, ("rows", "feat"), ring) for b in blocks[-1]])

    sums = jnp.stack([jnp.sum(a, axis=0, dtype=F32) for a in (features, grad_out)])
    means = jnp.sum(copy_for_each(sums, "rows"), axis=0) / total
    packed = [p.reshape(-1, narrow) for p in three_parts(means)]
    shared = copy_for_each(jnp.concatenate([eigvecs.astype(BF16), *packed]), "feat")
    basis_r = shared[:, :width].reshape(dim, narrow)
    all_means = jnp.sum(
        shared[:, width:].astype(F32).reshape(planes, 3, 2, width), axis=1
    )
    basis_t = lax.all_gather(basis_r.T, "rows", axis=0, tiled=True)

    def outer(a, b):
        return a[:, None] * b[None, :]

    parts = []
    for h in range(half + 1):
        there = lax.dynamic_index_in_dim(all_means, (f + way * h) % planes, 0, False)
        if h == 0:
            raw = contract_first(features, grad_out)
            raw -= outer(sums[0], means[1]) + outer(means[0], sums[1] - n * means[1])
        else:
            raw = sum(contract_first(a, b) for a, b in zip(own, blocks[h]))
            sum_g = sum(jnp.sum(b[:step], axis=0, dtype=F32) for b in blocks[h])
            sum_x = sum(jnp.sum(b[step:], axis=0, dtype=F32) for b in blocks[h])
            raw -= outer(sums[0], there[1]) + outer(sums[1], there[0])
            raw -= outer(means[0], sum_g - n * there[1]) + outer(means[1], sum_x - n * there[0])
            if h == half:
                raw = 0.5 * raw
        parts.append(raw.astype(BF16))
    mixed = jnp.concatenate(parts, axis=1)

    got = exchange(mixed.reshape(groups, width // groups, -1), "rows").astype(F32)
    got = jnp.sum(got.reshape(groups // 2, 2, width // groups, -1), axis=0)
    piece = lambda c, h: got[c, :, h * width : (h + 1) * width]
    pair = [piece(0, 0) + piece(1, 0)]
    pair += [piece(1, h) for h in range(1, half)]
    pair += [piece(0, half) + piece(1, half)]
    pair += [piece(0, h) for h in range(half - 1, 0, -1)]
    gram = copy_for_each(jnp.concatenate(pair, axis=1).astype(BF16), "rows")
    gram = gram.reshape(width, dim)

    twice = jnp.concatenate([basis_r, basis_r])
    turned = lax.dynamic_slice_in_dim(twice, f * width, dim)
    right = jnp.dot(gram, turned, preferred_element_type=F32).astype(BF16)
    right = copy_for_each(right, "feat").reshape(dim, narrow)
    rot = jnp.dot(basis_t, right, preferred_element_type=F32)
    back = exchange(rot.astype(BF16).reshape(groups, narrow, narrow), "rows")
    rot = rot + jnp.swapaxes(back, 1, 2).reshape(dim, narrow).astype(F32)
    first_col = r * narrow
    lam_col = lax.dynamic_slice_in_dim(eigvals, first_col, narrow)
    scaled = divided(eigvals, lam_col, first_col) * rot

    high = lax.reduce_precision(scaled, 8, 7)
    both = jnp.concatenate([high.astype(BF16), (scaled - high).astype(BF16)], axis=1)
    basis_f = lax.dynamic_slice_in_dim(basis_t, f * width, width, axis=1)
    undone = contract_first(both, basis_f)
    undone = (undone[:narrow] + undone[narrow:]).astype(BF16)
    undone = copy_for_each(undone, "rows").reshape(dim, width)
    sens = contract_first(basis_t, undone)
    sens_scaled = (sens * (1.0 / total)).astype(BF16)

    shifted = jnp.zeros((n, dim), BF16)
    centered = jnp.zeros((n, dim), BF16)
    for h in range(planes):
        g = (f + way * h) % planes
        there = lax.dynamic_index_in_dim(all_means, g, 0, False)
        for k, b in enumerate(blocks[h]):
            at = (k * step, g * width)
            shifted = lax.dynamic_update_slice(
                shifted, (b[:step].astype(F32) - there[1]).astype(BF16), at
            )
            centered = lax.dynamic_update_slice(
                centered, (b[step:].astype(F32) - there[0]).astype(BF16), at
            )
    grad_in = jnp.dot(shifted, whiten, preferred_element_type=F32)
    grad_in = grad_in + jnp.dot(centered, sens_scaled, preferred_element_type=F32)
    return grad_in.astype(BF16)


def solution(mesh):
    in_specs = (P("rows", "feat"), P("rows", "feat"), P("feat", "rows"), P(), P(None, "feat"))
    out_specs = P("rows", "feat")
    return jax.shard_map(local, mesh=mesh, in_specs=in_specs, out_specs=out_specs, check_vma=False)
```

time: 376 us -> 239 us (0.64)
  blocking collectives: 198 us -> 21.8 us
  waiting for transfers between devices: 114 us -> 69 us
  other arithmetic: 7.15 us -> 38 us
  starting transfers between devices: 14.2 us -> 44.1 us
  matrix products: 20.9 us -> 32.5 us
  local copies, waits for them, and re-layouts: 7.75 us -> 17.5 us
    psum x1 -> x0, blocking collectives: 124 us -> none  [local(): lax.psum((cross_one, cross_two, sum_x, sum_g), 'rows')]
    all_gather x1, waiting for transfers between devices: 66.8 us -> 0.02 us  [local(): basis_t = lax.all_gather(basis_r.T, 'rows', axis=0, tiled=True)]
    ppermute x0 -> x14, waiting for transfers between devices: none -> 28.7 us  [local(): blocks.append([lax.ppermute(b, ('rows', 'feat'), ring) for b in blocks[-1]])]
    dynamic_update_slice x0 -> x17, other arithmetic: none -> 28.3 us  [the longest x16 26.9 us: local(): lax.dynamic_update_slice(centered, (b[step:].astype(F32) - there[0]).asty...]
    all_to_all x2 -> x1, blocking collectives: 48.6 us -> 21.8 us  [copy_for_each(): return lax.all_to_all(copies, axis, split_axis=0, concat_axis=0, tiled=True)]
    all_to_all x1 -> x0, blocking collectives: 25.3 us -> none  [summed_on_arrival(): parts = lax.all_to_all(split_up(shard, dim, peers), axis, 0, 0, tiled=True)]
    all_to_all x2 -> x4, waiting for transfers between devices: 47.3 us -> 27.5 us  [copy_for_each(): return lax.all_to_all(copies, axis, split_axis=0, concat_axis=0, tiled=True)]
    all_to_all x0 -> x2, waiting for transfers between devices: none -> 12.8 us  [exchange(): return lax.all_to_all(parts, axis, split_axis=0, concat_axis=0, tiled=True)]
  transfers between devices with their start and end apart: 4 -> 21, of which waited for: 2 -> 14; matrix products, arithmetic and copies ran while one was open for 5% -> 30% of each run, Pallas kernels for 0% -> 0%
where the time goes in v1:
time: 239 us; the launch traced here: 237 us
  waiting for transfers between devices  69 us (29%)
  starting transfers between devices  44.1 us (18%)
  other arithmetic  38 us (16%)
  matrix products  32.5 us (14%)
  blocking collectives  21.8 us (9%)
  local copies, waits for them, and re-layouts  17.5 us (7%)
  between operations  14.3 us (6%)
    ppermute x14, waiting for transfers between devices, local(): blocks.append([lax.ppermute(b, ('rows', 'feat'), ring) for b in blocks[-1]])  28.7 us
    all_to_all x4, waiting for transfers between devices, copy_for_each(): return lax.all_to_all(copies, axis, split_axis=0, concat_axis=0, tiled=True)  27.5 us
    dynamic_update_slice x16, other arithmetic, local(): lax.dynamic_update_slice(centered, (b[step:].astype(F32) - there[0]).asty...  26.9 us
    all_to_all x1, blocking collectives, copy_for_each(): return lax.all_to_all(copies, axis, split_axis=0, concat_axis=0, tiled=True)  21.8 us
    all_to_all x4, starting transfers between devices, copy_for_each(): return lax.all_to_all(copies, axis, split_axis=0, concat_axis=0, tiled=True)  20.8 us
    all_to_all x2, waiting for transfers between devices, exchange(): return lax.all_to_all(parts, axis, split_axis=0, concat_axis=0, tiled=True)  12.8 us
    all_to_all x2, starting transfers between devices, exchange(): return lax.all_to_all(parts, axis, split_axis=0, concat_axis=0, tiled=True)  11.6 us
    ppermute x14, starting transfers between devices, local(): blocks.append([lax.ppermute(b, ('rows', 'feat'), ring) for b in blocks[-1]])  11.6 us
  transfers between devices with their start and end apart: 21, of which 14 were waited for; matrix products, arithmetic and copies ran while one was open for 30% of the time, Pallas kernels for 0%

profile of v1, /device:TPU:1, one launch (start us, length us, event | category | flops | bytes accessed | tf_op | source)
XLA Modules:
  0.0 237.2 jit_solution(6058048820309710288)
XLA Ops:
  9.7 8.6 %all-to-all-start = ((f32[32,2,256]{2,1,0:T(2,128)}), f32[32,2,256]{2,1,0:T(2,128)S(1)}, u32[]{:S(2)}, u32[]{:S(2)}) async-start(f32[32,2,256]{2,1,0:T(2,128)} %broadcast_in_dim.12), calls=%async_computation | async-start | bytes 131072 | tf_op jit(solution)/shard_map/all_to_all | solution.py:13
  19.2 6.4 %all-to-all-done = f32[32,2,256]{2,1,0:T(2,128)S(1)} async-done(((f32[32,2,256]{2,1,0:T(2,128)}), f32[32,2,256]{2,1,0:T(2,128)S(1)}, u32[]{:S(2)}, u32[]{:S(2)}) %all-to-all-start) | async-done | bytes 65568 | tf_op jit(solution)/shard_map/all_to_all | solution.py:13
  26.7 21.8 %all_to_all.35 = bf16[8,280,64]{1,2,0:T(8,128)(2,1)S(1)} all-to-all(bf16[8,280,64]{1,2,0:T(8,128)(2,1)S(1)} %broadcast_in_dim.13), channel_id=1, replica_groups=mesh['rows'=32,'feat'=8] {'feat'}, dimensions={0} | all-to-all | bytes 573440 | tf_op jit(solution)/shard_map/all_to_all | solution.py:13
  51.7 2.5 %broadcast.69.clone = bf16[1024,2048]{1,0:T(8,128)(2,1)} broadcast(bf16[]{:T(256)} %constant.111.clone.1), dimensions={} | broadcast | bytes 4194306 | tf_op jit(solution)/shard_map/broadcast.2
  55.0 2.5 %broadcast.69 = bf16[1024,2048]{1,0:T(8,128)(2,1)} broadcast(bf16[]{:T(256)} %constant.111.clone.1), dimensions={} | broadcast | bytes 4194306 | tf_op jit(solution)/shard_map/broadcast.2
  64.8 3.8 %collective-permute-done = bf16[1024,256]{1,0:T(8,128)(2,1)S(1)} collective-permute-done((bf16[1024,256]{1,0:T(8,128)(2,1)}, bf16[1024,256]{1,0:T(8,128)(2,1)S(1)}, u32[]{:S(2)}, u32[]{:S(2)}) %collective-permute-start) | collective-permute-done | bytes 524320 | tf_op jit(solution)/shard_map/ppermute | solution.py:65
  69.5 4.7 %collective-permute-done.1 = bf16[1024,256]{1,0:T(8,128)(2,1)S(1)} collective-permute-done((bf16[1024,256]{1,0:T(8,128)(2,1)}, bf16[1024,256]{1,0:T(8,128)(2,1)S(1)}, u32[]{:S(2)}, u32[]{:S(2)}) %collective-permute-start.1) | collective-permute-done | bytes 524320 | tf_op jit(solution)/shard_map/ppermute | solution.py:65
  80.7 4.8 %collective-permute-done.3 = bf16[1024,256]{1,0:T(8,128)(2,1)S(1)} collective-permute-done((bf16[1024,256]{1,0:T(8,128)(2,1)S(1)}, bf16[1024,256]{1,0:T(8,128)(2,1)S(1)}, u32[]{:S(2)}, u32[]{:S(2)}) %collective-permute-start.3) | collective-permute-done | bytes 524320 | tf_op jit(solution)/shard_map/ppermute | solution.py:65
  88.5 2.7 %collective-permute-done.4 = bf16[1024,256]{1,0:T(8,128)(2,1)S(1)} collective-permute-done((bf16[1024,256]{1,0:T(8,128)(2,1)S(1)}, bf16[1024,256]{1,0:T(8,128)(2,1)S(1)}, u32[]{:S(2)}, u32[]{:S(2)}) %collective-permute-start.4) | collective-permute-done | bytes 524320 | tf_op jit(solution)/shard_map/ppermute | solution.py:65
  92.4 4.4 %collective-permute-done.5 = bf16[1024,256]{1,0:T(8,128)(2,1)S(1)} collective-permute-done((bf16[1024,256]{1,0:T(8,128)(2,1)S(1)}, bf16[1024,256]{1,0:T(8,128)(2,1)S(1)}, u32[]{:S(2)}, u32[]{:S(2)}) %collective-permute-start.5) | collective-permute-done | bytes 524320 | tf_op jit(solution)/shard_map/ppermute | solution.py:65
  99.6 2.6 %collective-permute-done.6 = bf16[1024,256]{1,0:T(8,128)(2,1)S(1)} collective-permute-done((bf16[1024,256]{1,0:T(8,128)(2,1)S(1)}, bf16[1024,256]{1,0:T(8,128)(2,1)S(1)}, u32[]{:S(2)}, u32[]{:S(2)}) %collective-permute-start.6) | collective-permute-done | bytes 524320 | tf_op jit(solution)/shard_map/ppermute | solution.py:65
  102.4 5.5 %collective-permute-done.7 = bf16[1024,256]{1,0:T(8,128)(2,1)S(1)} collective-permute-done((bf16[1024,256]{1,0:T(8,128)(2,1)S(1)}, bf16[1024,256]{1,0:T(8,128)(2,1)S(1)}, u32[]{:S(2)}, u32[]{:S(2)}) %collective-permute-start.7) | collective-permute-done | bytes 524320 | tf_op jit(solution)/shard_map/ppermute | solution.py:65
  109.5 2.2 copy.56
  111.6 7.4 %all-to-all-start.2 = ((bf16[32,8,1280]{2,1,0:T(8,128)(2,1)}), bf16[32,8,1280]{2,1,0:T(8,128)(2,1)S(1)}, u32[]{:S(2)}, u32[]{:S(2)}) async-start(bf16[32,8,1280]{2,1,0:T(8,128)(2,1)} %bitcast.22), calls=%async_computation.2 | async-start | bytes 1310720 | tf_op jit(solution)/shard_map/all_to_all | solution.py:17
  123.8 8.2 %all-to-all-done.2 = bf16[32,8,1280]{2,1,0:T(8,128)(2,1)S(1)} async-done(((bf16[32,8,1280]{2,1,0:T(8,128)(2,1)}), bf16[32,8,1280]{2,1,0:T(8,128)(2,1)S(1)}, u32[]{:S(2)}, u32[]{:S(2)}) %all-to-all-start.2) | async-done | bytes 655392 | tf_op jit(solution)/shard_map/all_to_all | solution.py:17
  133.3 4.7 %all-to-all-start.3 = ((bf16[32,8,2048]{2,1,0:T(8,128)(2,1)}), bf16[32,8,2048]{2,1,0:T(8,128)(2,1)}, u32[]{:S(2)}, u32[]{:S(2)}) async-start(bf16[32,8,2048]{2,1,0:T(8,128)(2,1)} %broadcast_in_dim.15), calls=%async_computation.3 | async-start | bytes 2097152 | tf_op jit(solution)/shard_map/all_to_all | solution.py:13
  141.4 2.0 fusion.65
  143.4 2.0 fusion.64
  147.2 8.0 %all-to-all-done.3 = bf16[32,8,2048]{2,1,0:T(8,128)(2,1)} async-done(((bf16[32,8,2048]{2,1,0:T(8,128)(2,1)}), bf16[32,8,2048]{2,1,0:T(8,128)(2,1)}, u32[]{:S(2)}, u32[]{:S(2)}) %all-to-all-start.3) | async-done | bytes 1048608 | tf_op jit(solution)/shard_map/all_to_all | solution.py:13
  157.7 3.4 %all-to-all-start.4 = ((bf16[8,256,64]{1,2,0:T(8,128)(2,1)}), bf16[8,256,64]{1,2,0:T(8,128)(2,1)S(1)}, u32[]{:S(2)}, u32[]{:S(2)}) async-start(bf16[8,256,64]{1,2,0:T(8,128)(2,1)} %broadcast_in_dim.16), calls=%async_computation.4 | async-start | bytes 524288 | tf_op jit(solution)/shard_map/all_to_all | solution.py:13
  162.1 2.6 %collective-permute-start.10 = (bf16[1024,256]{1,0:T(8,128)(2,1)}, bf16[1024,256]{1,0:T(8,128)(2,1)}, u32[]{:S(2)}, u32[]{:S(2)}) collective-permute-start(bf16[1024,256]{1,0:T(8,128)(2,1)} %collective-permute-done.8), channel_id=1, source_target_pairs={{0,1},{1,2},{2,3},{3,4},{4,5},{5,6},{6,7},{7,0},{8,15},{9,8},{10,9... | collective-permute-start | bytes 1572872 | tf_op jit(solution)/shard_map/ppermute | solution.py:65
  165.9 2.0 fusion.54
  167.9 5.4 %all-to-all-done.4 = bf16[8,256,64]{1,2,0:T(8,128)(2,1)S(1)} async-done(((bf16[8,256,64]{1,2,0:T(8,128)(2,1)}), bf16[8,256,64]{1,2,0:T(8,128)(2,1)S(1)}, u32[]{:S(2)}, u32[]{:S(2)}) %all-to-all-start.4) | async-done | bytes 262176 | tf_op jit(solution)/shard_map/all_to_all | solution.py:13
  173.4 6.0 %fusion.95 = (bf16[2048,64]{0,1:T(8,128)(2,1)S(1)}, f32[2048,64]{0,1:T(8,128)S(1)}) fusion(bf16[2048,2048]{1,0:T(8,128)(2,1)} %all-gather.2.cloned.1.call-done, bf16[2048,64]{0,1:T(8,128)(2,1)S(1)} %bitcast.91), kind=kOutput, calls=%fused_computation.218 | convolution fusion | flops 537001984 | bytes 9437184 | tf_op jit(solution)/shard_map/dot_general | solution.py:111
  180.8 4.2 %all-to-all-start.5 = ((bf16[32,2,2048]{2,1,0:T(2,128)(2,1)}), bf16[32,2,2048]{2,1,0:T(2,128)(2,1)S(1)}, u32[]{:S(2)}, u32[]{:S(2)}) async-start(bf16[32,2,2048]{2,1,0:T(2,128)(2,1)} %reshape.204), calls=%async_computation.5 | async-start | bytes 524288 | tf_op jit(solution)/shard_map/all_to_all | solution.py:17
  189.3 4.6 %all-to-all-done.5 = bf16[32,2,2048]{2,1,0:T(2,128)(2,1)S(1)} async-done(((bf16[32,2,2048]{2,1,0:T(2,128)(2,1)}), bf16[32,2,2048]{2,1,0:T(2,128)(2,1)S(1)}, u32[]{:S(2)}, u32[]{:S(2)}) %all-to-all-start.5) | async-done | bytes 262176 | tf_op jit(solution)/shard_map/all_to_all | solution.py:17
  198.5 4.1 %all-to-all-start.6 = ((bf16[32,64,256]{2,1,0:T(8,128)(2,1)}), bf16[32,64,256]{2,1,0:T(8,128)(2,1)S(1)}, u32[]{:S(2)}, u32[]{:S(2)}) async-start(bf16[32,64,256]{2,1,0:T(8,128)(2,1)} %broadcast_in_dim.17), calls=%async_computation.6 | async-start | bytes 2097152 | tf_op jit(solution)/shard_map/all_to_all | solution.py:13
  204.5 2.0 fusion.58
  206.5 2.0 fusion.59
  208.6 3.4 %fusion.96 = f32[1024,256]{1,0:T(8,128)S(1)} fusion(bf16[1024,2048]{1,0:T(8,128)(2,1)} %get-tuple-element.26, bf16[2048,256]{1,0:T(8,128)(2,1)S(1)} %copy-done), kind=kOutput, calls=%fused_computation.219 | convolution fusion | flops 1073741824 | bytes 6291456 | tf_op jit(solution)/shard_map/dot_general | solution.py:140
  212.0 7.6 %all-to-all-done.6 = bf16[32,64,256]{2,1,0:T(8,128)(2,1)S(1)} async-done(((bf16[32,64,256]{2,1,0:T(8,128)(2,1)}), bf16[32,64,256]{2,1,0:T(8,128)(2,1)S(1)}, u32[]{:S(2)}, u32[]{:S(2)}) %all-to-all-start.6) | async-done | bytes 1048608 | tf_op jit(solution)/shard_map/all_to_all | solution.py:13
  219.6 10.8 %fusion.1 = bf16[1024,256]{1,0:T(8,128)(2,1)} fusion(f32[1024,256]{1,0:T(8,128)S(1)} %fusion.96, bf16[1024,2048]{1,0:T(8,128)(2,1)} %get-tuple-element.25, bf16[2048,2048]{1,0:T(8,128)(2,1)} %all-gather.2.cloned.1.call-done, bf16[2048,256]{1,0:T(8,128)(2,1)S(1)} %bitcast.92), kind=kOutput, calls=%fused_computation.4 | convolution fusion | flops 3222798336 | bytes 15204352 | tf_op jit(solution)/shard_map/dot_general | solution.py:141
  (206 shorter events, 59.8 us)
Async XLA Ops:
  6.5 202.0 %copy-start = (bf16[2048,256]{1,0:T(8,128)(2,1)S(1)}, bf16[2048,256]{1,0:T(8,128)(2,1)}, u32[]{:S(2)}) copy-start(bf16[2048,256]{1,0:T(8,128)(2,1)} %param.9) | copy-start | bytes 3145732
  6.5 43.0 %copy-start.22 = (f32[2048]{0:T(1024)S(1)}, f32[2048]{0:T(1024)}, u32[]{:S(2)}) copy-start(f32[2048]{0:T(1024)} %param.8) | copy-start | bytes 24580
  9.0 45.1 %copy-start.1 = (bf16[1024,256]{1,0:T(8,128)(2,1)S(1)}, bf16[1024,256]{1,0:T(8,128)(2,1)}, u32[]{:S(2)}) copy-start(bf16[1024,256]{1,0:T(8,128)(2,1)} %param.5) | copy-start | bytes 1572868
  9.7 15.9 %all-to-all-start = ((f32[32,2,256]{2,1,0:T(2,128)}), f32[32,2,256]{2,1,0:T(2,128)S(1)}, u32[]{:S(2)}, u32[]{:S(2)}) async-start(f32[32,2,256]{2,1,0:T(2,128)} %broadcast_in_dim.12), calls=%async_computation | async-start | bytes 131072 | tf_op jit(solution)/shard_map/all_to_all | solution.py:13
  18.3 155.0 %all-gather.2.cloned.1.call-start = ((), (), s32[]{:S(2)}) async-start(), calls=%async_computation.7 | async-start | bytes 8650752 | tf_op jit(solution)/shard_map/all_gather | solution.py:75
  60.0 8.6 %collective-permute-start = (bf16[1024,256]{1,0:T(8,128)(2,1)}, bf16[1024,256]{1,0:T(8,128)(2,1)S(1)}, u32[]{:S(2)}, u32[]{:S(2)}) collective-permute-start(bf16[1024,256]{1,0:T(8,128)(2,1)} %pad_maximum_fusion), channel_id=1, source_target_pairs={{0,1},{1,2},{2,3},{3,4},{4,5},{5,6},{6,7},{7,0},{8,15},{9,8},{10,9... | collective-permute-start | bytes 1572872 | tf_op jit(solution)/shard_map/ppermute | solution.py:65
  60.9 26.1 %copy-start.32 = (f32[1,1,256]{2,1,0:T(1,128)S(1)}, f32[1,1,256]{2,1,0:T(1,128)}, u32[]{:S(2)}) copy-start(f32[1,1,256]{2,1,0:T(1,128)} %get-tuple-element.72) | copy-start | bytes 3076
  60.9 26.1 %copy-start.31 = (f32[1,1,256]{2,1,0:T(1,128)S(1)}, f32[1,1,256]{2,1,0:T(1,128)}, u32[]{:S(2)}) copy-start(f32[1,1,256]{2,1,0:T(1,128)} %get-tuple-element.65) | copy-start | bytes 3076
  60.9 13.3 %collective-permute-start.1 = (bf16[1024,256]{1,0:T(8,128)(2,1)}, bf16[1024,256]{1,0:T(8,128)(2,1)S(1)}, u32[]{:S(2)}, u32[]{:S(2)}) collective-permute-start(bf16[1024,256]{1,0:T(8,128)(2,1)} %pad_maximum_fusion.1), channel_id=1, source_target_pairs={{0,1},{1,2},{2,3},{3,4},{4,5},{5,6},{6,7},{7,0},{8,15},{9,8},{10,9... | collective-permute-start | bytes 1572872 | tf_op jit(solution)/shard_map/ppermute | solution.py:65
  62.4 24.6 %copy-start.19 = (bf16[512,256]{1,0:T(8,128)(2,1)S(1)}, bf16[512,256]{1,0:T(8,128)(2,1)}, u32[]{:S(2)}) copy-start(bf16[512,256]{1,0:T(8,128)(2,1)} %copy-done.18) | copy-start | bytes 786436
  62.4 24.6 %copy-start.21 = (bf16[512,256]{1,0:T(8,128)(2,1)S(1)}, bf16[512,256]{1,0:T(8,128)(2,1)}, u32[]{:S(2)}) copy-start(bf16[512,256]{1,0:T(8,128)(2,1)} %copy-done.20) | copy-start | bytes 786436
  68.7 11.1 %collective-permute-start.2 = (bf16[1024,256]{1,0:T(8,128)(2,1)S(1)}, bf16[1024,256]{1,0:T(8,128)(2,1)S(1)}, u32[]{:S(2)}, u32[]{:S(2)}) collective-permute-start(bf16[1024,256]{1,0:T(8,128)(2,1)S(1)} %collective-permute-done), channel_id=1, source_target_pairs={{0,1},{1,2},{2,3},{3,4},{4,5},{5,6},{6,7},{7,0},{8,15},{9,8},{10,9... | collective-permute-start | bytes 1572872 | tf_op jit(solution)/shard_map/ppermute | solution.py:65
  74.2 11.3 %collective-permute-start.3 = (bf16[1024,256]{1,0:T(8,128)(2,1)S(1)}, bf16[1024,256]{1,0:T(8,128)(2,1)S(1)}, u32[]{:S(2)}, u32[]{:S(2)}) collective-permute-start(bf16[1024,256]{1,0:T(8,128)(2,1)S(1)} %collective-permute-done.1), channel_id=1, source_target_pairs={{0,1},{1,2},{2,3},{3,4},{4,5},{5,6},{6,7},{7,0},{8,15},{9,8},{10,9... | collective-permute-start | bytes 1572872 | tf_op jit(solution)/shard_map/ppermute | solution.py:65
  79.8 11.3 %collective-permute-start.4 = (bf16[1024,256]{1,0:T(8,128)(2,1)S(1)}, bf16[1024,256]{1,0:T(8,128)(2,1)S(1)}, u32[]{:S(2)}, u32[]{:S(2)}) collective-permute-start(bf16[1024,256]{1,0:T(8,128)(2,1)S(1)} %collective-permute-done.2), channel_id=1, source_target_pairs={{0,1},{1,2},{2,3},{3,4},{4,5},{5,6},{6,7},{7,0},{8,15},{9,8},{10,9... | collective-permute-start | bytes 1572872 | tf_op jit(solution)/shard_map/ppermute | solution.py:65
  85.5 11.2 %collective-permute-start.5 = (bf16[1024,256]{1,0:T(8,128)(2,1)S(1)}, bf16[1024,256]{1,0:T(8,128)(2,1)S(1)}, u32[]{:S(2)}, u32[]{:S(2)}) collective-permute-start(bf16[1024,256]{1,0:T(8,128)(2,1)S(1)} %collective-permute-done.3), channel_id=1, source_target_pairs={{0,1},{1,2},{2,3},{3,4},{4,5},{5,6},{6,7},{7,0},{8,15},{9,8},{10,9... | collective-permute-start | bytes 1572872 | tf_op jit(solution)/shard_map/ppermute | solution.py:65
  91.2 11.1 %collective-permute-start.6 = (bf16[1024,256]{1,0:T(8,128)(2,1)S(1)}, bf16[1024,256]{1,0:T(8,128)(2,1)S(1)}, u32[]{:S(2)}, u32[]{:S(2)}) collective-permute-start(bf16[1024,256]{1,0:T(8,128)(2,1)S(1)} %collective-permute-done.4), channel_id=1, source_target_pairs={{0,1},{1,2},{2,3},{3,4},{4,5},{5,6},{6,7},{7,0},{8,15},{9,8},{10,9... | collective-permute-start | bytes 1572872 | tf_op jit(solution)/shard_map/ppermute | solution.py:65
  96.8 11.1 %collective-permute-start.7 = (bf16[1024,256]{1,0:T(8,128)(2,1)S(1)}, bf16[1024,256]{1,0:T(8,128)(2,1)S(1)}, u32[]{:S(2)}, u32[]{:S(2)}) collective-permute-start(bf16[1024,256]{1,0:T(8,128)(2,1)S(1)} %collective-permute-done.5), channel_id=1, source_target_pairs={{0,1},{1,2},{2,3},{3,4},{4,5},{5,6},{6,7},{7,0},{8,15},{9,8},{10,9... | collective-permute-start | bytes 1572872 | tf_op jit(solution)/shard_map/ppermute | solution.py:65
  111.6 20.4 %all-to-all-start.2 = ((bf16[32,8,1280]{2,1,0:T(8,128)(2,1)}), bf16[32,8,1280]{2,1,0:T(8,128)(2,1)S(1)}, u32[]{:S(2)}, u32[]{:S(2)}) async-start(bf16[32,8,1280]{2,1,0:T(8,128)(2,1)} %bitcast.22), calls=%async_computation.2 | async-start | bytes 1310720 | tf_op jit(solution)/shard_map/all_to_all | solution.py:17
  132.2 23.1 %copy-start.15 = (bf16[8,8,8,256]{3,2,0,1:T(8,128)(2,1)S(1)}, bf16[8,8,8,256]{3,2,0,1:T(8,128)(2,1)}, u32[]{:S(2)}) copy-start(bf16[8,8,8,256]{3,2,0,1:T(8,128)(2,1)} %copy.63) | copy-start | bytes 786436
  133.3 21.9 %all-to-all-start.3 = ((bf16[32,8,2048]{2,1,0:T(8,128)(2,1)}), bf16[32,8,2048]{2,1,0:T(8,128)(2,1)}, u32[]{:S(2)}, u32[]{:S(2)}) async-start(bf16[32,8,2048]{2,1,0:T(8,128)(2,1)} %broadcast_in_dim.15), calls=%async_computation.3 | async-start | bytes 2097152 | tf_op jit(solution)/shard_map/all_to_all | solution.py:13
  138.1 23.0 %copy-start.26 = (f32[1,1,256]{2,1,0:T(1,128)S(1)}, f32[1,1,256]{2,1,0:T(1,128)}, u32[]{:S(2)}) copy-start(f32[1,1,256]{2,1,0:T(1,128)} %get-tuple-element.63) | copy-start | bytes 3076
  138.1 27.8 %copy-start.40 = (f32[1,1,256]{2,1,0:T(1,128)S(1)}, f32[1,1,256]{2,1,0:T(1,128)}, u32[]{:S(2)}) copy-start(f32[1,1,256]{2,1,0:T(1,128)} %get-tuple-element.62) | copy-start | bytes 3076
  138.1 27.8 %copy-start.41 = (f32[1,1,256]{2,1,0:T(1,128)S(1)}, f32[1,1,256]{2,1,0:T(1,128)}, u32[]{:S(2)}) copy-start(f32[1,1,256]{2,1,0:T(1,128)} %get-tuple-element.69) | copy-start | bytes 3076
  145.4 16.7 %collective-permute-start.8 = (bf16[1024,256]{1,0:T(8,128)(2,1)S(1)}, bf16[1024,256]{1,0:T(8,128)(2,1)}, u32[]{:S(2)}, u32[]{:S(2)}) collective-permute-start(bf16[1024,256]{1,0:T(8,128)(2,1)S(1)} %copy-done.12), channel_id=1, source_target_pairs={{0,1},{1,2},{2,3},{3,4},{4,5},{5,6},{6,7},{7,0},{8,15},{9,8},{10,9... | collective-permute-start | bytes 1572872 | tf_op jit(solution)/shard_map/ppermute | solution.py:65
  145.5 19.2 %collective-permute-start.9 = (bf16[1024,256]{1,0:T(8,128)(2,1)S(1)}, bf16[1024,256]{1,0:T(8,128)(2,1)}, u32[]{:S(2)}, u32[]{:S(2)}) collective-permute-start(bf16[1024,256]{1,0:T(8,128)(2,1)S(1)} %copy-done.10), channel_id=1, source_target_pairs={{0,1},{1,2},{2,3},{3,4},{4,5},{5,6},{6,7},{7,0},{8,15},{9,8},{10,9... | collective-permute-start | bytes 1572872 | tf_op jit(solution)/shard_map/ppermute | solution.py:65
  157.7 15.6 %all-to-all-start.4 = ((bf16[8,256,64]{1,2,0:T(8,128)(2,1)}), bf16[8,256,64]{1,2,0:T(8,128)(2,1)S(1)}, u32[]{:S(2)}, u32[]{:S(2)}) async-start(bf16[8,256,64]{1,2,0:T(8,128)(2,1)} %broadcast_in_dim.16), calls=%async_computation.4 | async-start | bytes 524288 | tf_op jit(solution)/shard_map/all_to_all | solution.py:13
  162.1 24.9 %collective-permute-start.10 = (bf16[1024,256]{1,0:T(8,128)(2,1)}, bf16[1024,256]{1,0:T(8,128)(2,1)}, u32[]{:S(2)}, u32[]{:S(2)}) collective-permute-start(bf16[1024,256]{1,0:T(8,128)(2,1)} %collective-permute-done.8), channel_id=1, source_target_pairs={{0,1},{1,2},{2,3},{3,4},{4,5},{5,6},{6,7},{7,0},{8,15},{9,8},{10,9... | collective-permute-start | bytes 1572872 | tf_op jit(solution)/shard_map/ppermute | solution.py:65
  164.7 22.3 %collective-permute-start.11 = (bf16[1024,256]{1,0:T(8,128)(2,1)}, bf16[1024,256]{1,0:T(8,128)(2,1)}, u32[]{:S(2)}, u32[]{:S(2)}) collective-permute-start(bf16[1024,256]{1,0:T(8,128)(2,1)} %collective-permute-done.9), channel_id=1, source_target_pairs={{0,1},{1,2},{2,3},{3,4},{4,5},{5,6},{6,7},{7,0},{8,15},{9,8},{10,9... | collective-permute-start | bytes 1572872 | tf_op jit(solution)/shard_map/ppermute | solution.py:65
  180.8 13.1 %all-to-all-start.5 = ((bf16[32,2,2048]{2,1,0:T(2,128)(2,1)}), bf16[32,2,2048]{2,1,0:T(2,128)(2,1)S(1)}, u32[]{:S(2)}, u32[]{:S(2)}) async-start(bf16[32,2,2048]{2,1,0:T(2,128)(2,1)} %reshape.204), calls=%async_computation.5 | async-start | bytes 524288 | tf_op jit(solution)/shard_map/all_to_all | solution.py:17
  187.0 17.5 %collective-permute-start.12 = (bf16[1024,256]{1,0:T(8,128)(2,1)}, bf16[1024,256]{1,0:T(8,128)(2,1)}, u32[]{:S(2)}, u32[]{:S(2)}) collective-permute-start(bf16[1024,256]{1,0:T(8,128)(2,1)} %collective-permute-done.10), channel_id=1, source_target_pairs={{0,1},{1,2},{2,3},{3,4},{4,5},{5,6},{6,7},{7,0},{8,15},{9,8},{10,9... | collective-permute-start | bytes 1572872 | tf_op jit(solution)/shard_map/ppermute | solution.py:65
  187.0 19.5 %collective-permute-start.13 = (bf16[1024,256]{1,0:T(8,128)(2,1)}, bf16[1024,256]{1,0:T(8,128)(2,1)}, u32[]{:S(2)}, u32[]{:S(2)}) collective-permute-start(bf16[1024,256]{1,0:T(8,128)(2,1)} %collective-permute-done.11), channel_id=1, source_target_pairs={{0,1},{1,2},{2,3},{3,4},{4,5},{5,6},{6,7},{7,0},{8,15},{9,8},{10,9... | collective-permute-start | bytes 1572872 | tf_op jit(solution)/shard_map/ppermute | solution.py:65
  198.5 21.1 %all-to-all-start.6 = ((bf16[32,64,256]{2,1,0:T(8,128)(2,1)}), bf16[32,64,256]{2,1,0:T(8,128)(2,1)S(1)}, u32[]{:S(2)}, u32[]{:S(2)}) async-start(bf16[32,64,256]{2,1,0:T(8,128)(2,1)} %broadcast_in_dim.17), calls=%async_computation.6 | async-start | bytes 2097152 | tf_op jit(solution)/shard_map/all_to_all | solution.py:13
  (36 other events, 451.4 us)
Sparse Core Ops, SparseCore 0:
  49.4 51.7 all-gather.1

commit v2 on v1

--- a/solution.py
+++ b/solution.py
@@ -3,9 +3,9 @@
 from jax import lax
 from jax.sharding import PartitionSpec as P
 
+
 F32 = jnp.float32
 BF16 = jnp.bfloat16
-CHUNKS = 2
 
 
 def copy_for_each(shard, axis):
@@ -19,6 +19,10 @@
 
 def contract_first(a, b):
     return lax.dot_general(a, b, (((0,), (0,)), ((), ())), preferred_element_type=F32)
+
+
+def contract_last(a, b):
+    return lax.dot_general(a, b, (((1,), (1,)), ((), ())), preferred_element_type=F32)
 
 
 def three_parts(x):
@@ -57,22 +61,19 @@
         for b in range(planes)
     ]
 
-    step = n // CHUNKS
-    cut = lambda a, k: a[k * step : (k + 1) * step]
-    own = [jnp.concatenate([cut(features, k), cut(grad_out, k)]) for k in range(CHUNKS)]
-    blocks = [[jnp.concatenate([cut(grad_out, k), cut(features, k)]) for k in range(CHUNKS)]]
-    for _ in range(planes - 1):
-        blocks.append([lax.ppermute(b, ("rows", "feat"), ring) for b in blocks[-1]])
+    blocks = [(grad_out, features)]
+    for _ in range(1, planes):
+        blocks.append(tuple(lax.ppermute(b, ("rows", "feat"), ring) for b in blocks[-1]))
 
     sums = jnp.stack([jnp.sum(a, axis=0, dtype=F32) for a in (features, grad_out)])
     means = jnp.sum(copy_for_each(sums, "rows"), axis=0) / total
-    packed = [p.reshape(-1, narrow) for p in three_parts(means)]
-    shared = copy_for_each(jnp.concatenate([eigvecs.astype(BF16), *packed]), "feat")
-    basis_r = shared[:, :width].reshape(dim, narrow)
+    shared = jnp.concatenate([eigvecs.astype(BF16).T, *three_parts(means)])
+    shared = copy_for_each(shared, "feat")
+    basis_rt = jnp.swapaxes(shared[:, :narrow], 0, 1).reshape(narrow, dim)
     all_means = jnp.sum(
-        shared[:, width:].astype(F32).reshape(planes, 3, 2, width), axis=1
+        shared[:, narrow:].astype(F32).reshape(planes, 3, 2, width), axis=1
     )
-    basis_t = lax.all_gather(basis_r.T, "rows", axis=0, tiled=True)
+    basis_t = lax.all_gather(basis_rt, "rows", axis=0, tiled=True)
 
     def outer(a, b):
         return a[:, None] * b[None, :]
@@ -84,9 +85,8 @@
             raw = contract_first(features, grad_out)
             raw -= outer(sums[0], means[1]) + outer(means[0], sums[1] - n * means[1])
         else:
-            raw = sum(contract_first(a, b) for a, b in zip(own, blocks[h]))
-            sum_g = sum(jnp.sum(b[:step], axis=0, dtype=F32) for b in blocks[h])
-            sum_x = sum(jnp.sum(b[step:], axis=0, dtype=F32) for b in blocks[h])
+            raw = contract_first(features, blocks[h][0]) + contract_first(grad_out, blocks[h][1])
+            sum_g, sum_x = (jnp.sum(b, axis=0, dtype=F32) for b in blocks[h])
             raw -= outer(sums[0], there[1]) + outer(sums[1], there[0])
             raw -= outer(means[0], sum_g - n * there[1]) + outer(means[1], sum_x - n * there[0])
             if h == half:
@@ -104,9 +104,9 @@
     gram = copy_for_each(jnp.concatenate(pair, axis=1).astype(BF16), "rows")
     gram = gram.reshape(width, dim)
 
-    twice = jnp.concatenate([basis_r, basis_r])
-    turned = lax.dynamic_slice_in_dim(twice, f * width, dim)
-    right = jnp.dot(gram, turned, preferred_element_type=F32).astype(BF16)
+    twice = jnp.concatenate([basis_rt, basis_rt], axis=1)
+    turned = lax.dynamic_slice_in_dim(twice, f * width, dim, axis=1)
+    right = contract_last(gram, turned).astype(BF16)
     right = copy_for_each(right, "feat").reshape(dim, narrow)
     rot = jnp.dot(basis_t, right, preferred_element_type=F32)
     back = exchange(rot.astype(BF16).reshape(groups, narrow, narrow), "rows")
@@ -122,23 +122,22 @@
     undone = (undone[:narrow] + undone[narrow:]).astype(BF16)
     undone = copy_for_each(undone, "rows").reshape(dim, width)
     sens = contract_first(basis_t, undone)
-    sens_scaled = (sens * (1.0 / total)).astype(BF16)
+    sens_scaled = lax.optimization_barrier((sens * (1.0 / total)).astype(BF16))
 
-    shifted = jnp.zeros((n, dim), BF16)
+    grad_in = jnp.zeros((n, width), F32)
     centered = jnp.zeros((n, dim), BF16)
     for h in range(planes):
         g = (f + way * h) % planes
         there = lax.dynamic_index_in_dim(all_means, g, 0, False)
-        for k, b in enumerate(blocks[h]):
-            at = (k * step, g * width)
-            shifted = lax.dynamic_update_slice(
-                shifted, (b[:step].astype(F32) - there[1]).astype(BF16), at
-            )
-            centered = lax.dynamic_update_slice(
-                centered, (b[step:].astype(F32) - there[0]).astype(BF16), at
-            )
-    grad_in = jnp.dot(shifted, whiten, preferred_element_type=F32)
-    grad_in = grad_in + jnp.dot(centered, sens_scaled, preferred_element_type=F32)
+        grads, inputs = blocks[h]
+        at = (0, g * width)
+        shifted = (grads.astype(F32) - there[1]).astype(BF16)
+        mine = lax.dynamic_slice_in_dim(whiten, g * width, width)
+        grad_in += jnp.dot(shifted, mine, preferred_element_type=F32)
+        centered = lax.dynamic_update_slice(
+            centered, (inputs.astype(F32) - there[0]).astype(BF16), at
+        )
+    grad_in += jnp.dot(centered, sens_scaled, preferred_element_type=F32)
     return grad_in.astype(BF16)
 
 

time: 239 us -> 230 us (0.962)
  other arithmetic: 38 us -> 18.3 us
  waiting for transfers between devices: 69 us -> 81 us
  matrix products: 32.5 us -> 39.8 us
  local copies, waits for them, and re-layouts: 17.5 us -> 11.5 us
    dynamic_update_slice x17 -> x8, other arithmetic: 28.3 us -> 8.86 us  [local(): lax.dynamic_update_slice(centered, (inputs.astype(F32) - there[0]).astype...]
    dot_general x10 -> x11, matrix products: 10.5 us -> 18.2 us  [contract_first(): lax.dot_general(a, b, (((0,), (0,)), ((), ())), preferred_element_type=F32)]
    ppermute x14, waiting for transfers between devices: 28.7 us -> 34.2 us  [local(): lax.ppermute(b, ('rows', 'feat'), ring)]
    another operation x2 -> x0, local copies, waits for them, and re-layouts: 5 us -> none
    all_to_all x2, waiting for transfers between devices: 12.8 us -> 16.8 us  [exchange(): return lax.all_to_all(parts, axis, split_axis=0, concat_axis=0, tiled=True)]
    all_to_all x4, waiting for transfers between devices: 27.5 us -> 30 us  [copy_for_each(): return lax.all_to_all(copies, axis, split_axis=0, concat_axis=0, tiled=True)]
    reduce_sum x9, other arithmetic: 0.84 us -> 3.32 us  [the longest x8 3.31 us: local(): sum_g, sum_x = (jnp.sum(b, axis=0, dtype=F32) for b in blocks[h])]
    dot_general x3 -> x10, matrix products: 15.9 us -> 14.8 us  [the longest x8 11.8 us: local(): grad_in += jnp.dot(shifted, mine, preferred_element_type=F32)]
  transfers between devices with their start and end apart: 21 -> 21, of which waited for: 14 -> 13; matrix products, arithmetic and copies ran while one was open for 30% -> 28% of each run, Pallas kernels for 0% -> 0%
where the time goes in v2:
time: 230 us; the launch traced here: 229 us
  waiting for transfers between devices  81 us (35%)
  starting transfers between devices  43.9 us (19%)
  matrix products  39.8 us (17%)
  blocking collectives  20.2 us (9%)
  other arithmetic  18.3 us (8%)
  between operations  14.2 us (6%)
  local copies, waits for them, and re-layouts  11.5 us (5%)
    ppermute x14, waiting for transfers between devices, local(): lax.ppermute(b, ('rows', 'feat'), ring)  34.2 us
    all_to_all x4, waiting for transfers between devices, copy_for_each(): return lax.all_to_all(copies, axis, split_axis=0, concat_axis=0, tiled=True)  30 us
    all_to_all x4, starting transfers between devices, copy_for_each(): return lax.all_to_all(copies, axis, split_axis=0, concat_axis=0, tiled=True)  21.2 us
    all_to_all x1, blocking collectives, copy_for_each(): return lax.all_to_all(copies, axis, split_axis=0, concat_axis=0, tiled=True)  20.2 us
    dot_general x11, matrix products, contract_first(): lax.dot_general(a, b, (((0,), (0,)), ((), ())), preferred_element_type=F32)  18.2 us
    all_to_all x2, waiting for transfers between devices, exchange(): return lax.all_to_all(parts, axis, split_axis=0, concat_axis=0, tiled=True)  16.8 us
    dot_general x8, matrix products, local(): grad_in += jnp.dot(shifted, mine, preferred_element_type=F32)  11.8 us
    all_to_all x2, starting transfers between devices, exchange(): return lax.all_to_all(parts, axis, split_axis=0, concat_axis=0, tiled=True)  11.8 us
  transfers between devices with their start and end apart: 21, of which 13 were waited for; matrix products, arithmetic and copies ran while one was open for 28% of the time, Pallas kernels for 0%

profile of v2, /device:TPU:1, one launch (start us, length us, event | category | flops | bytes accessed | tf_op | source)
XLA Modules:
  0.0 228.8 jit_solution(11169574753002721536)
XLA Ops:
  8.7 8.6 %all-to-all-start = ((f32[32,2,256]{2,1,0:T(2,128)}), f32[32,2,256]{2,1,0:T(2,128)S(1)}, u32[]{:S(2)}, u32[]{:S(2)}) async-start(f32[32,2,256]{2,1,0:T(2,128)} %broadcast_in_dim.14), calls=%async_computation | async-start | bytes 131072 | tf_op jit(solution)/shard_map/all_to_all | solution.py:13
  18.2 6.4 %all-to-all-done = f32[32,2,256]{2,1,0:T(2,128)S(1)} async-done(((f32[32,2,256]{2,1,0:T(2,128)}), f32[32,2,256]{2,1,0:T(2,128)S(1)}, u32[]{:S(2)}, u32[]{:S(2)}) %all-to-all-start) | async-done | bytes 65568 | tf_op jit(solution)/shard_map/all_to_all | solution.py:13
  24.7 20.2 %all_to_all.35 = bf16[8,70,256]{2,1,0:T(8,128)(2,1)S(1)} all-to-all(bf16[8,70,256]{2,1,0:T(8,128)(2,1)S(1)} %broadcast_in_dim.15), channel_id=1, replica_groups=mesh['rows'=32,'feat'=8] {'feat'}, dimensions={0} | all-to-all | bytes 573440 | tf_op jit(solution)/shard_map/all_to_all | solution.py:13
  48.3 2.3 fusion.13
  50.6 3.7 %collective-permute-done = bf16[1024,256]{1,0:T(8,128)(2,1)} collective-permute-done((bf16[1024,256]{1,0:T(8,128)(2,1)}, bf16[1024,256]{1,0:T(8,128)(2,1)}, u32[]{:S(2)}, u32[]{:S(2)}) %collective-permute-start) | collective-permute-done | bytes 524320 | tf_op jit(solution)/shard_map/ppermute | solution.py:66
  55.3 4.7 %collective-permute-done.7 = bf16[1024,256]{1,0:T(8,128)(2,1)S(1)} collective-permute-done((bf16[1024,256]{1,0:T(8,128)(2,1)}, bf16[1024,256]{1,0:T(8,128)(2,1)S(1)}, u32[]{:S(2)}, u32[]{:S(2)}) %collective-permute-start.7) | collective-permute-done | bytes 524320 | tf_op jit(solution)/shard_map/ppermute | solution.py:66
  63.3 2.5 %fusion.21 = bf16[256,1280]{0,1:T(8,128)(2,1)} fusion(bf16[256,1280]{0,1:T(8,128)(2,1)} %fusion.13, f32[256,256]{0,1:T(8,128)S(1)} %fusion.91, bf16[1024,256]{1,0:T(8,128)(2,1)S(1)} %copy-done.7, bf16[1024,256]{1,0:T(8,128)(2,1)} %collective-permute-done, f32[256]{0:T(256)S(1)} %multiply_subtract_fusion.6, f32[256]{0:T(256)S(1)} %bitcast.142, ...), kind=kOutput, calls=%fused_computation.55 | convolution fusion | flops 134873088 | bytes 1449984 | tf_op jit(solution)/shard_map/dot_general | solution.py:21
  66.4 4.7 %collective-permute-done.8 = bf16[1024,256]{1,0:T(8,128)(2,1)S(1)} collective-permute-done((bf16[1024,256]{1,0:T(8,128)(2,1)S(1)}, bf16[1024,256]{1,0:T(8,128)(2,1)S(1)}, u32[]{:S(2)}, u32[]{:S(2)}) %collective-permute-start.8) | collective-permute-done | bytes 524320 | tf_op jit(solution)/shard_map/ppermute | solution.py:66
  73.8 3.0 %collective-permute-done.2 = bf16[1024,256]{1,0:T(8,128)(2,1)S(1)} collective-permute-done((bf16[1024,256]{1,0:T(8,128)(2,1)S(1)}, bf16[1024,256]{1,0:T(8,128)(2,1)S(1)}, u32[]{:S(2)}, u32[]{:S(2)}) %collective-permute-start.2) | collective-permute-done | bytes 524320 | tf_op jit(solution)/shard_map/ppermute | solution.py:66
  77.6 4.8 %collective-permute-done.9 = bf16[1024,256]{1,0:T(8,128)(2,1)S(1)} collective-permute-done((bf16[1024,256]{1,0:T(8,128)(2,1)S(1)}, bf16[1024,256]{1,0:T(8,128)(2,1)S(1)}, u32[]{:S(2)}, u32[]{:S(2)}) %collective-permute-start.9) | collective-permute-done | bytes 524320 | tf_op jit(solution)/shard_map/ppermute | solution.py:66
  85.4 8.3 %collective-permute-done.10 = bf16[1024,256]{1,0:T(8,128)(2,1)S(1)} collective-permute-done((bf16[1024,256]{1,0:T(8,128)(2,1)S(1)}, bf16[1024,256]{1,0:T(8,128)(2,1)S(1)}, u32[]{:S(2)}, u32[]{:S(2)}) %collective-permute-start.10) | collective-permute-done | bytes 524320 | tf_op jit(solution)/shard_map/ppermute | solution.py:66
  95.4 2.1 fusion.15
  97.5 2.2 copy.31
  99.7 7.5 %all-to-all-start.2 = ((bf16[32,8,1280]{2,1,0:T(8,128)(2,1)}), bf16[32,8,1280]{2,1,0:T(8,128)(2,1)}, u32[]{:S(2)}, u32[]{:S(2)}) async-start(bf16[32,8,1280]{2,1,0:T(8,128)(2,1)} %bitcast.99), calls=%async_computation.2 | async-start | bytes 1310720 | tf_op jit(solution)/shard_map/all_to_all | solution.py:17
  108.5 2.4 %convolution_add_fusion.6 = f32[1024,256]{1,0:T(8,128)} fusion(f32[1024,256]{1,0:T(8,128)S(1)} %fusion.48, bf16[1024,256]{1,0:T(8,128)(2,1)} %collective-permute-done, f32[256]{0:T(256)S(1)} %bitcast.126, bf16[2048,256]{1,0:T(8,128)(2,1)S(1)} %copy-done, s32[]{:T(128)S(6)} %select_n.135), kind=kOutput, calls=%fused_computation.9 | convolution fusion | flops 135266304 | bytes 2753540 | tf_op jit(solution)/shard_map/dot_general | solution.py:136
  110.9 9.3 %all-to-all-done.2 = bf16[32,8,1280]{2,1,0:T(8,128)(2,1)} async-done(((bf16[32,8,1280]{2,1,0:T(8,128)(2,1)}), bf16[32,8,1280]{2,1,0:T(8,128)(2,1)}, u32[]{:S(2)}, u32[]{:S(2)}) %all-to-all-start.2) | async-done | bytes 655392 | tf_op jit(solution)/shard_map/all_to_all | solution.py:17
  122.7 4.7 %all-to-all-start.3 = ((bf16[32,8,2048]{2,1,0:T(8,128)(2,1)}), bf16[32,8,2048]{2,1,0:T(8,128)(2,1)}, u32[]{:S(2)}, u32[]{:S(2)}) async-start(bf16[32,8,2048]{2,1,0:T(8,128)(2,1)} %broadcast_in_dim.18), calls=%async_computation.3 | async-start | bytes 2097152 | tf_op jit(solution)/shard_map/all_to_all | solution.py:13
  131.7 12.9 %all-to-all-done.3 = bf16[32,8,2048]{2,1,0:T(8,128)(2,1)} async-done(((bf16[32,8,2048]{2,1,0:T(8,128)(2,1)}), bf16[32,8,2048]{2,1,0:T(8,128)(2,1)}, u32[]{:S(2)}, u32[]{:S(2)}) %all-to-all-start.3) | async-done | bytes 1048608 | tf_op jit(solution)/shard_map/all_to_all | solution.py:13
  147.0 3.4 %all-to-all-start.4 = ((bf16[8,256,64]{1,2,0:T(8,128)(2,1)}), bf16[8,256,64]{1,2,0:T(8,128)(2,1)S(1)}, u32[]{:S(2)}, u32[]{:S(2)}) async-start(bf16[8,256,64]{1,2,0:T(8,128)(2,1)} %broadcast_in_dim.19), calls=%async_computation.4 | async-start | bytes 524288 | tf_op jit(solution)/shard_map/all_to_all | solution.py:13
  151.4 2.4 %convolution_add_fusion.3 = f32[1024,256]{1,0:T(8,128)} fusion(f32[1024,256]{1,0:T(8,128)S(1)} %convolution_add_fusion.4, bf16[1024,256]{1,0:T(8,128)(2,1)} %collective-permute-done.3, f32[256]{0:T(256)S(1)} %bitcast.108, bf16[2048,256]{1,0:T(8,128)(2,1)S(1)} %copy-done, s32[]{:T(128)S(6)} %select_n.144), kind=kOutput, calls=%fused_computation.6 | convolution fusion | flops 135266304 | bytes 2753540 | tf_op jit(solution)/shard_map/dot_general | solution.py:136
  153.8 2.6 %collective-permute-start.5 = (bf16[1024,256]{1,0:T(8,128)(2,1)}, bf16[1024,256]{1,0:T(8,128)(2,1)}, u32[]{:S(2)}, u32[]{:S(2)}) collective-permute-start(bf16[1024,256]{1,0:T(8,128)(2,1)} %collective-permute-done.4), channel_id=1, source_target_pairs={{0,1},{1,2},{2,3},{3,4},{4,5},{5,6},{6,7},{7,0},{8,15},{9,8},{10,9... | collective-permute-start | bytes 1572872 | tf_op jit(solution)/shard_map/ppermute | solution.py:66
  157.6 5.1 %all-to-all-done.4 = bf16[8,256,64]{1,2,0:T(8,128)(2,1)S(1)} async-done(((bf16[8,256,64]{1,2,0:T(8,128)(2,1)}), bf16[8,256,64]{1,2,0:T(8,128)(2,1)S(1)}, u32[]{:S(2)}, u32[]{:S(2)}) %all-to-all-start.4) | async-done | bytes 262176 | tf_op jit(solution)/shard_map/all_to_all | solution.py:13
  162.7 6.9 %fusion.90 = (bf16[2048,64]{0,1:T(8,128)(2,1)S(1)}, f32[2048,64]{0,1:T(8,128)}) fusion(bf16[2048,2048]{1,0:T(8,128)(2,1)} %all-gather.2.cloned.1.call-done, bf16[2048,64]{0,1:T(8,128)(2,1)S(1)} %bitcast.101), kind=kOutput, calls=%fused_computation.188 | convolution fusion | flops 537001984 | bytes 9437184 | tf_op jit(solution)/shard_map/dot_general | solution.py:111
  171.0 4.2 %all-to-all-start.5 = ((bf16[32,2,2048]{2,1,0:T(2,128)(2,1)}), bf16[32,2,2048]{2,1,0:T(2,128)(2,1)S(1)}, u32[]{:S(2)}, u32[]{:S(2)}) async-start(bf16[32,2,2048]{2,1,0:T(2,128)(2,1)} %reshape.172), calls=%async_computation.5 | async-start | bytes 524288 | tf_op jit(solution)/shard_map/all_to_all | solution.py:17
  176.6 7.5 %all-to-all-done.5 = bf16[32,2,2048]{2,1,0:T(2,128)(2,1)S(1)} async-done(((bf16[32,2,2048]{2,1,0:T(2,128)(2,1)}), bf16[32,2,2048]{2,1,0:T(2,128)(2,1)S(1)}, u32[]{:S(2)}, u32[]{:S(2)}) %all-to-all-start.5) | async-done | bytes 262176 | tf_op jit(solution)/shard_map/all_to_all | solution.py:17
  190.6 4.4 %all-to-all-start.6 = ((bf16[32,64,256]{2,1,0:T(8,128)(2,1)}), bf16[32,64,256]{2,1,0:T(8,128)(2,1)}, u32[]{:S(2)}, u32[]{:S(2)}) async-start(bf16[32,64,256]{2,1,0:T(8,128)(2,1)} %broadcast_in_dim.20), calls=%async_computation.6 | async-start | bytes 2097152 | tf_op jit(solution)/shard_map/all_to_all | solution.py:13
  195.1 2.0 fusion.36
  197.4 2.0 fusion.37
  200.7 5.0 %collective-permute-done.13 = bf16[1024,256]{1,0:T(8,128)(2,1)S(1)} collective-permute-done((bf16[1024,256]{1,0:T(8,128)(2,1)}, bf16[1024,256]{1,0:T(8,128)(2,1)S(1)}, u32[]{:S(2)}, u32[]{:S(2)}) %collective-permute-start.13) | collective-permute-done | bytes 524320 | tf_op jit(solution)/shard_map/ppermute | solution.py:66
  206.6 5.6 %all-to-all-done.6 = bf16[32,64,256]{2,1,0:T(8,128)(2,1)} async-done(((bf16[32,64,256]{2,1,0:T(8,128)(2,1)}), bf16[32,64,256]{2,1,0:T(8,128)(2,1)}, u32[]{:S(2)}, u32[]{:S(2)}) %all-to-all-start.6) | async-done | bytes 1048608 | tf_op jit(solution)/shard_map/all_to_all | solution.py:13
  212.2 6.3 %fusion = bf16[2048,256]{1,0:T(8,128)(2,1)S(1)} fusion(bf16[2048,2048]{1,0:T(8,128)(2,1)} %all-gather.2.cloned.1.call-done, bf16[2048,256]{1,0:T(8,128)(2,1)} %bitcast.37), kind=kOutput, calls=%fused_computation.1 | convolution fusion | flops 2148532224 | bytes 10485760 | tf_op jit(solution)/shard_map/dot_general | solution.py:21
  219.8 2.2 fusion.2
  (131 shorter events, 44.8 us)
Async XLA Ops:
  6.5 101.7 %copy-start = (bf16[2048,256]{1,0:T(8,128)(2,1)S(1)}, bf16[2048,256]{1,0:T(8,128)(2,1)}, u32[]{:S(2)}) copy-start(bf16[2048,256]{1,0:T(8,128)(2,1)} %param.9) | copy-start | bytes 3145732
  6.5 55.6 %copy-start.1 = (bf16[1024,256]{1,0:T(8,128)(2,1)S(1)}, bf16[1024,256]{1,0:T(8,128)(2,1)}, u32[]{:S(2)}) copy-start(bf16[1024,256]{1,0:T(8,128)(2,1)} %param.6) | copy-start | bytes 1572868
  8.7 15.9 %all-to-all-start = ((f32[32,2,256]{2,1,0:T(2,128)}), f32[32,2,256]{2,1,0:T(2,128)S(1)}, u32[]{:S(2)}, u32[]{:S(2)}) async-start(f32[32,2,256]{2,1,0:T(2,128)} %broadcast_in_dim.14), calls=%async_computation | async-start | bytes 131072 | tf_op jit(solution)/shard_map/all_to_all | solution.py:13
  17.3 145.4 %all-gather.2.cloned.1.call-start = ((), (), s32[]{:S(2)}) async-start(), calls=%async_computation.7 | async-start | bytes 8650752 | tf_op jit(solution)/shard_map/all_gather | solution.py:76
  45.6 8.7 %collective-permute-start = (bf16[1024,256]{1,0:T(8,128)(2,1)}, bf16[1024,256]{1,0:T(8,128)(2,1)}, u32[]{:S(2)}, u32[]{:S(2)}) collective-permute-start(bf16[1024,256]{1,0:T(8,128)(2,1)} %param.6), channel_id=1, source_target_pairs={{0,1},{1,2},{2,3},{3,4},{4,5},{5,6},{6,7},{7,0},{8,15},{9,8},{10,9... | collective-permute-start | bytes 1572872 | tf_op jit(solution)/shard_map/ppermute | solution.py:66
  45.7 14.2 %collective-permute-start.7 = (bf16[1024,256]{1,0:T(8,128)(2,1)}, bf16[1024,256]{1,0:T(8,128)(2,1)S(1)}, u32[]{:S(2)}, u32[]{:S(2)}) collective-permute-start(bf16[1024,256]{1,0:T(8,128)(2,1)} %param.5), channel_id=1, source_target_pairs={{0,1},{1,2},{2,3},{3,4},{4,5},{5,6},{6,7},{7,0},{8,15},{9,8},{10,9... | collective-permute-start | bytes 1572872 | tf_op jit(solution)/shard_map/ppermute | solution.py:66
  48.3 14.9 %copy-start.7 = (bf16[1024,256]{1,0:T(8,128)(2,1)S(1)}, bf16[1024,256]{1,0:T(8,128)(2,1)}, u32[]{:S(2)}) copy-start(bf16[1024,256]{1,0:T(8,128)(2,1)} %param.5) | copy-start | bytes 1572868
  54.3 11.5 %collective-permute-start.1 = (bf16[1024,256]{1,0:T(8,128)(2,1)}, bf16[1024,256]{1,0:T(8,128)(2,1)S(1)}, u32[]{:S(2)}, u32[]{:S(2)}) collective-permute-start(bf16[1024,256]{1,0:T(8,128)(2,1)} %collective-permute-done), channel_id=1, source_target_pairs={{0,1},{1,2},{2,3},{3,4},{4,5},{5,6},{6,7},{7,0},{8,15},{9,8},{10,9... | collective-permute-start | bytes 1572872 | tf_op jit(solution)/shard_map/ppermute | solution.py:66
  60.0 11.1 %collective-permute-start.8 = (bf16[1024,256]{1,0:T(8,128)(2,1)S(1)}, bf16[1024,256]{1,0:T(8,128)(2,1)S(1)}, u32[]{:S(2)}, u32[]{:S(2)}) collective-permute-start(bf16[1024,256]{1,0:T(8,128)(2,1)S(1)} %collective-permute-done.7), channel_id=1, source_target_pairs={{0,1},{1,2},{2,3},{3,4},{4,5},{5,6},{6,7},{7,0},{8,15},{9,8},{10,9... | collective-permute-start | bytes 1572872 | tf_op jit(solution)/shard_map/ppermute | solution.py:66
  63.3 21.1 %copy-start.4 = (bf16[1024,2048]{1,0:T(8,128)(2,1)}, bf16[1024,2048]{1,0:T(8,128)(2,1)S(1)}, u32[]{:S(2)}) copy-start(bf16[1024,2048]{1,0:T(8,128)(2,1)S(1)} %fusion.47) | copy-start | bytes 12582916
  63.3 21.1 %copy-start.8 = (bf16[1024,256]{1,0:T(8,128)(2,1)S(1)}, bf16[1024,256]{1,0:T(8,128)(2,1)}, u32[]{:S(2)}) copy-start(bf16[1024,256]{1,0:T(8,128)(2,1)} %param.5) | copy-start | bytes 1572868
  65.8 19.6 %copy-start.9 = (bf16[1024,256]{1,0:T(8,128)(2,1)}, bf16[1024,256]{1,0:T(8,128)(2,1)S(1)}, u32[]{:S(2)}) copy-start(bf16[1024,256]{1,0:T(8,128)(2,1)S(1)} %collective-permute-done.1) | copy-start | bytes 1572868
  65.8 10.9 %collective-permute-start.2 = (bf16[1024,256]{1,0:T(8,128)(2,1)S(1)}, bf16[1024,256]{1,0:T(8,128)(2,1)S(1)}, u32[]{:S(2)}, u32[]{:S(2)}) collective-permute-start(bf16[1024,256]{1,0:T(8,128)(2,1)S(1)} %collective-permute-done.1), channel_id=1, source_target_pairs={{0,1},{1,2},{2,3},{3,4},{4,5},{5,6},{6,7},{7,0},{8,15},{9,8},{10,9... | collective-permute-start | bytes 1572872 | tf_op jit(solution)/shard_map/ppermute | solution.py:66
  71.1 11.3 %collective-permute-start.9 = (bf16[1024,256]{1,0:T(8,128)(2,1)S(1)}, bf16[1024,256]{1,0:T(8,128)(2,1)S(1)}, u32[]{:S(2)}, u32[]{:S(2)}) collective-permute-start(bf16[1024,256]{1,0:T(8,128)(2,1)S(1)} %collective-permute-done.8), channel_id=1, source_target_pairs={{0,1},{1,2},{2,3},{3,4},{4,5},{5,6},{6,7},{7,0},{8,15},{9,8},{10,9... | collective-permute-start | bytes 1572872 | tf_op jit(solution)/shard_map/ppermute | solution.py:66
  76.7 17.1 %copy-start.11 = (bf16[1024,256]{1,0:T(8,128)(2,1)}, bf16[1024,256]{1,0:T(8,128)(2,1)S(1)}, u32[]{:S(2)}) copy-start(bf16[1024,256]{1,0:T(8,128)(2,1)S(1)} %collective-permute-done.2) | copy-start | bytes 1572868
  76.7 17.1 %collective-permute-start.3 = (bf16[1024,256]{1,0:T(8,128)(2,1)S(1)}, bf16[1024,256]{1,0:T(8,128)(2,1)}, u32[]{:S(2)}, u32[]{:S(2)}) collective-permute-start(bf16[1024,256]{1,0:T(8,128)(2,1)S(1)} %collective-permute-done.2), channel_id=1, source_target_pairs={{0,1},{1,2},{2,3},{3,4},{4,5},{5,6},{6,7},{7,0},{8,15},{9,8},{10,9... | collective-permute-start | bytes 1572872 | tf_op jit(solution)/shard_map/ppermute | solution.py:66
  82.4 11.2 %collective-permute-start.10 = (bf16[1024,256]{1,0:T(8,128)(2,1)S(1)}, bf16[1024,256]{1,0:T(8,128)(2,1)S(1)}, u32[]{:S(2)}, u32[]{:S(2)}) collective-permute-start(bf16[1024,256]{1,0:T(8,128)(2,1)S(1)} %collective-permute-done.9), channel_id=1, source_target_pairs={{0,1},{1,2},{2,3},{3,4},{4,5},{5,6},{6,7},{7,0},{8,15},{9,8},{10,9... | collective-permute-start | bytes 1572872 | tf_op jit(solution)/shard_map/ppermute | solution.py:66
  99.7 20.5 %all-to-all-start.2 = ((bf16[32,8,1280]{2,1,0:T(8,128)(2,1)}), bf16[32,8,1280]{2,1,0:T(8,128)(2,1)}, u32[]{:S(2)}, u32[]{:S(2)}) async-start(bf16[32,8,1280]{2,1,0:T(8,128)(2,1)} %bitcast.99), calls=%async_computation.2 | async-start | bytes 1310720 | tf_op jit(solution)/shard_map/all_to_all | solution.py:17
  108.5 19.9 %copy-start.10 = (bf16[1024,256]{1,0:T(8,128)(2,1)S(1)}, bf16[1024,256]{1,0:T(8,128)(2,1)}, u32[]{:S(2)}) copy-start(bf16[1024,256]{1,0:T(8,128)(2,1)} %copy-done.9) | copy-start | bytes 1572868
  110.9 19.0 %copy-start.3 = (bf16[1024,256]{1,0:T(8,128)(2,1)S(1)}, bf16[1024,256]{1,0:T(8,128)(2,1)}, u32[]{:S(2)}) copy-start(bf16[1024,256]{1,0:T(8,128)(2,1)} %copy-done.2) | copy-start | bytes 1572868
  122.7 21.9 %all-to-all-start.3 = ((bf16[32,8,2048]{2,1,0:T(8,128)(2,1)}), bf16[32,8,2048]{2,1,0:T(8,128)(2,1)}, u32[]{:S(2)}, u32[]{:S(2)}) async-start(bf16[32,8,2048]{2,1,0:T(8,128)(2,1)} %broadcast_in_dim.18), calls=%async_computation.3 | async-start | bytes 2097152 | tf_op jit(solution)/shard_map/all_to_all | solution.py:13
  127.4 17.2 %copy-start.13 = (bf16[8,8,8,256]{3,2,0,1:T(8,128)(2,1)S(1)}, bf16[8,8,8,256]{3,2,0,1:T(8,128)(2,1)}, u32[]{:S(2)}) copy-start(bf16[8,8,8,256]{3,2,0,1:T(8,128)(2,1)} %copy.38) | copy-start | bytes 786436
  131.2 22.6 %collective-permute-start.4 = (bf16[1024,256]{1,0:T(8,128)(2,1)}, bf16[1024,256]{1,0:T(8,128)(2,1)}, u32[]{:S(2)}, u32[]{:S(2)}) collective-permute-start(bf16[1024,256]{1,0:T(8,128)(2,1)} %collective-permute-done.3), channel_id=1, source_target_pairs={{0,1},{1,2},{2,3},{3,4},{4,5},{5,6},{6,7},{7,0},{8,15},{9,8},{10,9... | collective-permute-start | bytes 1572872 | tf_op jit(solution)/shard_map/ppermute | solution.py:66
  131.6 24.8 %collective-permute-start.11 = (bf16[1024,256]{1,0:T(8,128)(2,1)S(1)}, bf16[1024,256]{1,0:T(8,128)(2,1)}, u32[]{:S(2)}, u32[]{:S(2)}) collective-permute-start(bf16[1024,256]{1,0:T(8,128)(2,1)S(1)} %collective-permute-done.10), channel_id=1, source_target_pairs={{0,1},{1,2},{2,3},{3,4},{4,5},{5,6},{6,7},{7,0},{8,15},{9,8},{10,9... | collective-permute-start | bytes 1572872 | tf_op jit(solution)/shard_map/ppermute | solution.py:66
  147.0 15.6 %all-to-all-start.4 = ((bf16[8,256,64]{1,2,0:T(8,128)(2,1)}), bf16[8,256,64]{1,2,0:T(8,128)(2,1)S(1)}, u32[]{:S(2)}, u32[]{:S(2)}) async-start(bf16[8,256,64]{1,2,0:T(8,128)(2,1)} %broadcast_in_dim.19), calls=%async_computation.4 | async-start | bytes 524288 | tf_op jit(solution)/shard_map/all_to_all | solution.py:13
  153.8 43.3 %collective-permute-start.5 = (bf16[1024,256]{1,0:T(8,128)(2,1)}, bf16[1024,256]{1,0:T(8,128)(2,1)}, u32[]{:S(2)}, u32[]{:S(2)}) collective-permute-start(bf16[1024,256]{1,0:T(8,128)(2,1)} %collective-permute-done.4), channel_id=1, source_target_pairs={{0,1},{1,2},{2,3},{3,4},{4,5},{5,6},{6,7},{7,0},{8,15},{9,8},{10,9... | collective-permute-start | bytes 1572872 | tf_op jit(solution)/shard_map/ppermute | solution.py:66
  156.4 40.7 %collective-permute-start.12 = (bf16[1024,256]{1,0:T(8,128)(2,1)}, bf16[1024,256]{1,0:T(8,128)(2,1)}, u32[]{:S(2)}, u32[]{:S(2)}) collective-permute-start(bf16[1024,256]{1,0:T(8,128)(2,1)} %collective-permute-done.11), channel_id=1, source_target_pairs={{0,1},{1,2},{2,3},{3,4},{4,5},{5,6},{6,7},{7,0},{8,15},{9,8},{10,9... | collective-permute-start | bytes 1572872 | tf_op jit(solution)/shard_map/ppermute | solution.py:66
  162.7 12.6 %copy-start.6 = (f32[1024,256]{1,0:T(8,128)S(1)}, f32[1024,256]{1,0:T(8,128)}, u32[]{:S(2)}) copy-start(f32[1024,256]{1,0:T(8,128)} %convolution_add_fusion.3) | copy-start | bytes 3145732
  171.0 13.1 %all-to-all-start.5 = ((bf16[32,2,2048]{2,1,0:T(2,128)(2,1)}), bf16[32,2,2048]{2,1,0:T(2,128)(2,1)S(1)}, u32[]{:S(2)}, u32[]{:S(2)}) async-start(bf16[32,2,2048]{2,1,0:T(2,128)(2,1)} %reshape.172), calls=%async_computation.5 | async-start | bytes 524288 | tf_op jit(solution)/shard_map/all_to_all | solution.py:17
  190.6 21.6 %all-to-all-start.6 = ((bf16[32,64,256]{2,1,0:T(8,128)(2,1)}), bf16[32,64,256]{2,1,0:T(8,128)(2,1)}, u32[]{:S(2)}, u32[]{:S(2)}) async-start(bf16[32,64,256]{2,1,0:T(8,128)(2,1)} %broadcast_in_dim.20), calls=%async_computation.6 | async-start | bytes 2097152 | tf_op jit(solution)/shard_map/all_to_all | solution.py:13
  197.1 8.6 %collective-permute-start.13 = (bf16[1024,256]{1,0:T(8,128)(2,1)}, bf16[1024,256]{1,0:T(8,128)(2,1)S(1)}, u32[]{:S(2)}, u32[]{:S(2)}) collective-permute-start(bf16[1024,256]{1,0:T(8,128)(2,1)} %collective-permute-done.12), channel_id=1, source_target_pairs={{0,1},{1,2},{2,3},{3,4},{4,5},{5,6},{6,7},{7,0},{8,15},{9,8},{10,9... | collective-permute-start | bytes 1572872 | tf_op jit(solution)/shard_map/ppermute | solution.py:66
  197.1 22.7 %collective-permute-start.6 = (bf16[1024,256]{1,0:T(8,128)(2,1)}, bf16[1024,256]{1,0:T(8,128)(2,1)}, u32[]{:S(2)}, u32[]{:S(2)}) collective-permute-start(bf16[1024,256]{1,0:T(8,128)(2,1)} %collective-permute-done.5), channel_id=1, source_target_pairs={{0,1},{1,2},{2,3},{3,4},{4,5},{5,6},{6,7},{7,0},{8,15},{9,8},{10,9... | collective-permute-start | bytes 1572872 | tf_op jit(solution)/shard_map/ppermute | solution.py:66
  (4 other events, 32.2 us)
Sparse Core Ops, SparseCore 0:
  45.7 51.3 all-gather.1

commit v3 on v2

v3 whole, which is shorter than its diff:
```python
import jax
import jax.numpy as jnp
from jax import lax
from jax.experimental import pallas as pl
from jax.experimental.pallas import tpu as pltpu
from jax.sharding import PartitionSpec as P


F32 = jnp.float32
BF16 = jnp.bfloat16
VMEM = pl.BlockSpec(memory_space=pltpu.VMEM)
LIMIT = 40 * 1024 * 1024


def copy_for_each(shard, axis):
    copies = jnp.broadcast_to(shard, (lax.axis_size(axis), *shard.shape))
    return lax.all_to_all(copies, axis, split_axis=0, concat_axis=0, tiled=True)


def exchange(parts, axis):
    return lax.all_to_all(parts, axis, split_axis=0, concat_axis=0, tiled=True)


def contract_last(a, b):
    return lax.dot_general(a, b, (((1,), (1,)), ((), ())), preferred_element_type=F32)


def product(a, b):
    return jnp.dot(a, b, preferred_element_type=F32)


def three_parts(x):
    a = lax.reduce_precision(x, 8, 7)
    b = lax.reduce_precision(x - a, 8, 7)
    c = x - a - b
    return [part.astype(BF16) for part in (a, b, c)]


def divided(lam_row, lam_col, first_row):
    on_diag = (
        (first_row + jnp.arange(lam_row.shape[0], dtype=jnp.int32))[:, None]
        == jnp.arange(lam_col.shape[0], dtype=jnp.int32)[None, :]
    )
    root_row = lam_row ** (-0.5)
    root_col = lam_col ** (-0.5)
    gaps_lam = lam_row[:, None] - lam_col[None, :]
    safe_gap = jnp.where(on_diag, jnp.ones_like(gaps_lam), gaps_lam)
    off_diag = (root_row[:, None] - root_col[None, :]) / safe_gap
    diag_vals = -0.5 * lam_row[:, None] ** (-1.5) + jnp.zeros_like(gaps_lam)
    return jnp.where(on_diag, diag_vals, off_diag)


def cost(flops, nbytes):
    return pl.CostEstimate(flops=flops, bytes_accessed=nbytes, transcendentals=0)


def params():
    return pltpu.CompilerParams(vmem_limit_bytes=LIMIT)


def gram_body(hops, half, n, own_ref, mean_ref, told_ref, *refs):
    out_ref = refs[-1]
    xt, gt = own_ref[:, :n], own_ref[:, n:]
    sum_x = jnp.sum(xt.astype(F32), axis=1, keepdims=True)
    sum_g = jnp.sum(gt.astype(F32), axis=1, keepdims=True)
    mean_x, mean_g = mean_ref[:, 0:1], mean_ref[:, 1:2]
    width = xt.shape[0]
    for i, h in enumerate(hops):
        grads, inputs = refs[2 * i][...], refs[2 * i + 1][...]
        there_x, there_g = told_ref[2 * i : 2 * i + 1, :], told_ref[2 * i + 1 : 2 * i + 2, :]
        left_g = jnp.sum(grads.astype(F32), axis=0, keepdims=True) - n * there_g
        value = product(xt, grads) - (sum_x * there_g + mean_x * left_g)
        if h > 0:
            left_x = jnp.sum(inputs.astype(F32), axis=0, keepdims=True) - n * there_x
            value += product(gt, inputs) - (sum_g * there_x + mean_g * left_x)
        if h == half:
            value = 0.5 * value
        out_ref[:, i * width : (i + 1) * width] = value.astype(BF16)


def gram_first(own, mean_cols, told, blocks, half):
    width, n = own.shape[0], own.shape[1] // 2
    flat = [b for pair in blocks for b in pair]
    return pl.pallas_call(
        lambda *refs: gram_body(range(half), half, n, *refs),
        out_shape=jax.ShapeDtypeStruct((width, (half + 1) * width), BF16),
        grid=(1,),
        in_specs=[VMEM] * (3 + len(flat)),
        out_specs=pl.BlockSpec((width, half * width), lambda i: (0, 0)),
        compiler_params=params(),
        cost_estimate=cost(4 * half * n * width * width, 2 * n * width * 2 * (half + 1)),
        name="gram_first",
    )(own, mean_cols, told, *flat)


def gram_last(partial, own, mean_cols, told, block, half):
    width, n = own.shape[0], own.shape[1] // 2

    def body(partial_ref, *refs):
        gram_body((half,), half, n, *refs)

    return pl.pallas_call(
        body,
        out_shape=jax.ShapeDtypeStruct(partial.shape, BF16),
        grid=(1,),
        in_specs=[pl.BlockSpec(memory_space=pl.ANY)] + [VMEM] * 5,
        out_specs=pl.BlockSpec((width, width), lambda i: (0, half)),
        input_output_aliases={0: 0},
        compiler_params=params(),
        cost_estimate=cost(4 * n * width * width, 8 * n * width),
        name="gram_last",
    )(partial, own, mean_cols, told, *block)


def gathered_sum(got, width, half):
    groups, few, _ = got.shape

    def body(got_ref, out_ref):
        def add(i, sums):
            return sums[0] + got_ref[2 * i].astype(F32), sums[1] + got_ref[2 * i + 1].astype(F32)

        zero = jnp.zeros(got_ref.shape[1:], F32)
        down, up = lax.fori_loop(0, groups // 2, add, (zero, zero))
        piece = lambda a, h: a[:, h * width : (h + 1) * width]
        pair = [piece(down, 0) + piece(up, 0)]
        pair += [piece(up, h) for h in range(1, half)]
        pair += [piece(down, half) + piece(up, half)]
        pair += [piece(down, h) for h in range(half - 1, 0, -1)]
        value = jnp.concatenate(pair, axis=1).astype(BF16)

        def store(i, carry):
            out_ref[i] = value
            return carry

        lax.fori_loop(0, groups, store, 0)

    return pl.pallas_call(
        body,
        out_shape=jax.ShapeDtypeStruct((groups, few, 2 * half * width), BF16),
        in_specs=[VMEM],
        out_specs=VMEM,
        compiler_params=params(),
        cost_estimate=cost(2 * got.size, 4 * got.size),
        name="gathered_sum",
    )(got)


def rotated_cols(basis_t, right):
    dim, narrow = right.shape
    rows = 256

    def body(basis_ref, right_ref, out_ref, low_ref):
        value = product(basis_ref[...], right_ref[...])
        out_ref[...] = value
        low_ref[...] = value.astype(BF16)

    block = pl.BlockSpec((rows, narrow), lambda i: (i, 0))
    return pl.pallas_call(
        body,
        out_shape=[
            jax.ShapeDtypeStruct((dim, narrow), F32),
            jax.ShapeDtypeStruct((dim, narrow), BF16),
        ],
        grid=(dim // rows,),
        in_specs=[
            pl.BlockSpec((rows, dim), lambda i: (i, 0)),
            pl.BlockSpec((dim, narrow), lambda i: (0, 0)),
        ],
        out_specs=[block, block],
        compiler_params=params(),
        cost_estimate=cost(2 * dim * dim * narrow, 2 * dim * dim),
        name="rotated_cols",
    )(basis_t, right)


def undone_copies(rot, back, kernel_t, basis_t, plane, groups, width):
    dim, narrow = rot.shape

    def body(plane_ref, rot_ref, back_ref, kernel_ref, basis_ref, out_ref):
        scaled = (rot_ref[...].T + back_ref[...].astype(F32)) * kernel_ref[...]
        high = scaled.astype(BF16)
        low = (scaled - high.astype(F32)).astype(BF16)
        basis = basis_ref[...]
        value = (product(high, basis) + product(low, basis)).astype(BF16)

        def store(i, carry):
            out_ref[i] = value
            return carry

        lax.fori_loop(0, groups, store, 0)

    full = lambda shape: pl.BlockSpec(shape, lambda i, plane_ref: (0,) * len(shape))
    return pl.pallas_call(
        body,
        out_shape=jax.ShapeDtypeStruct((groups, narrow, width), BF16),
        grid_spec=pltpu.PrefetchScalarGridSpec(
            num_scalar_prefetch=1,
            grid=(1,),
            in_specs=[
                full((dim, narrow)),
                full((narrow, dim)),
                full((narrow, dim)),
                pl.BlockSpec((dim, width), lambda i, plane_ref: (0, plane_ref[0])),
            ],
            out_specs=full((groups, narrow, width)),
        ),
        compiler_params=params(),
        cost_estimate=cost(4 * dim * narrow * width, 4 * dim * width),
        name="undone_copies",
    )(plane, rot, back, kernel_t, basis_t)


def first_product(places, told, whiten, blocks):
    n, width = blocks[0][0].shape
    dim = whiten.shape[0]
    planes = len(blocks)
    rows = 256

    def body(place_ref, told_ref, whiten_ref, *refs):
        centered_ref, out_ref = refs[-2:]
        total = jnp.zeros((rows, width), F32)
        for h in range(planes):
            at = pl.ds(pl.multiple_of(place_ref[h] * width, width), width)
            mean_x, mean_g = told_ref[2 * h : 2 * h + 1, :], told_ref[2 * h + 1 : 2 * h + 2, :]
            shifted = (refs[2 * h][...].astype(F32) - mean_g).astype(BF16)
            total += product(shifted, whiten_ref[at, :])
            centered_ref[:, at] = (refs[2 * h + 1][...].astype(F32) - mean_x).astype(BF16)
        out_ref[...] = total

    full = lambda shape: pl.BlockSpec(shape, lambda i, place_ref: (0,) * len(shape))
    part = lambda cols: pl.BlockSpec((rows, cols), lambda i, place_ref: (i, 0))
    flat = [b for pair in blocks for b in pair]
    return pl.pallas_call(
        body,
        out_shape=[
            jax.ShapeDtypeStruct((n, dim), BF16),
            jax.ShapeDtypeStruct((n, width), F32),
        ],
        grid_spec=pltpu.PrefetchScalarGridSpec(
            num_scalar_prefetch=1,
            grid=(n // rows,),
            in_specs=[full(told.shape), full(whiten.shape)] + [part(width)] * len(flat),
            out_specs=[part(dim), part(width)],
        ),
        compiler_params=params(),
        cost_estimate=cost(2 * n * dim * width, 6 * n * dim),
        name="first_product",
    )(places, told, whiten, *flat)


def last_product(undone, basis_t, centered, running, scale):
    dim, width = undone.shape
    n = centered.shape[0]
    cols = 256

    def body(undone_ref, basis_ref, centered_ref, running_ref, out_ref, turned_ref, total_ref):
        step = pl.program_id(0)

        @pl.when(step == 0)
        def _():
            turned_ref[...] = undone_ref[...].T
            total_ref[...] = running_ref[...]

        sens = (product(turned_ref[...], basis_ref[...]) * scale).astype(BF16)
        total_ref[...] += contract_last(centered_ref[...], sens)

        @pl.when(step == pl.num_programs(0) - 1)
        def _():
            out_ref[...] = total_ref[...].astype(BF16)

    full = lambda shape: pl.BlockSpec(shape, lambda i: (0,) * len(shape))
    return pl.pallas_call(
        body,
        out_shape=jax.ShapeDtypeStruct((n, width), BF16),
        grid=(dim // cols,),
        in_specs=[
            full((dim, width)),
            pl.BlockSpec((dim, cols), lambda i: (0, i)),
            pl.BlockSpec((n, cols), lambda i: (0, i)),
            full((n, width)),
        ],
        out_specs=full((n, width)),
        scratch_shapes=[pltpu.VMEM((width, dim), BF16), pltpu.VMEM((n, width), F32)],
        compiler_params=params(),
        cost_estimate=cost(2 * dim * width * (dim + n), 2 * dim * (dim + n)),
        name="last_product",
    )(undone, basis_t, centered, running)


def local(features, grad_out, eigvecs, eigvals, whiten):
    n, width = features.shape
    groups, planes = lax.axis_size("rows"), lax.axis_size("feat")
    total = n * groups
    dim = width * planes
    narrow = eigvecs.shape[1]
    half = planes // 2
    r, f = lax.axis_index("rows"), lax.axis_index("feat")
    way = jnp.where(r % 2 == 0, -1, 1)

    def pass_on(value, hops=1):
        pairs = [
            (a * planes + b, a * planes + (b + (hops if a % 2 == 0 else -hops)) % planes)
            for a in range(groups)
            for b in range(planes)
        ]
        return lax.ppermute(value, ("rows", "feat"), pairs)

    blocks = [(grad_out, features)]
    for _ in range(1, planes):
        blocks.append(tuple(pass_on(b) for b in blocks[-1]))

    sums = jnp.stack([jnp.sum(a, axis=0, dtype=F32) for a in (features, grad_out)])
    means = jnp.sum(copy_for_each(sums, "rows"), axis=0) / total
    packed = jnp.concatenate(three_parts(means))
    told = [packed, pass_on(packed)]
    told.append(pass_on(packed, 2))
    for _ in range(3, planes):
        told.append(pass_on(told[-1]))
    told = [jnp.sum(t.astype(F32).reshape(3, 2, width), axis=0) for t in told]

    basis_rt = copy_for_each(eigvecs.astype(BF16).T, "feat")
    basis_rt = jnp.swapaxes(basis_rt, 0, 1).reshape(narrow, dim)
    basis_t = lax.all_gather(basis_rt, "rows", axis=0, tiled=True)

    own = jnp.concatenate([features.T, grad_out.T], axis=1)
    mean_cols = means.T
    mixed = gram_first(own, mean_cols, jnp.concatenate(told[:half]), blocks[:half], half)
    mixed = gram_last(mixed, own, mean_cols, told[half], blocks[half], half)

    got = exchange(mixed.reshape(groups, width // groups, -1), "rows")
    copies = gathered_sum(got, width, half)
    gram = exchange(copies, "rows").reshape(width, dim)

    twice = jnp.concatenate([basis_rt, basis_rt], axis=1)
    turned = lax.dynamic_slice_in_dim(twice, f * width, dim, axis=1)
    right = contract_last(gram, turned).astype(BF16)
    right = copy_for_each(right, "feat").reshape(dim, narrow)
    rot, low = rotated_cols(basis_t, right)
    back = exchange(low.reshape(groups, narrow, narrow), "rows")
    back = jnp.swapaxes(back, 0, 1).reshape(narrow, dim)
    first = r * narrow
    kernel_t = divided(lax.dynamic_slice_in_dim(eigvals, first, narrow), eigvals, first)

    copies = undone_copies(rot, back, kernel_t, basis_t, f[None], groups, width)
    undone = exchange(copies, "rows").reshape(dim, width)

    places = ((f + way * jnp.arange(planes, dtype=jnp.int32)) % planes).astype(jnp.int32)
    centered, running = first_product(places, jnp.concatenate(told), whiten, blocks)
    return last_product(undone, basis_t, centered, running, 1.0 / total)


def solution(mesh):
    in_specs = (P("rows", "feat"), P("rows", "feat"), P("feat", "rows"), P(), P(None, "feat"))
    out_specs = P("rows", "feat")
    return jax.shard_map(local, mesh=mesh, in_specs=in_specs, out_specs=out_specs, check_vma=False)
```

time: 230 us -> 255 us (1.11)
  the two profiles are of different devices: /device:TPU:1 before, /device:TPU:2 now
where the time goes in v3:
time: 255 us; the launch traced here: 254 us
  waiting for transfers between devices  104 us (41%)
  blocking collectives  39.1 us (15%)
  starting transfers between devices  35 us (14%)
  Pallas kernels  29.4 us (12%)
  local copies, waits for them, and re-layouts  28 us (11%)
  between operations  13.8 us (5%)
  other arithmetic  4.2 us (2%)
    ppermute x21, waiting for transfers between devices, pass_on(): return lax.ppermute(value, ('rows', 'feat'), pairs)  67.1 us
    all_to_all x3, waiting for transfers between devices, exchange(): return lax.all_to_all(parts, axis, split_axis=0, concat_axis=0, tiled=True)  23.2 us
    unnamed x40, local copies, waits for them, and re-layouts  22.3 us
    all_to_all x1, blocking collectives, copy_for_each(): return lax.all_to_all(copies, axis, split_axis=0, concat_axis=0, tiled=True)  20.1 us
    all_to_all x1, blocking collectives, exchange(): return lax.all_to_all(parts, axis, split_axis=0, concat_axis=0, tiled=True)  19 us
    all_to_all x3, starting transfers between devices, exchange(): return lax.all_to_all(parts, axis, split_axis=0, concat_axis=0, tiled=True)  15.2 us
    all_to_all x2, waiting for transfers between devices, copy_for_each(): return lax.all_to_all(copies, axis, split_axis=0, concat_axis=0, tiled=True)  13.7 us
    pallas_call x1, Pallas kernels, last_product(): pl.pallas_call(body, out_shape=jax.ShapeDtypeStruct((n, width), BF16), gr...  11.1 us
  transfers between devices with their start and end apart: 27, of which 15 were waited for; matrix products, arithmetic and copies ran while one was open for 5% of the time, Pallas kernels for 7%

profile of v3, /device:TPU:2, one launch (start us, length us, event | category | flops | bytes accessed | tf_op | source)
XLA Modules:
  0.0 253.8 jit_solution(4137944221683092730)
XLA Ops:
  7.5 20.1 %all_to_all.35 = bf16[8,64,256]{2,1,0:T(8,128)(2,1)S(1)} all-to-all(bf16[8,64,256]{2,1,0:T(8,128)(2,1)S(1)} %broadcast_in_dim.11), channel_id=1, replica_groups=mesh['rows'=32,'feat'=8] {'feat'}, dimensions={0} | all-to-all | bytes 524288 | tf_op jit(solution)/shard_map/all_to_all | solution.py:17
  29.1 9.9 %collective-permute-done.3.refs_5_.refs_2_ = bf16[1024,256]{1,0:T(8,128)(2,1)S(1)} collective-permute-done((bf16[1024,256]{1,0:T(8,128)(2,1)}, bf16[1024,256]{1,0:T(8,128)(2,1)S(1)}, u32[]{:S(2)}, u32[]{:S(2)}) %collective-permute-start.3) | collective-permute-done | bytes 524320 | tf_op jit(solution)/shard_map/ppermute | solution.py:306
  39.1 5.6 %collective-permute-done.4.refs_6_.refs_3_ = bf16[1024,256]{1,0:T(8,128)(2,1)S(1)} collective-permute-done((bf16[1024,256]{1,0:T(8,128)(2,1)}, bf16[1024,256]{1,0:T(8,128)(2,1)S(1)}, u32[]{:S(2)}, u32[]{:S(2)}) %collective-permute-start.4) | collective-permute-done | bytes 524320 | tf_op jit(solution)/shard_map/ppermute | solution.py:306
  46.7 7.6 %all-to-all-start.1 = ((f32[32,2,256]{2,1,0:T(2,128)}), f32[32,2,256]{2,1,0:T(2,128)S(1)}, u32[]{:S(2)}, u32[]{:S(2)}) async-start(f32[32,2,256]{2,1,0:T(2,128)} %broadcast_in_dim.24), calls=%async_computation.1 | async-start | bytes 131072 | tf_op jit(solution)/shard_map/all_to_all | solution.py:17
  55.9 4.7 %all-to-all-done.1 = f32[32,2,256]{2,1,0:T(2,128)S(1)} async-done(((f32[32,2,256]{2,1,0:T(2,128)}), f32[32,2,256]{2,1,0:T(2,128)S(1)}, u32[]{:S(2)}, u32[]{:S(2)}) %all-to-all-start.1) | async-done | bytes 65568 | tf_op jit(solution)/shard_map/all_to_all | solution.py:17
  61.2 3.8 %collective-permute-done.7.refs_9_.refs_6_ = bf16[1024,256]{1,0:T(8,128)(2,1)} collective-permute-done((bf16[1024,256]{1,0:T(8,128)(2,1)S(1)}, bf16[1024,256]{1,0:T(8,128)(2,1)}, u32[]{:S(2)}, u32[]{:S(2)}) %collective-permute-start.7) | collective-permute-done | bytes 524320 | tf_op jit(solution)/shard_map/ppermute | solution.py:306
  64.9 5.6 %collective-permute-done.8.refs_10_.refs_7_ = bf16[1024,256]{1,0:T(8,128)(2,1)} collective-permute-done((bf16[1024,256]{1,0:T(8,128)(2,1)S(1)}, bf16[1024,256]{1,0:T(8,128)(2,1)}, u32[]{:S(2)}, u32[]{:S(2)}) %collective-permute-start.8) | collective-permute-done | bytes 524320 | tf_op jit(solution)/shard_map/ppermute | solution.py:306
  74.6 8.6 %collective-permute-done.1 = bf16[6,256]{1,0:T(8,128)(2,1)S(1)} collective-permute-done((bf16[6,256]{1,0:T(8,128)(2,1)S(1)}, bf16[6,256]{1,0:T(8,128)(2,1)S(1)}, u32[]{:S(2)}, u32[]{:S(2)}) %collective-permute-start.1) | collective-permute-done | bytes 3104 | tf_op jit(solution)/shard_map/ppermute | solution.py:306
  84.6 3.4 %collective-permute-done.2 = bf16[6,256]{1,0:T(8,128)(2,1)S(1)} collective-permute-done((bf16[6,256]{1,0:T(8,128)(2,1)S(1)}, bf16[6,256]{1,0:T(8,128)(2,1)S(1)}, u32[]{:S(2)}, u32[]{:S(2)}) %collective-permute-start.2) | collective-permute-done | bytes 3104 | tf_op jit(solution)/shard_map/ppermute | solution.py:306
  88.4 4.8 %collective-permute-done.9 = bf16[6,256]{1,0:T(8,128)(2,1)S(1)} collective-permute-done((bf16[6,256]{1,0:T(8,128)(2,1)S(1)}, bf16[6,256]{1,0:T(8,128)(2,1)S(1)}, u32[]{:S(2)}, u32[]{:S(2)}) %collective-permute-start.9) | collective-permute-done | bytes 3104 | tf_op jit(solution)/shard_map/ppermute | solution.py:306
  95.3 2.8 %gram_first.1.partial_ref = bf16[256,1280]{1,0:T(8,128)(2,1)S(1)} custom-call(bf16[256,2048]{1,0:T(8,128)(2,1)S(1)} %pad_maximum_fusion.refs_0_, f32[256,2]{1,0:T(8,128)S(1)} %get-tuple-element.17.refs_1_, f32[8,256]{1,0:T(8,128)S(1)} %pad_maximum_fusion.1.refs_2_, bf16[1024,256]{1,0:T(8,128)(2,1)S(1)} %copy-done.2, bf16[1024,256]{1,0:T(8,128)(2,1)S(1)} %copy-done.3, ...), custom_call_target="tpu_custom_call" | custom-call | flops 1073741824 | bytes 5242880 | tf_op jit(solution)/shard_map/gram_first/pallas_call | solution.py:84
  98.0 1.9 gram_last.1
  99.9 19.0 %all_to_all.36.got_ref = bf16[32,8,1280]{2,1,0:T(8,128)(2,1)S(1)} all-to-all(bf16[32,8,1280]{2,1,0:T(8,128)(2,1)S(1)} %bitcast.20), channel_id=1, replica_groups=mesh['rows'=32,'feat'=8] {'rows'}, dimensions={0} | all-to-all | bytes 1310720 | tf_op jit(solution)/shard_map/all_to_all | solution.py:21
  120.3 5.1 %all-to-all-start.3 = ((bf16[32,8,2048]{2,1,0:T(8,128)(2,1)}), bf16[32,8,2048]{2,1,0:T(8,128)(2,1)S(1)}, u32[]{:S(2)}, u32[]{:S(2)}) async-start(bf16[32,8,2048]{2,1,0:T(8,128)(2,1)} %gathered_sum.1), calls=%async_computation.3 | async-start | bytes 2097152 | tf_op jit(solution)/shard_map/all_to_all | solution.py:21
  125.7 15.9 %all-to-all-done.3 = bf16[32,8,2048]{2,1,0:T(8,128)(2,1)S(1)} async-done(((bf16[32,8,2048]{2,1,0:T(8,128)(2,1)}), bf16[32,8,2048]{2,1,0:T(8,128)(2,1)S(1)}, u32[]{:S(2)}, u32[]{:S(2)}) %all-to-all-start.3) | async-done | bytes 1048608 | tf_op jit(solution)/shard_map/all_to_all | solution.py:21
  142.7 3.4 %all-to-all-start.4 = ((bf16[8,256,64]{1,2,0:T(8,128)(2,1)}), bf16[8,256,64]{1,2,0:T(8,128)(2,1)S(1)}, u32[]{:S(2)}, u32[]{:S(2)}) async-start(bf16[8,256,64]{1,2,0:T(8,128)(2,1)} %broadcast_in_dim.25), calls=%async_computation.4 | async-start | bytes 524288 | tf_op jit(solution)/shard_map/all_to_all | solution.py:17
  146.2 2.0 collective-permute-start.17
  149.7 9.0 %all-to-all-done.4 = bf16[8,256,64]{1,2,0:T(8,128)(2,1)S(1)} async-done(((bf16[8,256,64]{1,2,0:T(8,128)(2,1)}), bf16[8,256,64]{1,2,0:T(8,128)(2,1)S(1)}, u32[]{:S(2)}, u32[]{:S(2)}) %all-to-all-start.4) | async-done | bytes 262176 | tf_op jit(solution)/shard_map/all_to_all | solution.py:17
  159.0 3.4 %copy-done = bf16[2048,2048]{1,0:T(8,128)(2,1)S(1)} copy-done((bf16[2048,2048]{1,0:T(8,128)(2,1)S(1)}, bf16[2048,2048]{1,0:T(8,128)(2,1)}, u32[]{:S(2)}) %copy-start) | copy-done | bytes 8388632
  162.4 3.4 %rotated_cols.1 = (f32[2048,64]{1,0:T(8,128)S(1)}, bf16[2048,64]{1,0:T(8,128)(2,1)S(1)}) custom-call(bf16[2048,2048]{1,0:T(8,128)(2,1)S(1)} %copy-done, bf16[2048,64]{1,0:T(8,128)(2,1)S(1)} %bitcast.22), custom_call_target="tpu_custom_call" | custom-call | flops 536870912 | bytes 8388608 | tf_op jit(solution)/shard_map/rotated_cols/pallas_call | solution.py:158
  168.0 5.0 %all-to-all-start.5 = ((bf16[32,2,2048]{2,1,0:T(2,128)(2,1)}), bf16[32,2,2048]{2,1,0:T(2,128)(2,1)S(1)}, u32[]{:S(2)}, u32[]{:S(2)}) async-start(bf16[32,2,2048]{2,1,0:T(2,128)(2,1)} %reshape.114), calls=%async_computation.5 | async-start | bytes 524288 | tf_op jit(solution)/shard_map/all_to_all | solution.py:21
  173.2 7.3 %all-to-all-done.5 = bf16[32,2,2048]{2,1,0:T(2,128)(2,1)S(1)} async-done(((bf16[32,2,2048]{2,1,0:T(2,128)(2,1)}), bf16[32,2,2048]{2,1,0:T(2,128)(2,1)S(1)}, u32[]{:S(2)}, u32[]{:S(2)}) %all-to-all-start.5) | async-done | bytes 262176 | tf_op jit(solution)/shard_map/all_to_all | solution.py:21
  182.0 1.5 reshape.91.back_ref
  183.5 3.4 %copy-done.1 = bf16[2048,2048]{1,0:T(8,128)(2,1)S(1)} copy-done((bf16[2048,2048]{1,0:T(8,128)(2,1)S(1)}, bf16[2048,2048]{1,0:T(8,128)(2,1)}, u32[]{:S(2)}) %copy-start.1) | copy-done | bytes 8388632
  188.1 1.8 undone_copies.1
  189.9 5.1 %all-to-all-start.6 = ((bf16[32,64,256]{2,1,0:T(8,128)(2,1)}), bf16[32,64,256]{2,1,0:T(8,128)(2,1)S(1)}, u32[]{:S(2)}, u32[]{:S(2)}) async-start(bf16[32,64,256]{2,1,0:T(8,128)(2,1)} %undone_copies.1), calls=%async_computation.6 | async-start | bytes 2097152 | tf_op jit(solution)/shard_map/all_to_all | solution.py:21
  197.1 14.3 %collective-permute-done.12 = bf16[6,256]{1,0:T(8,128)(2,1)S(1)} collective-permute-done((bf16[6,256]{1,0:T(8,128)(2,1)S(1)}, bf16[6,256]{1,0:T(8,128)(2,1)S(1)}, u32[]{:S(2)}, u32[]{:S(2)}) %collective-permute-start.12) | collective-permute-done | bytes 3104 | tf_op jit(solution)/shard_map/ppermute | solution.py:306
  211.4 4.8 %collective-permute-done.13 = bf16[6,256]{1,0:T(8,128)(2,1)S(1)} collective-permute-done((bf16[6,256]{1,0:T(8,128)(2,1)S(1)}, bf16[6,256]{1,0:T(8,128)(2,1)S(1)}, u32[]{:S(2)}, u32[]{:S(2)}) %collective-permute-start.13) | collective-permute-done | bytes 3104 | tf_op jit(solution)/shard_map/ppermute | solution.py:306
  216.3 4.7 %collective-permute-done.14 = bf16[6,256]{1,0:T(8,128)(2,1)S(1)} collective-permute-done((bf16[6,256]{1,0:T(8,128)(2,1)S(1)}, bf16[6,256]{1,0:T(8,128)(2,1)S(1)}, u32[]{:S(2)}, u32[]{:S(2)}) %collective-permute-start.14) | collective-permute-done | bytes 3104 | tf_op jit(solution)/shard_map/ppermute | solution.py:306
  224.4 7.0 %first_product.1 = (bf16[1024,2048]{1,0:T(8,128)(2,1)}, f32[1024,256]{1,0:T(8,128)S(1)}) custom-call(s32[8]{0:T(128)S(1)} %and_select_fusion.place_ref, f32[16,256]{1,0:T(8,128)S(1)} %concatenate.19.told_ref, bf16[2048,256]{1,0:T(8,128)(2,1)S(1)} %copy-done.11, bf16[1024,256]{1,0:T(8,128)(2,1)S(1)} %copy-done.2, bf16[1024,256]{1,0:T(8,128)(2,1)S(1)} %copy-done.3, ...), custom_call_target="tpu_custom_call" | custom-call | flops 1073741824 | bytes 12582912 | tf_op jit(solution)/shard_map/first_product/pallas_call | solution.py:233
  232.5 2.2 copy-done.4
  235.9 11.1 %last_product.1 = bf16[1024,256]{1,0:T(8,128)(2,1)} custom-call(bf16[2048,256]{1,0:T(8,128)(2,1)S(1)} %bitcast.21, bf16[2048,2048]{1,0:T(8,128)(2,1)} %all-gather.2.cloned.1.call-done.basis_ref, bf16[1024,2048]{1,0:T(8,128)(2,1)S(1)} %copy-done.4, f32[1024,256]{1,0:T(8,128)S(1)} %copy-done.15), custom_call_target="tpu_custom_call" | custom-call | flops 3221225472 | bytes 12582912 | tf_op jit(solution)/shard_map/last_product/pallas_call | solution.py:272
  (117 shorter events, 31.9 us)
Async XLA Ops:
  6.5 39.3 %copy-start.2 = (bf16[1024,256]{1,0:T(8,128)(2,1)S(1)}, bf16[1024,256]{1,0:T(8,128)(2,1)}, u32[]{:S(2)}) copy-start(bf16[1024,256]{1,0:T(8,128)(2,1)} %refs_0_.1) | copy-start | bytes 1572868
  6.5 64.6 %copy-start.3 = (bf16[1024,256]{1,0:T(8,128)(2,1)S(1)}, bf16[1024,256]{1,0:T(8,128)(2,1)}, u32[]{:S(2)}) copy-start(bf16[1024,256]{1,0:T(8,128)(2,1)} %refs_1_.1) | copy-start | bytes 1572868
  6.5 152.4 %all-gather.2.cloned.1.call-start = ((), (), s32[]{:S(2)}) async-start(), calls=%async_computation.7 | async-start | bytes 8650752 | tf_op jit(solution)/shard_map/all_gather | solution.py:323
  28.4 10.7 %collective-permute-start.3 = (bf16[1024,256]{1,0:T(8,128)(2,1)}, bf16[1024,256]{1,0:T(8,128)(2,1)S(1)}, u32[]{:S(2)}, u32[]{:S(2)}) collective-permute-start(bf16[1024,256]{1,0:T(8,128)(2,1)} %refs_0_.1), channel_id=1, source_target_pairs={{0,1},{1,2},{2,3},{3,4},{4,5},{5,6},{6,7},{7,0},{8,15},{9,8},{10,9... | collective-permute-start | bytes 1572872 | tf_op jit(solution)/shard_map/ppermute | solution.py:306
  29.0 15.7 %collective-permute-start.4 = (bf16[1024,256]{1,0:T(8,128)(2,1)}, bf16[1024,256]{1,0:T(8,128)(2,1)S(1)}, u32[]{:S(2)}, u32[]{:S(2)}) collective-permute-start(bf16[1024,256]{1,0:T(8,128)(2,1)} %refs_1_.1), channel_id=1, source_target_pairs={{0,1},{1,2},{2,3},{3,4},{4,5},{5,6},{6,7},{7,0},{8,15},{9,8},{10,9... | collective-permute-start | bytes 1572872 | tf_op jit(solution)/shard_map/ppermute | solution.py:306
  39.1 15.3 %collective-permute-start.5 = (bf16[1024,256]{1,0:T(8,128)(2,1)S(1)}, bf16[1024,256]{1,0:T(8,128)(2,1)S(1)}, u32[]{:S(2)}, u32[]{:S(2)}) collective-permute-start(bf16[1024,256]{1,0:T(8,128)(2,1)S(1)} %collective-permute-done.3.refs_5_.refs_2_), channel_id=1, source_target_pairs={{0,1},{1,2},{2,3},{3,4},{4,5},{5,6},{6,7},{7,0},{8,15},{9,8},{10,9... | collective-permute-start | bytes 1572872 | tf_op jit(solution)/shard_map/ppermute | solution.py:306
  44.7 11.2 %collective-permute-start.6 = (bf16[1024,256]{1,0:T(8,128)(2,1)S(1)}, bf16[1024,256]{1,0:T(8,128)(2,1)S(1)}, u32[]{:S(2)}, u32[]{:S(2)}) collective-permute-start(bf16[1024,256]{1,0:T(8,128)(2,1)S(1)} %collective-permute-done.4.refs_6_.refs_3_), channel_id=1, source_target_pairs={{0,1},{1,2},{2,3},{3,4},{4,5},{5,6},{6,7},{7,0},{8,15},{9,8},{10,9... | collective-permute-start | bytes 1572872 | tf_op jit(solution)/shard_map/ppermute | solution.py:306
  46.7 13.9 %all-to-all-start.1 = ((f32[32,2,256]{2,1,0:T(2,128)}), f32[32,2,256]{2,1,0:T(2,128)S(1)}, u32[]{:S(2)}, u32[]{:S(2)}) async-start(f32[32,2,256]{2,1,0:T(2,128)} %broadcast_in_dim.24), calls=%async_computation.1 | async-start | bytes 131072 | tf_op jit(solution)/shard_map/all_to_all | solution.py:17
  54.3 28.9 %copy-start.5 = (bf16[1024,256]{1,0:T(8,128)(2,1)}, bf16[1024,256]{1,0:T(8,128)(2,1)S(1)}, u32[]{:S(2)}) copy-start(bf16[1024,256]{1,0:T(8,128)(2,1)S(1)} %collective-permute-done.5.refs_7_.refs_4_) | copy-start | bytes 1572868
  54.3 10.6 %collective-permute-start.7 = (bf16[1024,256]{1,0:T(8,128)(2,1)S(1)}, bf16[1024,256]{1,0:T(8,128)(2,1)}, u32[]{:S(2)}, u32[]{:S(2)}) collective-permute-start(bf16[1024,256]{1,0:T(8,128)(2,1)S(1)} %collective-permute-done.5.refs_7_.refs_4_), channel_id=1, source_target_pairs={{0,1},{1,2},{2,3},{3,4},{4,5},{5,6},{6,7},{7,0},{8,15},{9,8},{10,9... | collective-permute-start | bytes 1572872 | tf_op jit(solution)/shard_map/ppermute | solution.py:306
  55.9 27.3 %copy-start.8 = (bf16[1024,256]{1,0:T(8,128)(2,1)}, bf16[1024,256]{1,0:T(8,128)(2,1)S(1)}, u32[]{:S(2)}) copy-start(bf16[1024,256]{1,0:T(8,128)(2,1)S(1)} %collective-permute-done.6.refs_8_.refs_5_) | copy-start | bytes 1572868
  55.9 14.6 %collective-permute-start.8 = (bf16[1024,256]{1,0:T(8,128)(2,1)S(1)}, bf16[1024,256]{1,0:T(8,128)(2,1)}, u32[]{:S(2)}, u32[]{:S(2)}) collective-permute-start(bf16[1024,256]{1,0:T(8,128)(2,1)S(1)} %collective-permute-done.6.refs_8_.refs_5_), channel_id=1, source_target_pairs={{0,1},{1,2},{2,3},{3,4},{4,5},{5,6},{6,7},{7,0},{8,15},{9,8},{10,9... | collective-permute-start | bytes 1572872 | tf_op jit(solution)/shard_map/ppermute | solution.py:306
  64.9 33.1 %collective-permute-start.10 = (bf16[1024,256]{1,0:T(8,128)(2,1)}, bf16[1024,256]{1,0:T(8,128)(2,1)}, u32[]{:S(2)}, u32[]{:S(2)}) collective-permute-start(bf16[1024,256]{1,0:T(8,128)(2,1)} %collective-permute-done.7.refs_9_.refs_6_), channel_id=1, source_target_pairs={{0,1},{1,2},{2,3},{3,4},{4,5},{5,6},{6,7},{7,0},{8,15},{9,8},{10,9... | collective-permute-start | bytes 1572872 | tf_op jit(solution)/shard_map/ppermute | solution.py:306
  70.6 27.5 %collective-permute-start.11 = (bf16[1024,256]{1,0:T(8,128)(2,1)}, bf16[1024,256]{1,0:T(8,128)(2,1)}, u32[]{:S(2)}, u32[]{:S(2)}) collective-permute-start(bf16[1024,256]{1,0:T(8,128)(2,1)} %collective-permute-done.8.refs_10_.refs_7_), channel_id=1, source_target_pairs={{0,1},{1,2},{2,3},{3,4},{4,5},{5,6},{6,7},{7,0},{8,15},{9,8},{10,9... | collective-permute-start | bytes 1572872 | tf_op jit(solution)/shard_map/ppermute | solution.py:306
  70.6 12.7 %collective-permute-start.1 = (bf16[6,256]{1,0:T(8,128)(2,1)S(1)}, bf16[6,256]{1,0:T(8,128)(2,1)S(1)}, u32[]{:S(2)}, u32[]{:S(2)}) collective-permute-start(bf16[6,256]{1,0:T(8,128)(2,1)S(1)} %get-tuple-element.19), channel_id=1, source_target_pairs={{0,2},{1,3},{2,4},{3,5},{4,6},{5,7},{6,0},{7,1},{8,14},{9,15},{10,... | collective-permute-start | bytes 9224 | tf_op jit(solution)/shard_map/ppermute | solution.py:306
  73.2 11.4 %collective-permute-start = (bf16[6,256]{1,0:T(8,128)(2,1)S(1)}, bf16[6,256]{1,0:T(8,128)(2,1)S(1)}, u32[]{:S(2)}, u32[]{:S(2)}) collective-permute-start(bf16[6,256]{1,0:T(8,128)(2,1)S(1)} %get-tuple-element.19), channel_id=1, source_target_pairs={{0,1},{1,2},{2,3},{3,4},{4,5},{5,6},{6,7},{7,0},{8,15},{9,8},{10,9... | collective-permute-start | bytes 9224 | tf_op jit(solution)/shard_map/ppermute | solution.py:306
  83.2 4.8 %collective-permute-start.2 = (bf16[6,256]{1,0:T(8,128)(2,1)S(1)}, bf16[6,256]{1,0:T(8,128)(2,1)S(1)}, u32[]{:S(2)}, u32[]{:S(2)}) collective-permute-start(bf16[6,256]{1,0:T(8,128)(2,1)S(1)} %collective-permute-done.1), channel_id=1, source_target_pairs={{0,1},{1,2},{2,3},{3,4},{4,5},{5,6},{6,7},{7,0},{8,15},{9,8},{10,9... | collective-permute-start | bytes 9224 | tf_op jit(solution)/shard_map/ppermute | solution.py:306
  88.1 5.1 %collective-permute-start.9 = (bf16[6,256]{1,0:T(8,128)(2,1)S(1)}, bf16[6,256]{1,0:T(8,128)(2,1)S(1)}, u32[]{:S(2)}, u32[]{:S(2)}) collective-permute-start(bf16[6,256]{1,0:T(8,128)(2,1)S(1)} %collective-permute-done.2), channel_id=1, source_target_pairs={{0,1},{1,2},{2,3},{3,4},{4,5},{5,6},{6,7},{7,0},{8,15},{9,8},{10,9... | collective-permute-start | bytes 9224 | tf_op jit(solution)/shard_map/ppermute | solution.py:306
  118.9 22.6 %copy-start.16 = (bf16[8,8,8,256]{3,2,0,1:T(8,128)(2,1)S(1)}, bf16[8,8,8,256]{3,2,0,1:T(8,128)(2,1)}, u32[]{:S(2)}) copy-start(bf16[8,8,8,256]{3,2,0,1:T(8,128)(2,1)} %copy.62) | copy-start | bytes 786436
  120.3 21.2 %all-to-all-start.3 = ((bf16[32,8,2048]{2,1,0:T(8,128)(2,1)}), bf16[32,8,2048]{2,1,0:T(8,128)(2,1)S(1)}, u32[]{:S(2)}, u32[]{:S(2)}) async-start(bf16[32,8,2048]{2,1,0:T(8,128)(2,1)} %gathered_sum.1), calls=%async_computation.3 | async-start | bytes 2097152 | tf_op jit(solution)/shard_map/all_to_all | solution.py:21
  125.5 20.6 %collective-permute-start.15 = (bf16[1024,256]{1,0:T(8,128)(2,1)}, bf16[1024,256]{1,0:T(8,128)(2,1)}, u32[]{:S(2)}, u32[]{:S(2)}) collective-permute-start(bf16[1024,256]{1,0:T(8,128)(2,1)} %collective-permute-done.10.refs_3_.refs_8_), channel_id=1, source_target_pairs={{0,1},{1,2},{2,3},{3,4},{4,5},{5,6},{6,7},{7,0},{8,15},{9,8},{10,9... | collective-permute-start | bytes 1572872 | tf_op jit(solution)/shard_map/ppermute | solution.py:306
  125.6 22.6 %collective-permute-start.16 = (bf16[1024,256]{1,0:T(8,128)(2,1)}, bf16[1024,256]{1,0:T(8,128)(2,1)}, u32[]{:S(2)}, u32[]{:S(2)}) collective-permute-start(bf16[1024,256]{1,0:T(8,128)(2,1)} %collective-permute-done.11.refs_4_.refs_9_), channel_id=1, source_target_pairs={{0,1},{1,2},{2,3},{3,4},{4,5},{5,6},{6,7},{7,0},{8,15},{9,8},{10,9... | collective-permute-start | bytes 1572872 | tf_op jit(solution)/shard_map/ppermute | solution.py:306
  142.7 15.9 %all-to-all-start.4 = ((bf16[8,256,64]{1,2,0:T(8,128)(2,1)}), bf16[8,256,64]{1,2,0:T(8,128)(2,1)S(1)}, u32[]{:S(2)}, u32[]{:S(2)}) async-start(bf16[8,256,64]{1,2,0:T(8,128)(2,1)} %broadcast_in_dim.25), calls=%async_computation.4 | async-start | bytes 524288 | tf_op jit(solution)/shard_map/all_to_all | solution.py:17
  146.2 48.8 %collective-permute-start.17 = (bf16[1024,256]{1,0:T(8,128)(2,1)}, bf16[1024,256]{1,0:T(8,128)(2,1)}, u32[]{:S(2)}, u32[]{:S(2)}) collective-permute-start(bf16[1024,256]{1,0:T(8,128)(2,1)} %collective-permute-done.15.refs_10_), channel_id=1, source_target_pairs={{0,1},{1,2},{2,3},{3,4},{4,5},{5,6},{6,7},{7,0},{8,15},{9,8},{10,9... | collective-permute-start | bytes 1572872 | tf_op jit(solution)/shard_map/ppermute | solution.py:306
  148.2 48.1 %collective-permute-start.18 = (bf16[1024,256]{1,0:T(8,128)(2,1)}, bf16[1024,256]{1,0:T(8,128)(2,1)}, u32[]{:S(2)}, u32[]{:S(2)}) collective-permute-start(bf16[1024,256]{1,0:T(8,128)(2,1)} %collective-permute-done.16.refs_11_), channel_id=1, source_target_pairs={{0,1},{1,2},{2,3},{3,4},{4,5},{5,6},{6,7},{7,0},{8,15},{9,8},{10,9... | collective-permute-start | bytes 1572872 | tf_op jit(solution)/shard_map/ppermute | solution.py:306
  168.0 12.6 %all-to-all-start.5 = ((bf16[32,2,2048]{2,1,0:T(2,128)(2,1)}), bf16[32,2,2048]{2,1,0:T(2,128)(2,1)S(1)}, u32[]{:S(2)}, u32[]{:S(2)}) async-start(bf16[32,2,2048]{2,1,0:T(2,128)(2,1)} %reshape.114), calls=%async_computation.5 | async-start | bytes 524288 | tf_op jit(solution)/shard_map/all_to_all | solution.py:21
  189.9 42.6 %all-to-all-start.6 = ((bf16[32,64,256]{2,1,0:T(8,128)(2,1)}), bf16[32,64,256]{2,1,0:T(8,128)(2,1)S(1)}, u32[]{:S(2)}, u32[]{:S(2)}) async-start(bf16[32,64,256]{2,1,0:T(8,128)(2,1)} %undone_copies.1), calls=%async_computation.6 | async-start | bytes 2097152 | tf_op jit(solution)/shard_map/all_to_all | solution.py:21
  195.0 26.1 %collective-permute-start.19 = (bf16[1024,256]{1,0:T(8,128)(2,1)}, bf16[1024,256]{1,0:T(8,128)(2,1)}, u32[]{:S(2)}, u32[]{:S(2)}) collective-permute-start(bf16[1024,256]{1,0:T(8,128)(2,1)} %collective-permute-done.17.refs_12_), channel_id=1, source_target_pairs={{0,1},{1,2},{2,3},{3,4},{4,5},{5,6},{6,7},{7,0},{8,15},{9,8},{10,9... | collective-permute-start | bytes 1572872 | tf_op jit(solution)/shard_map/ppermute | solution.py:306
  196.3 24.8 %collective-permute-start.20 = (bf16[1024,256]{1,0:T(8,128)(2,1)}, bf16[1024,256]{1,0:T(8,128)(2,1)}, u32[]{:S(2)}, u32[]{:S(2)}) collective-permute-start(bf16[1024,256]{1,0:T(8,128)(2,1)} %collective-permute-done.18.refs_13_), channel_id=1, source_target_pairs={{0,1},{1,2},{2,3},{3,4},{4,5},{5,6},{6,7},{7,0},{8,15},{9,8},{10,9... | collective-permute-start | bytes 1572872 | tf_op jit(solution)/shard_map/ppermute | solution.py:306
  196.4 15.0 %collective-permute-start.12 = (bf16[6,256]{1,0:T(8,128)(2,1)S(1)}, bf16[6,256]{1,0:T(8,128)(2,1)S(1)}, u32[]{:S(2)}, u32[]{:S(2)}) collective-permute-start(bf16[6,256]{1,0:T(8,128)(2,1)S(1)} %collective-permute-done.9), channel_id=1, source_target_pairs={{0,1},{1,2},{2,3},{3,4},{4,5},{5,6},{6,7},{7,0},{8,15},{9,8},{10,9... | collective-permute-start | bytes 9224 | tf_op jit(solution)/shard_map/ppermute | solution.py:306
  211.4 4.8 %collective-permute-start.13 = (bf16[6,256]{1,0:T(8,128)(2,1)S(1)}, bf16[6,256]{1,0:T(8,128)(2,1)S(1)}, u32[]{:S(2)}, u32[]{:S(2)}) collective-permute-start(bf16[6,256]{1,0:T(8,128)(2,1)S(1)} %collective-permute-done.12), channel_id=1, source_target_pairs={{0,1},{1,2},{2,3},{3,4},{4,5},{5,6},{6,7},{7,0},{8,15},{9,8},{10,9... | collective-permute-start | bytes 9224 | tf_op jit(solution)/shard_map/ppermute | solution.py:306
  216.2 4.8 %collective-permute-start.14 = (bf16[6,256]{1,0:T(8,128)(2,1)S(1)}, bf16[6,256]{1,0:T(8,128)(2,1)S(1)}, u32[]{:S(2)}, u32[]{:S(2)}) collective-permute-start(bf16[6,256]{1,0:T(8,128)(2,1)S(1)} %collective-permute-done.13), channel_id=1, source_target_pairs={{0,1},{1,2},{2,3},{3,4},{4,5},{5,6},{6,7},{7,0},{8,15},{9,8},{10,9... | collective-permute-start | bytes 9224 | tf_op jit(solution)/shard_map/ppermute | solution.py:306
  (13 other events, 25.4 us)
Sparse Core Ops, SparseCore 0:
  28.5 54.0 all-gather.1

commit v4 on v3

v4 whole, which is shorter than its diff:
```python
import jax
import jax.numpy as jnp
from jax import lax
from jax.experimental import pallas as pl
from jax.experimental.pallas import tpu as pltpu
from jax.sharding import PartitionSpec as P


F32 = jnp.float32
BF16 = jnp.bfloat16
VMEM = pl.BlockSpec(memory_space=pltpu.VMEM)
LIMIT = 60 * 1024 * 1024


def copy_for_each(shard, axis):
    copies = jnp.broadcast_to(shard, (lax.axis_size(axis), *shard.shape))
    return lax.all_to_all(copies, axis, split_axis=0, concat_axis=0, tiled=True)


def exchange(parts, axis):
    return lax.all_to_all(parts, axis, split_axis=0, concat_axis=0, tiled=True)


def contract_last(a, b):
    return lax.dot_general(a, b, (((1,), (1,)), ((), ())), preferred_element_type=F32)


def product(a, b):
    return jnp.dot(a, b, preferred_element_type=F32)


def three_parts(x):
    a = lax.reduce_precision(x, 8, 7)
    b = lax.reduce_precision(x - a, 8, 7)
    c = x - a - b
    return [part.astype(BF16) for part in (a, b, c)]


def divided(lam_row, lam_col, first_row):
    on_diag = (
        (first_row + jnp.arange(lam_row.shape[0], dtype=jnp.int32))[:, None]
        == jnp.arange(lam_col.shape[0], dtype=jnp.int32)[None, :]
    )
    root_row = lam_row ** (-0.5)
    root_col = lam_col ** (-0.5)
    gaps_lam = lam_row[:, None] - lam_col[None, :]
    safe_gap = jnp.where(on_diag, jnp.ones_like(gaps_lam), gaps_lam)
    off_diag = (root_row[:, None] - root_col[None, :]) / safe_gap
    diag_vals = -0.5 * lam_row[:, None] ** (-1.5) + jnp.zeros_like(gaps_lam)
    return jnp.where(on_diag, diag_vals, off_diag)


def cost(flops, nbytes):
    return pl.CostEstimate(flops=flops, bytes_accessed=nbytes, transcendentals=0)


def params():
    return pltpu.CompilerParams(vmem_limit_bytes=LIMIT)


def gram_body(hops, half, own_ref, *refs):
    out_ref = refs[-1]
    width, n = own_ref.shape[0], own_ref.shape[1] // 2
    xt, gt = own_ref[:, :n], own_ref[:, n:]
    sum_x = jnp.sum(xt.astype(F32), axis=1, keepdims=True)
    sum_g = jnp.sum(gt.astype(F32), axis=1, keepdims=True)
    for i, h in enumerate(hops):
        grads, inputs = refs[2 * i][...], refs[2 * i + 1][...]
        value = product(xt, grads)
        value -= sum_x * (jnp.sum(grads.astype(F32), axis=0, keepdims=True) * (1.0 / n))
        if h > 0:
            value += product(gt, inputs)
            value -= sum_g * (jnp.sum(inputs.astype(F32), axis=0, keepdims=True) * (1.0 / n))
        if h == half:
            value = 0.5 * value
        out_ref[:, i * width : (i + 1) * width] = value.astype(BF16)


def gram_first(own, blocks, half):
    width, n = own.shape[0], own.shape[1] // 2
    flat = [b for pair in blocks for b in pair]
    return pl.pallas_call(
        lambda *refs: gram_body(range(half), half, *refs),
        out_shape=jax.ShapeDtypeStruct((width, (half + 1) * width), BF16),
        grid=(1,),
        in_specs=[VMEM] * (1 + len(flat)),
        out_specs=pl.BlockSpec((width, half * width), lambda i: (0, 0)),
        compiler_params=params(),
        cost_estimate=cost(4 * half * n * width * width, 2 * n * width * 2 * (half + 1)),
        name="gram_first",
    )(own, *flat)


def gram_last(partial, own, block, half):
    width, n = own.shape[0], own.shape[1] // 2

    def body(partial_ref, *refs):
        gram_body((half,), half, *refs)

    return pl.pallas_call(
        body,
        out_shape=jax.ShapeDtypeStruct(partial.shape, BF16),
        grid=(1,),
        in_specs=[pl.BlockSpec(memory_space=pl.ANY)] + [VMEM] * 3,
        out_specs=pl.BlockSpec((width, width), lambda i: (0, half)),
        input_output_aliases={0: 0},
        compiler_params=params(),
        cost_estimate=cost(4 * n * width * width, 8 * n * width),
        name="gram_last",
    )(partial, own, *block)


def gathered_sum(got, width, half):
    groups, few, _ = got.shape

    def body(got_ref, out_ref):
        def add(i, sums):
            return sums[0] + got_ref[2 * i].astype(F32), sums[1] + got_ref[2 * i + 1].astype(F32)

        zero = jnp.zeros(got_ref.shape[1:], F32)
        down, up = lax.fori_loop(0, groups // 2, add, (zero, zero))
        piece = lambda a, h: a[:, h * width : (h + 1) * width]
        pair = [piece(down, 0) + piece(up, 0)]
        pair += [piece(up, h) for h in range(1, half)]
        pair += [piece(down, half) + piece(up, half)]
        pair += [piece(down, h) for h in range(half - 1, 0, -1)]
        value = jnp.concatenate(pair, axis=1).astype(BF16)

        def store(i, carry):
            out_ref[i] = value
            return carry

        lax.fori_loop(0, groups, store, 0)

    return pl.pallas_call(
        body,
        out_shape=jax.ShapeDtypeStruct((groups, few, 2 * half * width), BF16),
        in_specs=[VMEM],
        out_specs=VMEM,
        compiler_params=params(),
        cost_estimate=cost(2 * got.size, 4 * got.size),
        name="gathered_sum",
    )(got)


def rotated_cols(basis_t, shared, spread):
    dim, narrow = basis_t.shape[0], spread.shape[0]
    planes, _, width = shared.shape
    rows = 256
    each = rows // narrow

    def body(basis_ref, shared_ref, spread_ref, out_ref, low_ref, right_ref):
        @pl.when(pl.program_id(0) == 0)
        def _():
            for p in range(planes):
                right_ref[:, p * width : (p + 1) * width] = shared_ref[p, :narrow, :]

        value = contract_last(basis_ref[...], right_ref[...])
        out_ref[...] = value
        for k in range(each):
            piece = value[k * narrow : (k + 1) * narrow].astype(BF16)
            low_ref[k] = jnp.concatenate([piece, spread_ref[...]], axis=1)

    return pl.pallas_call(
        body,
        out_shape=[
            jax.ShapeDtypeStruct((dim, narrow), F32),
            jax.ShapeDtypeStruct((dim // narrow, narrow, 2 * narrow), BF16),
        ],
        grid=(dim // rows,),
        in_specs=[
            pl.BlockSpec((rows, dim), lambda i: (i, 0)),
            pl.BlockSpec(shared.shape, lambda i: (0, 0, 0)),
            pl.BlockSpec(spread.shape, lambda i: (0, 0)),
        ],
        out_specs=[
            pl.BlockSpec((rows, narrow), lambda i: (i, 0)),
            pl.BlockSpec((each, narrow, 2 * narrow), lambda i: (i, 0, 0)),
        ],
        scratch_shapes=[pltpu.VMEM((narrow, dim), BF16)],
        compiler_params=params(),
        cost_estimate=cost(2 * dim * dim * narrow, 2 * dim * dim),
        name="rotated_cols",
    )(basis_t, shared, spread)


def undone_copies(rot, back, spread, kernel_t, basis_t, plane, n, width):
    dim, narrow = rot.shape
    groups = back.shape[0]

    def body(plane_ref, rot_ref, back_ref, spread_ref, kernel_ref, basis_ref, out_ref):
        halfway = narrow // 2
        crossed = jnp.concatenate([spread_ref[halfway:, :], spread_ref[:halfway, :]], axis=0)
        crossed = crossed.T.astype(BF16)
        total = jnp.zeros(out_ref.shape[1:], F32)
        for p in range(groups // 2):
            at = slice(2 * p * narrow, 2 * (p + 1) * narrow)
            two = (back_ref[2 * p], back_ref[2 * p + 1])
            mirrored = jnp.concatenate([t[:, :narrow] for t in two], axis=1)
            theirs = jnp.concatenate([t[:, narrow:] for t in two], axis=1)
            scaled = rot_ref[at, :].T + mirrored.astype(F32) + n * product(crossed, theirs)
            scaled = scaled * kernel_ref[:, at]
            high = scaled.astype(BF16)
            low = (scaled - high.astype(F32)).astype(BF16)
            basis = basis_ref[at, :]
            total += product(high, basis) + product(low, basis)
        value = total.astype(BF16)

        def store(i, carry):
            out_ref[i] = value
            return carry

        lax.fori_loop(0, groups, store, 0)

    full = lambda shape: pl.BlockSpec(shape, lambda i, plane_ref: (0,) * len(shape))
    return pl.pallas_call(
        body,
        out_shape=jax.ShapeDtypeStruct((groups, narrow, width), BF16),
        grid_spec=pltpu.PrefetchScalarGridSpec(
            num_scalar_prefetch=1,
            grid=(1,),
            in_specs=[
                full(rot.shape),
                full(back.shape),
                full(spread.shape),
                full(kernel_t.shape),
                pl.BlockSpec((dim, width), lambda i, plane_ref: (0, plane_ref[0])),
            ],
            out_specs=full((groups, narrow, width)),
        ),
        compiler_params=params(),
        cost_estimate=cost(4 * dim * narrow * width, 4 * dim * width),
        name="undone_copies",
    )(plane, rot, back, spread, kernel_t, basis_t)


def first_product(places, told, whiten, blocks):
    n, width = blocks[0][0].shape
    dim = whiten.shape[0]
    planes = len(blocks)
    rows = 256

    def body(place_ref, told_ref, whiten_ref, *refs):
        centered_ref, out_ref = refs[-2:]
        total = jnp.zeros((rows, width), F32)
        for h in range(planes):
            at = pl.ds(pl.multiple_of(place_ref[h] * width, width), width)
            mean_x = told_ref[pl.ds(2 * place_ref[h], 1), :]
            mean_g = told_ref[pl.ds(2 * place_ref[h] + 1, 1), :]
            shifted = (refs[2 * h][...].astype(F32) - mean_g).astype(BF16)
            total += product(shifted, whiten_ref[at, :])
            centered_ref[:, at] = (refs[2 * h + 1][...].astype(F32) - mean_x).astype(BF16)
        out_ref[...] = total

    full = lambda shape: pl.BlockSpec(shape, lambda i, place_ref: (0,) * len(shape))
    part = lambda cols: pl.BlockSpec((rows, cols), lambda i, place_ref: (i, 0))
    flat = [b for pair in blocks for b in pair]
    return pl.pallas_call(
        body,
        out_shape=[
            jax.ShapeDtypeStruct((n, dim), BF16),
            jax.ShapeDtypeStruct((n, width), F32),
        ],
        grid_spec=pltpu.PrefetchScalarGridSpec(
            num_scalar_prefetch=1,
            grid=(n // rows,),
            in_specs=[full(told.shape), full(whiten.shape)] + [part(width)] * len(flat),
            out_specs=[part(dim), part(width)],
        ),
        compiler_params=params(),
        cost_estimate=cost(2 * n * dim * width, 6 * n * dim),
        name="first_product",
    )(places, told, whiten, *flat)


def local(features, grad_out, eigvecs, eigvals, whiten):
    n, width = features.shape
    groups, planes = lax.axis_size("rows"), lax.axis_size("feat")
    total = n * groups
    dim = width * planes
    narrow = eigvecs.shape[1]
    half = planes // 2
    r, f = lax.axis_index("rows"), lax.axis_index("feat")
    way = jnp.where(r % 2 == 0, -1, 1)

    def pass_on(value, hops=1):
        pairs = [
            (a * planes + b, a * planes + (b + (hops if a % 2 == 0 else -hops)) % planes)
            for a in range(groups)
            for b in range(planes)
        ]
        return lax.ppermute(value, ("rows", "feat"), pairs)

    blocks = [(grad_out, features)]
    for _ in range(1, planes):
        blocks.append(tuple(pass_on(b) for b in blocks[-1]))

    sums = jnp.stack([jnp.sum(a, axis=0, dtype=F32) for a in (features, grad_out)])
    all_sums = copy_for_each(sums, "rows")
    means = jnp.sum(all_sums, axis=0) / total
    apart = jnp.swapaxes(all_sums * (1.0 / n) - means, 0, 1).reshape(2 * groups, width)
    spread = jnp.dot(apart, eigvecs, precision=lax.Precision.HIGHEST).astype(BF16)
    few = spread.size // width
    fold = spread.shape[0] // few
    spread = jnp.concatenate([spread[k * few : (k + 1) * few] for k in range(fold)], axis=1)

    basis_rt = copy_for_each(eigvecs.astype(BF16).T, "feat")
    basis_rt = jnp.swapaxes(basis_rt, 0, 1).reshape(narrow, dim)
    basis_t = lax.all_gather(basis_rt, "rows", axis=0, tiled=True)

    own = jnp.concatenate([features.T, grad_out.T], axis=1)
    mixed = gram_first(own, blocks[:half], half)
    mixed = gram_last(mixed, own, blocks[half], half)

    got = exchange(mixed.reshape(groups, width // groups, -1), "rows")
    copies = gathered_sum(got, width, half)
    gram = exchange(copies, "rows").reshape(width, dim)

    twice = jnp.concatenate([basis_rt, basis_rt], axis=1)
    turned = lax.dynamic_slice_in_dim(twice, f * width, dim, axis=1)
    right = contract_last(turned, gram).astype(BF16)
    shared = copy_for_each(jnp.concatenate([right, spread, *three_parts(means)]), "feat")
    spread = jnp.sum(shared[:, narrow : narrow + few].astype(F32), axis=0)
    spread = jnp.concatenate(
        [spread[:, k * narrow : (k + 1) * narrow] for k in range(fold)], axis=0
    )
    rot, low = rotated_cols(basis_t, shared, spread.astype(BF16))
    back = exchange(low, "rows")
    first = r * narrow
    kernel_t = divided(lax.dynamic_slice_in_dim(eigvals, first, narrow), eigvals, first)

    copies = undone_copies(rot, back, spread, kernel_t, basis_t, f[None], float(n), width)
    undone = exchange(copies, "rows").reshape(dim, width)

    places = ((f + way * jnp.arange(planes, dtype=jnp.int32)) % planes).astype(jnp.int32)
    told = shared[:, narrow + few :].astype(F32).reshape(planes, 3, 2, width)
    told = jnp.sum(told, axis=1).reshape(2 * planes, width)
    centered, running = first_product(places, told, whiten, blocks)
    turned = lax.optimization_barrier(contract_last(centered, basis_t).astype(BF16))
    return (running + product(turned, undone) * (1.0 / total)).astype(BF16)


def solution(mesh):
    in_specs = (P("rows", "feat"), P("rows", "feat"), P("feat", "rows"), P(), P(None, "feat"))
    out_specs = P("rows", "feat")
    return jax.shard_map(local, mesh=mesh, in_specs=in_specs, out_specs=out_specs, check_vma=False)
```

time: 255 us -> 230 us (0.902)
  the two profiles are of different devices: /device:TPU:2 before, /device:TPU:1 now
where the time goes in v4:
time: 230 us; the launch traced here: 229 us
  waiting for transfers between devices  74.9 us (33%)
  starting transfers between devices  54.1 us (24%)
  Pallas kernels  30.8 us (13%)
  blocking collectives  19.3 us (8%)
  matrix products  18 us (8%)
  between operations  13.7 us (6%)
  other arithmetic  10.4 us (5%)
  local copies, waits for them, and re-layouts  7.66 us (3%)
    ppermute x14, waiting for transfers between devices, pass_on(): return lax.ppermute(value, ('rows', 'feat'), pairs)  45 us
    all_to_all x4, waiting for transfers between devices, exchange(): return lax.all_to_all(parts, axis, split_axis=0, concat_axis=0, tiled=True)  29.9 us
    all_to_all x4, starting transfers between devices, exchange(): return lax.all_to_all(parts, axis, split_axis=0, concat_axis=0, tiled=True)  22.7 us
    all_to_all x1, blocking collectives, copy_for_each(): return lax.all_to_all(copies, axis, split_axis=0, concat_axis=0, tiled=True)  19.3 us
    ppermute x14, starting transfers between devices, pass_on(): return lax.ppermute(value, ('rows', 'feat'), pairs)  16.5 us
    all_to_all x2, starting transfers between devices, copy_for_each(): return lax.all_to_all(copies, axis, split_axis=0, concat_axis=0, tiled=True)  14.9 us
    dot_general x2, matrix products, contract_last(): lax.dot_general(a, b, (((1,), (1,)), ((), ())), preferred_element_type=F32)  14.3 us
    pallas_call x1, Pallas kernels, rotated_cols(): pl.pallas_call(body, out_shape=[jax.ShapeDtypeStruct((dim, narrow), F32),...  8.46 us
  transfers between devices with their start and end apart: 21, of which 12 were waited for; matrix products, arithmetic and copies ran while one was open for 12% of the time, Pallas kernels for 11%

profile of v4, /device:TPU:1, one launch (start us, length us, event | category | flops | bytes accessed | tf_op | source)
XLA Modules:
  0.0 228.9 jit_solution(6769877363232051257)
XLA Ops:
  7.5 19.3 %all_to_all.35 = bf16[8,64,256]{2,1,0:T(8,128)(2,1)S(1)} all-to-all(bf16[8,64,256]{2,1,0:T(8,128)(2,1)S(1)} %broadcast_in_dim.10), channel_id=1, replica_groups=mesh['rows'=32,'feat'=8] {'feat'}, dimensions={0} | all-to-all | bytes 524288 | tf_op jit(solution)/shard_map/all_to_all | solution.py:17
  27.6 1.6 collective-permute-start.1
  29.2 6.9 %collective-permute-done.refs_3_.refs_2_ = bf16[1024,256]{1,0:T(8,128)(2,1)S(1)} collective-permute-done((bf16[1024,256]{1,0:T(8,128)(2,1)}, bf16[1024,256]{1,0:T(8,128)(2,1)S(1)}, u32[]{:S(2)}, u32[]{:S(2)}) %collective-permute-start) | collective-permute-done | bytes 524320 | tf_op jit(solution)/shard_map/ppermute | solution.py:292
  37.0 4.8 %collective-permute-done.1.refs_4_.refs_3_ = bf16[1024,256]{1,0:T(8,128)(2,1)S(1)} collective-permute-done((bf16[1024,256]{1,0:T(8,128)(2,1)}, bf16[1024,256]{1,0:T(8,128)(2,1)S(1)}, u32[]{:S(2)}, u32[]{:S(2)}) %collective-permute-start.1) | collective-permute-done | bytes 524320 | tf_op jit(solution)/shard_map/ppermute | solution.py:292
  42.7 4.8 %collective-permute-done.2.refs_5_.refs_4_ = bf16[1024,256]{1,0:T(8,128)(2,1)S(1)} collective-permute-done((bf16[1024,256]{1,0:T(8,128)(2,1)S(1)}, bf16[1024,256]{1,0:T(8,128)(2,1)S(1)}, u32[]{:S(2)}, u32[]{:S(2)}) %collective-permute-start.2) | collective-permute-done | bytes 524320 | tf_op jit(solution)/shard_map/ppermute | solution.py:292
  48.3 4.7 %collective-permute-done.3.refs_6_.refs_5_ = bf16[1024,256]{1,0:T(8,128)(2,1)S(1)} collective-permute-done((bf16[1024,256]{1,0:T(8,128)(2,1)S(1)}, bf16[1024,256]{1,0:T(8,128)(2,1)S(1)}, u32[]{:S(2)}, u32[]{:S(2)}) %collective-permute-start.3) | collective-permute-done | bytes 524320 | tf_op jit(solution)/shard_map/ppermute | solution.py:292
  53.0 1.3 collective-permute-start.5
  55.5 3.1 %collective-permute-done.4.refs_7_.refs_6_ = bf16[1024,256]{1,0:T(8,128)(2,1)S(1)} collective-permute-done((bf16[1024,256]{1,0:T(8,128)(2,1)S(1)}, bf16[1024,256]{1,0:T(8,128)(2,1)S(1)}, u32[]{:S(2)}, u32[]{:S(2)}) %collective-permute-start.4) | collective-permute-done | bytes 524320 | tf_op jit(solution)/shard_map/ppermute | solution.py:292
  59.5 4.8 %collective-permute-done.5.refs_8_.refs_7_ = bf16[1024,256]{1,0:T(8,128)(2,1)} collective-permute-done((bf16[1024,256]{1,0:T(8,128)(2,1)S(1)}, bf16[1024,256]{1,0:T(8,128)(2,1)}, u32[]{:S(2)}, u32[]{:S(2)}) %collective-permute-start.5) | collective-permute-done | bytes 524320 | tf_op jit(solution)/shard_map/ppermute | solution.py:292
  67.1 10.6 %all-to-all-start.3 = ((f32[32,2,256]{2,1,0:T(2,128)}), f32[32,2,256]{2,1,0:T(2,128)S(1)}, u32[]{:S(2)}, u32[]{:S(2)}) async-start(f32[32,2,256]{2,1,0:T(2,128)} %broadcast_in_dim.11), calls=%async_computation.3 | async-start | bytes 131072 | tf_op jit(solution)/shard_map/all_to_all | solution.py:17
  77.7 2.1 copy.20
  80.7 2.3 %pad_maximum_fusion.refs_0_ = bf16[256,2048]{1,0:T(8,128)(2,1)} fusion(bf16[256,1024]{1,0:T(8,128)(2,1)} %bitcast.26, bf16[256,1024]{1,0:T(8,128)(2,1)} %bitcast.27), kind=kLoop, calls=%fused_computation.4 | loop fusion | flops 2097152 | bytes 2097152 | tf_op jit(solution)/shard_map/concatenate | solution.py:311
  83.1 4.5 %gram_first.1.partial_ref = bf16[256,1280]{1,0:T(8,128)(2,1)} custom-call(bf16[256,2048]{1,0:T(8,128)(2,1)} %pad_maximum_fusion.refs_0_, bf16[1024,256]{1,0:T(8,128)(2,1)} %refs_0_.1, bf16[1024,256]{1,0:T(8,128)(2,1)} %refs_1_.3, bf16[1024,256]{1,0:T(8,128)(2,1)} %copy-done.2, bf16[1024,256]{1,0:T(8,128)(2,1)} %copy-done.3, bf16[1024,256]{1,0:T(8,128)(2,1)} %copy-done.4, ...), custom_call_target="tpu_custom_call" | custom-call | flops 1073741824 | bytes 5242880 | tf_op jit(solution)/shard_map/gram_first/pallas_call | solution.py:82
  87.6 2.7 %gram_last.1 = bf16[256,1280]{1,0:T(8,128)(2,1)} custom-call(bf16[256,1280]{1,0:T(8,128)(2,1)} %gram_first.1.partial_ref, bf16[256,2048]{1,0:T(8,128)(2,1)} %pad_maximum_fusion.refs_0_, bf16[1024,256]{1,0:T(8,128)(2,1)} %collective-permute-done.6.refs_1_.refs_8_, bf16[1024,256]{1,0:T(8,128)(2,1)} %collective-permute-done.7.refs_2_.refs_9_), custom_call_target="tpu_custom_call", output_to_operand_aliasing={{}: (0, {})} | custom-call | flops 268435456 | bytes 2097152 | tf_op jit(solution)/shard_map/gram_last/pallas_call | solution.py:100
  90.3 7.4 %all-to-all-start.1 = ((bf16[32,8,1280]{2,1,0:T(8,128)(2,1)}), bf16[32,8,1280]{2,1,0:T(8,128)(2,1)S(1)}, u32[]{:S(2)}, u32[]{:S(2)}) async-start(bf16[32,8,1280]{2,1,0:T(8,128)(2,1)} %bitcast.25), calls=%async_computation.1 | async-start | bytes 1310720 | tf_op jit(solution)/shard_map/all_to_all | solution.py:21
  97.9 12.7 %all-to-all-done.1.got_ref = bf16[32,8,1280]{2,1,0:T(8,128)(2,1)S(1)} async-done(((bf16[32,8,1280]{2,1,0:T(8,128)(2,1)}), bf16[32,8,1280]{2,1,0:T(8,128)(2,1)S(1)}, u32[]{:S(2)}, u32[]{:S(2)}) %all-to-all-start.1) | async-done | bytes 655392 | tf_op jit(solution)/shard_map/all_to_all | solution.py:21
  111.4 2.5 %gathered_sum.1 = bf16[32,8,2048]{2,1,0:T(8,128)(2,1)} custom-call(bf16[32,8,1280]{2,1,0:T(8,128)(2,1)} %copy-done.1), custom_call_target="tpu_custom_call" | custom-call | flops 655360 | bytes 1310720 | tf_op jit(solution)/shard_map/gathered_sum/pallas_call | solution.py:135
  113.8 4.1 %all-to-all-start.2 = ((bf16[32,8,2048]{2,1,0:T(8,128)(2,1)}), bf16[32,8,2048]{2,1,0:T(8,128)(2,1)S(1)}, u32[]{:S(2)}, u32[]{:S(2)}) async-start(bf16[32,8,2048]{2,1,0:T(8,128)(2,1)} %gathered_sum.1), calls=%async_computation.2 | async-start | bytes 2097152 | tf_op jit(solution)/shard_map/all_to_all | solution.py:21
  118.2 3.1 %collective-permute-start.8 = (bf16[1024,256]{1,0:T(8,128)(2,1)}, bf16[1024,256]{1,0:T(8,128)(2,1)S(1)}, u32[]{:S(2)}, u32[]{:S(2)}) collective-permute-start(bf16[1024,256]{1,0:T(8,128)(2,1)} %collective-permute-done.6.refs_1_.refs_8_), channel_id=1, source_target_pairs={{0,1},{1,2},{2,3},{3,4},{4,5},{5,6},{6,7},{7,0},{8,15},{9,8},{10,9... | collective-permute-start | bytes 1572872 | tf_op jit(solution)/shard_map/ppermute | solution.py:292
  121.6 13.5 %all-to-all-done.2 = bf16[32,8,2048]{2,1,0:T(8,128)(2,1)S(1)} async-done(((bf16[32,8,2048]{2,1,0:T(8,128)(2,1)}), bf16[32,8,2048]{2,1,0:T(8,128)(2,1)S(1)}, u32[]{:S(2)}, u32[]{:S(2)}) %all-to-all-start.2) | async-done | bytes 1048608 | tf_op jit(solution)/shard_map/all_to_all | solution.py:21
  136.3 4.3 %all-to-all-start.4 = ((bf16[8,86,256]{2,1,0:T(8,128)(2,1)}), bf16[8,86,256]{2,1,0:T(8,128)(2,1)S(1)}, u32[]{:S(2)}, u32[]{:S(2)}) async-start(bf16[8,86,256]{2,1,0:T(8,128)(2,1)} %broadcast_in_dim.12), calls=%async_computation.4 | async-start | bytes 720896 | tf_op jit(solution)/shard_map/all_to_all | solution.py:17
  140.6 2.8 %collective-permute-start.10 = (bf16[1024,256]{1,0:T(8,128)(2,1)S(1)}, bf16[1024,256]{1,0:T(8,128)(2,1)S(1)}, u32[]{:S(2)}, u32[]{:S(2)}) collective-permute-start(bf16[1024,256]{1,0:T(8,128)(2,1)S(1)} %collective-permute-done.8.refs_10_), channel_id=1, source_target_pairs={{0,1},{1,2},{2,3},{3,4},{4,5},{5,6},{6,7},{7,0},{8,15},{9,8},{10,9... | collective-permute-start | bytes 1572872 | tf_op jit(solution)/shard_map/ppermute | solution.py:292
  145.6 11.2 %collective-permute-done.10.refs_12_ = bf16[1024,256]{1,0:T(8,128)(2,1)S(1)} collective-permute-done((bf16[1024,256]{1,0:T(8,128)(2,1)S(1)}, bf16[1024,256]{1,0:T(8,128)(2,1)S(1)}, u32[]{:S(2)}, u32[]{:S(2)}) %collective-permute-start.10) | collective-permute-done | bytes 524320 | tf_op jit(solution)/shard_map/ppermute | solution.py:292
  157.8 4.7 %collective-permute-done.11.refs_13_ = bf16[1024,256]{1,0:T(8,128)(2,1)S(1)} collective-permute-done((bf16[1024,256]{1,0:T(8,128)(2,1)S(1)}, bf16[1024,256]{1,0:T(8,128)(2,1)S(1)}, u32[]{:S(2)}, u32[]{:S(2)}) %collective-permute-start.11) | collective-permute-done | bytes 524320 | tf_op jit(solution)/shard_map/ppermute | solution.py:292
  164.1 8.5 %rotated_cols.1 = (f32[2048,64]{1,0:T(8,128)}, bf16[32,64,128]{2,1,0:T(8,128)(2,1)}) custom-call(bf16[2048,2048]{1,0:T(8,128)(2,1)} %all-gather.2.cloned.1.call-done.basis_ref, bf16[8,86,256]{2,1,0:T(8,128)(2,1)} %copy-done.8, bf16[64,64]{1,0:T(8,128)(2,1)} %fusion.8.spread_ref), custom_call_target="tpu_custom_call" | custom-call | flops 536870912 | bytes 8388608 | tf_op jit(solution)/shard_map/rotated_cols/pallas_call | solution.py:164
  172.6 4.5 %all-to-all-start.5 = ((bf16[32,64,128]{2,1,0:T(8,128)(2,1)}), bf16[32,64,128]{2,1,0:T(8,128)(2,1)S(1)}, u32[]{:S(2)}, u32[]{:S(2)}) async-start(bf16[32,64,128]{2,1,0:T(8,128)(2,1)} %get-tuple-element.12), calls=%async_computation.5 | async-start | bytes 1048576 | tf_op jit(solution)/shard_map/all_to_all | solution.py:21
  179.1 8.2 %first_product.1 = (bf16[1024,2048]{1,0:T(8,128)(2,1)}, f32[1024,256]{1,0:T(8,128)}) custom-call(s32[8]{0:T(128)} %and_select_fusion.place_ref, f32[16,256]{1,0:T(8,128)} %reshape.44.told_ref, bf16[2048,256]{1,0:T(8,128)(2,1)} %whiten_ref.1, bf16[1024,256]{1,0:T(8,128)(2,1)} %refs_0_.1, bf16[1024,256]{1,0:T(8,128)(2,1)} %refs_1_.3, ...), custom_call_target="tpu_custom_call" | custom-call | flops 1073741824 | bytes 12582912 | tf_op jit(solution)/shard_map/first_product/pallas_call | solution.py:258
  189.3 4.5 %undone_copies.1 = bf16[32,64,256]{2,1,0:T(8,128)(2,1)} custom-call(s32[1]{0:T(128)} %bitcast.11.plane_ref, f32[2048,64]{1,0:T(8,128)} %get-tuple-element.11.rot_ref, bf16[32,64,128]{2,1,0:T(8,128)(2,1)} %copy-done.7, f32[64,64]{1,0:T(8,128)} %pad_maximum_fusion.1.spread_ref, f32[64,2048]{1,0:T(8,128)} %divide_select_fusion.kernel_ref, ...), custom_call_target="tpu_custom_call" | custom-call | flops 134217728 | bytes 2097152 | tf_op jit(solution)/shard_map/undone_copies/pallas_call | solution.py:216
  193.8 6.8 %all-to-all-start.6 = ((bf16[32,64,256]{2,1,0:T(8,128)(2,1)}), bf16[32,64,256]{2,1,0:T(8,128)(2,1)S(1)}, u32[]{:S(2)}, u32[]{:S(2)}) async-start(bf16[32,64,256]{2,1,0:T(8,128)(2,1)} %undone_copies.1), calls=%async_computation.6 | async-start | bytes 2097152 | tf_op jit(solution)/shard_map/all_to_all | solution.py:21
  200.6 13.9 %convolution_convert_fusion = bf16[1024,2048]{1,0:T(8,128)(2,1)} fusion(bf16[1024,2048]{1,0:T(8,128)(2,1)} %get-tuple-element.10, bf16[2048,2048]{1,0:T(8,128)(2,1)} %all-gather.2.cloned.1.call-done.basis_ref), kind=kOutput, calls=%fused_computation | convolution fusion | flops 8592031744 | bytes 16777216 | tf_op jit(solution)/shard_map/dot_general | solution.py:25
  214.5 3.1 %all-to-all-done.6 = bf16[32,64,256]{2,1,0:T(8,128)(2,1)S(1)} async-done(((bf16[32,64,256]{2,1,0:T(8,128)(2,1)}), bf16[32,64,256]{2,1,0:T(8,128)(2,1)S(1)}, u32[]{:S(2)}, u32[]{:S(2)}) %all-to-all-start.6) | async-done | bytes 1048608 | tf_op jit(solution)/shard_map/all_to_all | solution.py:21
  217.6 3.4 %convolution_multiply_fusion = f32[1024,256]{1,0:T(8,128)S(1)} fusion(bf16[1024,2048]{1,0:T(8,128)(2,1)} %convolution_convert_fusion, bf16[2048,256]{1,0:T(8,128)(2,1)S(1)} %bitcast.28), kind=kOutput, calls=%fused_computation.1 | convolution fusion | flops 1074003968 | bytes 6291456 | tf_op jit(solution)/shard_map/dot_general | solution.py:29
  (89 shorter events, 22.8 us)
Async XLA Ops:
  6.5 73.2 %copy-start = (bf16[1024,256]{1,0:T(8,128)(2,1)S(1)}, bf16[1024,256]{1,0:T(8,128)(2,1)}, u32[]{:S(2)}) copy-start(bf16[1024,256]{1,0:T(8,128)(2,1)} %refs_1_.3) | copy-start | bytes 1572868
  6.5 157.6 %all-gather.2.cloned.1.call-start = ((), (), s32[]{:S(2)}) async-start(), calls=%async_computation.7 | async-start | bytes 8650752 | tf_op jit(solution)/shard_map/all_gather | solution.py:309
  27.5 8.6 %collective-permute-start = (bf16[1024,256]{1,0:T(8,128)(2,1)}, bf16[1024,256]{1,0:T(8,128)(2,1)S(1)}, u32[]{:S(2)}, u32[]{:S(2)}) collective-permute-start(bf16[1024,256]{1,0:T(8,128)(2,1)} %refs_0_.1), channel_id=1, source_target_pairs={{0,1},{1,2},{2,3},{3,4},{4,5},{5,6},{6,7},{7,0},{8,15},{9,8},{10,9... | collective-permute-start | bytes 1572872 | tf_op jit(solution)/shard_map/ppermute | solution.py:292
  27.6 14.2 %collective-permute-start.1 = (bf16[1024,256]{1,0:T(8,128)(2,1)}, bf16[1024,256]{1,0:T(8,128)(2,1)S(1)}, u32[]{:S(2)}, u32[]{:S(2)}) collective-permute-start(bf16[1024,256]{1,0:T(8,128)(2,1)} %refs_1_.3), channel_id=1, source_target_pairs={{0,1},{1,2},{2,3},{3,4},{4,5},{5,6},{6,7},{7,0},{8,15},{9,8},{10,9... | collective-permute-start | bytes 1572872 | tf_op jit(solution)/shard_map/ppermute | solution.py:292
  36.1 46.9 %copy-start.2 = (bf16[1024,256]{1,0:T(8,128)(2,1)}, bf16[1024,256]{1,0:T(8,128)(2,1)S(1)}, u32[]{:S(2)}) copy-start(bf16[1024,256]{1,0:T(8,128)(2,1)S(1)} %collective-permute-done.refs_3_.refs_2_) | copy-start | bytes 1572868
  36.1 11.3 %collective-permute-start.2 = (bf16[1024,256]{1,0:T(8,128)(2,1)S(1)}, bf16[1024,256]{1,0:T(8,128)(2,1)S(1)}, u32[]{:S(2)}, u32[]{:S(2)}) collective-permute-start(bf16[1024,256]{1,0:T(8,128)(2,1)S(1)} %collective-permute-done.refs_3_.refs_2_), channel_id=1, source_target_pairs={{0,1},{1,2},{2,3},{3,4},{4,5},{5,6},{6,7},{7,0},{8,15},{9,8},{10,9... | collective-permute-start | bytes 1572872 | tf_op jit(solution)/shard_map/ppermute | solution.py:292
  41.8 41.2 %copy-start.3 = (bf16[1024,256]{1,0:T(8,128)(2,1)}, bf16[1024,256]{1,0:T(8,128)(2,1)S(1)}, u32[]{:S(2)}) copy-start(bf16[1024,256]{1,0:T(8,128)(2,1)S(1)} %collective-permute-done.1.refs_4_.refs_3_) | copy-start | bytes 1572868
  41.8 11.1 %collective-permute-start.3 = (bf16[1024,256]{1,0:T(8,128)(2,1)S(1)}, bf16[1024,256]{1,0:T(8,128)(2,1)S(1)}, u32[]{:S(2)}, u32[]{:S(2)}) collective-permute-start(bf16[1024,256]{1,0:T(8,128)(2,1)S(1)} %collective-permute-done.1.refs_4_.refs_3_), channel_id=1, source_target_pairs={{0,1},{1,2},{2,3},{3,4},{4,5},{5,6},{6,7},{7,0},{8,15},{9,8},{10,9... | collective-permute-start | bytes 1572872 | tf_op jit(solution)/shard_map/ppermute | solution.py:292
  47.5 35.6 %copy-start.4 = (bf16[1024,256]{1,0:T(8,128)(2,1)}, bf16[1024,256]{1,0:T(8,128)(2,1)S(1)}, u32[]{:S(2)}) copy-start(bf16[1024,256]{1,0:T(8,128)(2,1)S(1)} %collective-permute-done.2.refs_5_.refs_4_) | copy-start | bytes 1572868
  47.5 11.1 %collective-permute-start.4 = (bf16[1024,256]{1,0:T(8,128)(2,1)S(1)}, bf16[1024,256]{1,0:T(8,128)(2,1)S(1)}, u32[]{:S(2)}, u32[]{:S(2)}) collective-permute-start(bf16[1024,256]{1,0:T(8,128)(2,1)S(1)} %collective-permute-done.2.refs_5_.refs_4_), channel_id=1, source_target_pairs={{0,1},{1,2},{2,3},{3,4},{4,5},{5,6},{6,7},{7,0},{8,15},{9,8},{10,9... | collective-permute-start | bytes 1572872 | tf_op jit(solution)/shard_map/ppermute | solution.py:292
  53.0 30.1 %copy-start.5 = (bf16[1024,256]{1,0:T(8,128)(2,1)}, bf16[1024,256]{1,0:T(8,128)(2,1)S(1)}, u32[]{:S(2)}) copy-start(bf16[1024,256]{1,0:T(8,128)(2,1)S(1)} %collective-permute-done.3.refs_6_.refs_5_) | copy-start | bytes 1572868
  53.0 11.3 %collective-permute-start.5 = (bf16[1024,256]{1,0:T(8,128)(2,1)S(1)}, bf16[1024,256]{1,0:T(8,128)(2,1)}, u32[]{:S(2)}, u32[]{:S(2)}) collective-permute-start(bf16[1024,256]{1,0:T(8,128)(2,1)S(1)} %collective-permute-done.3.refs_6_.refs_5_), channel_id=1, source_target_pairs={{0,1},{1,2},{2,3},{3,4},{4,5},{5,6},{6,7},{7,0},{8,15},{9,8},{10,9... | collective-permute-start | bytes 1572872 | tf_op jit(solution)/shard_map/ppermute | solution.py:292
  58.6 24.5 %copy-start.6 = (bf16[1024,256]{1,0:T(8,128)(2,1)}, bf16[1024,256]{1,0:T(8,128)(2,1)S(1)}, u32[]{:S(2)}) copy-start(bf16[1024,256]{1,0:T(8,128)(2,1)S(1)} %collective-permute-done.4.refs_7_.refs_6_) | copy-start | bytes 1572868
  58.6 29.0 %collective-permute-start.6 = (bf16[1024,256]{1,0:T(8,128)(2,1)S(1)}, bf16[1024,256]{1,0:T(8,128)(2,1)}, u32[]{:S(2)}, u32[]{:S(2)}) collective-permute-start(bf16[1024,256]{1,0:T(8,128)(2,1)S(1)} %collective-permute-done.4.refs_7_.refs_6_), channel_id=1, source_target_pairs={{0,1},{1,2},{2,3},{3,4},{4,5},{5,6},{6,7},{7,0},{8,15},{9,8},{10,9... | collective-permute-start | bytes 1572872 | tf_op jit(solution)/shard_map/ppermute | solution.py:292
  64.3 23.3 %collective-permute-start.7 = (bf16[1024,256]{1,0:T(8,128)(2,1)}, bf16[1024,256]{1,0:T(8,128)(2,1)}, u32[]{:S(2)}, u32[]{:S(2)}) collective-permute-start(bf16[1024,256]{1,0:T(8,128)(2,1)} %collective-permute-done.5.refs_8_.refs_7_), channel_id=1, source_target_pairs={{0,1},{1,2},{2,3},{3,4},{4,5},{5,6},{6,7},{7,0},{8,15},{9,8},{10,9... | collective-permute-start | bytes 1572872 | tf_op jit(solution)/shard_map/ppermute | solution.py:292
  67.1 23.2 %all-to-all-start.3 = ((f32[32,2,256]{2,1,0:T(2,128)}), f32[32,2,256]{2,1,0:T(2,128)S(1)}, u32[]{:S(2)}, u32[]{:S(2)}) async-start(f32[32,2,256]{2,1,0:T(2,128)} %broadcast_in_dim.11), calls=%async_computation.3 | async-start | bytes 131072 | tf_op jit(solution)/shard_map/all_to_all | solution.py:17
  87.6 30.4 %copy-start.15 = (f32[256,64]{0,1:T(8,128)S(1)}, f32[256,64]{0,1:T(8,128)}, u32[]{:S(2)}) copy-start(f32[256,64]{0,1:T(8,128)} %param.7) | copy-start | bytes 196612
  87.6 47.5 %copy-start.10 = (bf16[8,8,8,256]{3,2,0,1:T(8,128)(2,1)S(1)}, bf16[8,8,8,256]{3,2,0,1:T(8,128)(2,1)}, u32[]{:S(2)}) copy-start(bf16[8,8,8,256]{3,2,0,1:T(8,128)(2,1)} %copy.24) | copy-start | bytes 786436
  90.3 20.3 %all-to-all-start.1 = ((bf16[32,8,1280]{2,1,0:T(8,128)(2,1)}), bf16[32,8,1280]{2,1,0:T(8,128)(2,1)S(1)}, u32[]{:S(2)}, u32[]{:S(2)}) async-start(bf16[32,8,1280]{2,1,0:T(8,128)(2,1)} %bitcast.25), calls=%async_computation.1 | async-start | bytes 1310720 | tf_op jit(solution)/shard_map/all_to_all | solution.py:21
  113.8 21.2 %all-to-all-start.2 = ((bf16[32,8,2048]{2,1,0:T(8,128)(2,1)}), bf16[32,8,2048]{2,1,0:T(8,128)(2,1)S(1)}, u32[]{:S(2)}, u32[]{:S(2)}) async-start(bf16[32,8,2048]{2,1,0:T(8,128)(2,1)} %gathered_sum.1), calls=%async_computation.2 | async-start | bytes 2097152 | tf_op jit(solution)/shard_map/all_to_all | solution.py:21
  118.2 22.4 %collective-permute-start.8 = (bf16[1024,256]{1,0:T(8,128)(2,1)}, bf16[1024,256]{1,0:T(8,128)(2,1)S(1)}, u32[]{:S(2)}, u32[]{:S(2)}) collective-permute-start(bf16[1024,256]{1,0:T(8,128)(2,1)} %collective-permute-done.6.refs_1_.refs_8_), channel_id=1, source_target_pairs={{0,1},{1,2},{2,3},{3,4},{4,5},{5,6},{6,7},{7,0},{8,15},{9,8},{10,9... | collective-permute-start | bytes 1572872 | tf_op jit(solution)/shard_map/ppermute | solution.py:292
  121.2 22.1 %collective-permute-start.9 = (bf16[1024,256]{1,0:T(8,128)(2,1)}, bf16[1024,256]{1,0:T(8,128)(2,1)S(1)}, u32[]{:S(2)}, u32[]{:S(2)}) collective-permute-start(bf16[1024,256]{1,0:T(8,128)(2,1)} %collective-permute-done.7.refs_2_.refs_9_), channel_id=1, source_target_pairs={{0,1},{1,2},{2,3},{3,4},{4,5},{5,6},{6,7},{7,0},{8,15},{9,8},{10,9... | collective-permute-start | bytes 1572872 | tf_op jit(solution)/shard_map/ppermute | solution.py:292
  136.3 27.1 %all-to-all-start.4 = ((bf16[8,86,256]{2,1,0:T(8,128)(2,1)}), bf16[8,86,256]{2,1,0:T(8,128)(2,1)S(1)}, u32[]{:S(2)}, u32[]{:S(2)}) async-start(bf16[8,86,256]{2,1,0:T(8,128)(2,1)} %broadcast_in_dim.12), calls=%async_computation.4 | async-start | bytes 720896 | tf_op jit(solution)/shard_map/all_to_all | solution.py:17
  140.6 32.0 %copy-start.11 = (bf16[1024,256]{1,0:T(8,128)(2,1)}, bf16[1024,256]{1,0:T(8,128)(2,1)S(1)}, u32[]{:S(2)}) copy-start(bf16[1024,256]{1,0:T(8,128)(2,1)S(1)} %collective-permute-done.8.refs_10_) | copy-start | bytes 1572868
  140.6 16.2 %collective-permute-start.10 = (bf16[1024,256]{1,0:T(8,128)(2,1)S(1)}, bf16[1024,256]{1,0:T(8,128)(2,1)S(1)}, u32[]{:S(2)}, u32[]{:S(2)}) collective-permute-start(bf16[1024,256]{1,0:T(8,128)(2,1)S(1)} %collective-permute-done.8.refs_10_), channel_id=1, source_target_pairs={{0,1},{1,2},{2,3},{3,4},{4,5},{5,6},{6,7},{7,0},{8,15},{9,8},{10,9... | collective-permute-start | bytes 1572872 | tf_op jit(solution)/shard_map/ppermute | solution.py:292
  143.4 35.7 %copy-start.12 = (bf16[1024,256]{1,0:T(8,128)(2,1)}, bf16[1024,256]{1,0:T(8,128)(2,1)S(1)}, u32[]{:S(2)}) copy-start(bf16[1024,256]{1,0:T(8,128)(2,1)S(1)} %collective-permute-done.9.refs_11_) | copy-start | bytes 1572868
  143.4 19.1 %collective-permute-start.11 = (bf16[1024,256]{1,0:T(8,128)(2,1)S(1)}, bf16[1024,256]{1,0:T(8,128)(2,1)S(1)}, u32[]{:S(2)}, u32[]{:S(2)}) collective-permute-start(bf16[1024,256]{1,0:T(8,128)(2,1)S(1)} %collective-permute-done.9.refs_11_), channel_id=1, source_target_pairs={{0,1},{1,2},{2,3},{3,4},{4,5},{5,6},{6,7},{7,0},{8,15},{9,8},{10,9... | collective-permute-start | bytes 1572872 | tf_op jit(solution)/shard_map/ppermute | solution.py:292
  156.8 22.2 %copy-start.13 = (bf16[1024,256]{1,0:T(8,128)(2,1)}, bf16[1024,256]{1,0:T(8,128)(2,1)S(1)}, u32[]{:S(2)}) copy-start(bf16[1024,256]{1,0:T(8,128)(2,1)S(1)} %collective-permute-done.10.refs_12_) | copy-start | bytes 1572868
  156.8 22.2 %collective-permute-start.12 = (bf16[1024,256]{1,0:T(8,128)(2,1)S(1)}, bf16[1024,256]{1,0:T(8,128)(2,1)}, u32[]{:S(2)}, u32[]{:S(2)}) collective-permute-start(bf16[1024,256]{1,0:T(8,128)(2,1)S(1)} %collective-permute-done.10.refs_12_), channel_id=1, source_target_pairs={{0,1},{1,2},{2,3},{3,4},{4,5},{5,6},{6,7},{7,0},{8,15},{9,8},{10,9... | collective-permute-start | bytes 1572872 | tf_op jit(solution)/shard_map/ppermute | solution.py:292
  162.5 16.6 %collective-permute-start.13 = (bf16[1024,256]{1,0:T(8,128)(2,1)S(1)}, bf16[1024,256]{1,0:T(8,128)(2,1)}, u32[]{:S(2)}, u32[]{:S(2)}) collective-permute-start(bf16[1024,256]{1,0:T(8,128)(2,1)S(1)} %collective-permute-done.11.refs_13_), channel_id=1, source_target_pairs={{0,1},{1,2},{2,3},{3,4},{4,5},{5,6},{6,7},{7,0},{8,15},{9,8},{10,9... | collective-permute-start | bytes 1572872 | tf_op jit(solution)/shard_map/ppermute | solution.py:292
  172.6 15.9 %all-to-all-start.5 = ((bf16[32,64,128]{2,1,0:T(8,128)(2,1)}), bf16[32,64,128]{2,1,0:T(8,128)(2,1)S(1)}, u32[]{:S(2)}, u32[]{:S(2)}) async-start(bf16[32,64,128]{2,1,0:T(8,128)(2,1)} %get-tuple-element.12), calls=%async_computation.5 | async-start | bytes 1048576 | tf_op jit(solution)/shard_map/all_to_all | solution.py:21
  193.8 23.8 %all-to-all-start.6 = ((bf16[32,64,256]{2,1,0:T(8,128)(2,1)}), bf16[32,64,256]{2,1,0:T(8,128)(2,1)S(1)}, u32[]{:S(2)}, u32[]{:S(2)}) async-start(bf16[32,64,256]{2,1,0:T(8,128)(2,1)} %undone_copies.1), calls=%async_computation.6 | async-start | bytes 2097152 | tf_op jit(solution)/shard_map/all_to_all | solution.py:21
  (6 other events, 40.2 us)
Sparse Core Ops, SparseCore 0:
  27.6 56.1 all-gather.1

commit v5 on v4

--- a/solution.py
+++ b/solution.py
@@ -10,6 +10,7 @@
 BF16 = jnp.bfloat16
 VMEM = pl.BlockSpec(memory_space=pltpu.VMEM)
 LIMIT = 60 * 1024 * 1024
+SMALL = 20 * 1024 * 1024
 
 
 def copy_for_each(shard, axis):
@@ -54,8 +55,8 @@
     return pl.CostEstimate(flops=flops, bytes_accessed=nbytes, transcendentals=0)
 
 
-def params():
-    return pltpu.CompilerParams(vmem_limit_bytes=LIMIT)
+def params(limit=LIMIT):
+    return pltpu.CompilerParams(vmem_limit_bytes=limit)
 
 
 def gram_body(hops, half, own_ref, *refs):
@@ -137,7 +138,7 @@
         out_shape=jax.ShapeDtypeStruct((groups, few, 2 * half * width), BF16),
         in_specs=[VMEM],
         out_specs=VMEM,
-        compiler_params=params(),
+        compiler_params=params(SMALL),
         cost_estimate=cost(2 * got.size, 4 * got.size),
         name="gathered_sum",
     )(got)
@@ -153,9 +154,9 @@
         @pl.when(pl.program_id(0) == 0)
         def _():
             for p in range(planes):
-                right_ref[:, p * width : (p + 1) * width] = shared_ref[p, :narrow, :]
-
-        value = contract_last(basis_ref[...], right_ref[...])
+                right_ref[p * width : (p + 1) * width, :] = shared_ref[p, :narrow, :].T
+
+        value = product(basis_ref[...], right_ref[...])
         out_ref[...] = value
         for k in range(each):
             piece = value[k * narrow : (k + 1) * narrow].astype(BF16)
@@ -177,18 +178,18 @@
             pl.BlockSpec((rows, narrow), lambda i: (i, 0)),
             pl.BlockSpec((each, narrow, 2 * narrow), lambda i: (i, 0, 0)),
         ],
-        scratch_shapes=[pltpu.VMEM((narrow, dim), BF16)],
+        scratch_shapes=[pltpu.VMEM((dim, narrow), BF16)],
         compiler_params=params(),
         cost_estimate=cost(2 * dim * dim * narrow, 2 * dim * dim),
         name="rotated_cols",
     )(basis_t, shared, spread)
 
 
-def undone_copies(rot, back, spread, kernel_t, basis_t, plane, n, width):
+def undone_copies(rot, back, spread, kernel_t, basis, n):
     dim, narrow = rot.shape
-    groups = back.shape[0]
-
-    def body(plane_ref, rot_ref, back_ref, spread_ref, kernel_ref, basis_ref, out_ref):
+    groups, width = back.shape[0], basis.shape[1]
+
+    def body(rot_ref, back_ref, spread_ref, kernel_ref, basis_ref, out_ref):
         halfway = narrow // 2
         crossed = jnp.concatenate([spread_ref[halfway:, :], spread_ref[:halfway, :]], axis=0)
         crossed = crossed.T.astype(BF16)
@@ -202,8 +203,7 @@
             scaled = scaled * kernel_ref[:, at]
             high = scaled.astype(BF16)
             low = (scaled - high.astype(F32)).astype(BF16)
-            basis = basis_ref[at, :]
-            total += product(high, basis) + product(low, basis)
+            total += product(high, basis_ref[at, :]) + product(low, basis_ref[at, :])
         value = total.astype(BF16)
 
         def store(i, carry):
@@ -212,26 +212,15 @@
 
         lax.fori_loop(0, groups, store, 0)
 
-    full = lambda shape: pl.BlockSpec(shape, lambda i, plane_ref: (0,) * len(shape))
     return pl.pallas_call(
         body,
         out_shape=jax.ShapeDtypeStruct((groups, narrow, width), BF16),
-        grid_spec=pltpu.PrefetchScalarGridSpec(
-            num_scalar_prefetch=1,
-            grid=(1,),
-            in_specs=[
-                full(rot.shape),
-                full(back.shape),
-                full(spread.shape),
-                full(kernel_t.shape),
-                pl.BlockSpec((dim, width), lambda i, plane_ref: (0, plane_ref[0])),
-            ],
-            out_specs=full((groups, narrow, width)),
-        ),
-        compiler_params=params(),
+        in_specs=[VMEM] * 5,
+        out_specs=VMEM,
+        compiler_params=params(SMALL),
         cost_estimate=cost(4 * dim * narrow * width, 4 * dim * width),
         name="undone_copies",
-    )(plane, rot, back, spread, kernel_t, basis_t)
+    )(rot, back, spread, kernel_t, basis)
 
 
 def first_product(places, told, whiten, blocks):
@@ -329,15 +318,16 @@
     first = r * narrow
     kernel_t = divided(lax.dynamic_slice_in_dim(eigvals, first, narrow), eigvals, first)
 
-    copies = undone_copies(rot, back, spread, kernel_t, basis_t, f[None], float(n), width)
+    basis_f = lax.dynamic_slice_in_dim(basis_t, f * width, width, axis=1)
+    copies = undone_copies(rot, back, spread, kernel_t, basis_f, float(n))
     undone = exchange(copies, "rows").reshape(dim, width)
 
     places = ((f + way * jnp.arange(planes, dtype=jnp.int32)) % planes).astype(jnp.int32)
     told = shared[:, narrow + few :].astype(F32).reshape(planes, 3, 2, width)
     told = jnp.sum(told, axis=1).reshape(2 * planes, width)
     centered, running = first_product(places, told, whiten, blocks)
-    turned = lax.optimization_barrier(contract_last(centered, basis_t).astype(BF16))
-    return (running + product(turned, undone) * (1.0 / total)).astype(BF16)
+    turned = (contract_last(centered, basis_t) * (1.0 / total)).astype(BF16)
+    return (running + product(lax.optimization_barrier(turned), undone)).astype(BF16)
 
 
 def solution(mesh):

time: 230 us -> 226 us (0.983)
  Pallas kernels: 30.8 us -> 28.2 us
    unnamed x36 -> x30, local copies, waits for them, and re-layouts: 4.76 us -> 3.14 us
  transfers between devices with their start and end apart: 21 -> 21, of which waited for: 12 -> 12; matrix products, arithmetic and copies ran while one was open for 12% -> 13% of each run, Pallas kernels for 11% -> 11%
where the time goes in v5:
time: 226 us; the launch traced here: 225 us
  waiting for transfers between devices  75 us (33%)
  starting transfers between devices  54.2 us (24%)
  Pallas kernels  28.2 us (12%)
  blocking collectives  19.3 us (9%)
  matrix products  18 us (8%)
  between operations  13.7 us (6%)
  other arithmetic  9 us (4%)
  local copies, waits for them, and re-layouts  7.37 us (3%)
    ppermute x14, waiting for transfers between devices, pass_on(): return lax.ppermute(value, ('rows', 'feat'), pairs)  45.4 us
    all_to_all x4, waiting for transfers between devices, exchange(): return lax.all_to_all(parts, axis, split_axis=0, concat_axis=0, tiled=True)  29.5 us
    all_to_all x4, starting transfers between devices, exchange(): return lax.all_to_all(parts, axis, split_axis=0, concat_axis=0, tiled=True)  22.9 us
    all_to_all x1, blocking collectives, copy_for_each(): return lax.all_to_all(copies, axis, split_axis=0, concat_axis=0, tiled=True)  19.3 us
    ppermute x14, starting transfers between devices, pass_on(): return lax.ppermute(value, ('rows', 'feat'), pairs)  16.5 us
    all_to_all x2, starting transfers between devices, copy_for_each(): return lax.all_to_all(copies, axis, split_axis=0, concat_axis=0, tiled=True)  14.9 us
    dot_general x2, matrix products, contract_last(): lax.dot_general(a, b, (((1,), (1,)), ((), ())), preferred_element_type=F32)  14.4 us
    pallas_call x1, Pallas kernels, rotated_cols(): pl.pallas_call(body, out_shape=[jax.ShapeDtypeStruct((dim, narrow), F32),...  8.64 us
  transfers between devices with their start and end apart: 21, of which 12 were waited for; matrix products, arithmetic and copies ran while one was open for 13% of the time, Pallas kernels for 11%

profile of v5, /device:TPU:1, one launch (start us, length us, event | category | flops | bytes accessed | tf_op | source)
XLA Modules:
  0.0 224.8 jit_solution(8410536687972607800)
XLA Ops:
  7.5 19.3 %all_to_all.35 = bf16[8,64,256]{2,1,0:T(8,128)(2,1)S(1)} all-to-all(bf16[8,64,256]{2,1,0:T(8,128)(2,1)S(1)} %broadcast_in_dim.8), channel_id=1, replica_groups=mesh['rows'=32,'feat'=8] {'feat'}, dimensions={0} | all-to-all | bytes 524288 | tf_op jit(solution)/shard_map/all_to_all | solution.py:18
  27.6 1.6 collective-permute-start.1
  29.2 6.9 %collective-permute-done.refs_3_.refs_2_ = bf16[1024,256]{1,0:T(8,128)(2,1)S(1)} collective-permute-done((bf16[1024,256]{1,0:T(8,128)(2,1)}, bf16[1024,256]{1,0:T(8,128)(2,1)S(1)}, u32[]{:S(2)}, u32[]{:S(2)}) %collective-permute-start) | collective-permute-done | bytes 524320 | tf_op jit(solution)/shard_map/ppermute | solution.py:281
  37.1 4.8 %collective-permute-done.1.refs_4_.refs_3_ = bf16[1024,256]{1,0:T(8,128)(2,1)S(1)} collective-permute-done((bf16[1024,256]{1,0:T(8,128)(2,1)}, bf16[1024,256]{1,0:T(8,128)(2,1)S(1)}, u32[]{:S(2)}, u32[]{:S(2)}) %collective-permute-start.1) | collective-permute-done | bytes 524320 | tf_op jit(solution)/shard_map/ppermute | solution.py:281
  42.7 4.8 %collective-permute-done.2.refs_5_.refs_4_ = bf16[1024,256]{1,0:T(8,128)(2,1)S(1)} collective-permute-done((bf16[1024,256]{1,0:T(8,128)(2,1)S(1)}, bf16[1024,256]{1,0:T(8,128)(2,1)S(1)}, u32[]{:S(2)}, u32[]{:S(2)}) %collective-permute-start.2) | collective-permute-done | bytes 524320 | tf_op jit(solution)/shard_map/ppermute | solution.py:281
  48.3 4.7 %collective-permute-done.3.refs_6_.refs_5_ = bf16[1024,256]{1,0:T(8,128)(2,1)S(1)} collective-permute-done((bf16[1024,256]{1,0:T(8,128)(2,1)S(1)}, bf16[1024,256]{1,0:T(8,128)(2,1)S(1)}, u32[]{:S(2)}, u32[]{:S(2)}) %collective-permute-start.3) | collective-permute-done | bytes 524320 | tf_op jit(solution)/shard_map/ppermute | solution.py:281
  53.0 1.3 collective-permute-start.5
  55.5 3.1 %collective-permute-done.4.refs_7_.refs_6_ = bf16[1024,256]{1,0:T(8,128)(2,1)S(1)} collective-permute-done((bf16[1024,256]{1,0:T(8,128)(2,1)S(1)}, bf16[1024,256]{1,0:T(8,128)(2,1)S(1)}, u32[]{:S(2)}, u32[]{:S(2)}) %collective-permute-start.4) | collective-permute-done | bytes 524320 | tf_op jit(solution)/shard_map/ppermute | solution.py:281
  59.5 4.8 %collective-permute-done.5.refs_8_.refs_7_ = bf16[1024,256]{1,0:T(8,128)(2,1)} collective-permute-done((bf16[1024,256]{1,0:T(8,128)(2,1)S(1)}, bf16[1024,256]{1,0:T(8,128)(2,1)}, u32[]{:S(2)}, u32[]{:S(2)}) %collective-permute-start.5) | collective-permute-done | bytes 524320 | tf_op jit(solution)/shard_map/ppermute | solution.py:281
  67.1 10.6 %all-to-all-start.3 = ((f32[32,2,256]{2,1,0:T(2,128)}), f32[32,2,256]{2,1,0:T(2,128)S(1)}, u32[]{:S(2)}, u32[]{:S(2)}) async-start(f32[32,2,256]{2,1,0:T(2,128)} %broadcast_in_dim.9), calls=%async_computation.3 | async-start | bytes 131072 | tf_op jit(solution)/shard_map/all_to_all | solution.py:18
  77.7 2.1 copy.20
  80.8 2.3 %pad_maximum_fusion.refs_0_ = bf16[256,2048]{1,0:T(8,128)(2,1)} fusion(bf16[256,1024]{1,0:T(8,128)(2,1)} %bitcast.25, bf16[256,1024]{1,0:T(8,128)(2,1)} %bitcast.26), kind=kLoop, calls=%fused_computation.3 | loop fusion | flops 2097152 | bytes 2097152 | tf_op jit(solution)/shard_map/concatenate | solution.py:300
  83.1 4.5 %gram_first.1.partial_ref = bf16[256,1280]{1,0:T(8,128)(2,1)} custom-call(bf16[256,2048]{1,0:T(8,128)(2,1)} %pad_maximum_fusion.refs_0_, bf16[1024,256]{1,0:T(8,128)(2,1)} %refs_0_.1, bf16[1024,256]{1,0:T(8,128)(2,1)} %refs_1_.3, bf16[1024,256]{1,0:T(8,128)(2,1)} %copy-done.2, bf16[1024,256]{1,0:T(8,128)(2,1)} %copy-done.3, bf16[1024,256]{1,0:T(8,128)(2,1)} %copy-done.4, ...), custom_call_target="tpu_custom_call" | custom-call | flops 1073741824 | bytes 5242880 | tf_op jit(solution)/shard_map/gram_first/pallas_call | solution.py:83
  87.7 2.7 %gram_last.1 = bf16[256,1280]{1,0:T(8,128)(2,1)} custom-call(bf16[256,1280]{1,0:T(8,128)(2,1)} %gram_first.1.partial_ref, bf16[256,2048]{1,0:T(8,128)(2,1)} %pad_maximum_fusion.refs_0_, bf16[1024,256]{1,0:T(8,128)(2,1)} %collective-permute-done.6.refs_1_.refs_8_, bf16[1024,256]{1,0:T(8,128)(2,1)} %collective-permute-done.7.refs_2_.refs_9_), custom_call_target="tpu_custom_call", output_to_operand_aliasing={{}: (0, {})} | custom-call | flops 268435456 | bytes 2097152 | tf_op jit(solution)/shard_map/gram_last/pallas_call | solution.py:101
  90.4 7.4 %all-to-all-start.1 = ((bf16[32,8,1280]{2,1,0:T(8,128)(2,1)}), bf16[32,8,1280]{2,1,0:T(8,128)(2,1)S(1)}, u32[]{:S(2)}, u32[]{:S(2)}) async-start(bf16[32,8,1280]{2,1,0:T(8,128)(2,1)} %bitcast.24), calls=%async_computation.1 | async-start | bytes 1310720 | tf_op jit(solution)/shard_map/all_to_all | solution.py:22
  97.9 12.7 %all-to-all-done.1.got_ref = bf16[32,8,1280]{2,1,0:T(8,128)(2,1)S(1)} async-done(((bf16[32,8,1280]{2,1,0:T(8,128)(2,1)}), bf16[32,8,1280]{2,1,0:T(8,128)(2,1)S(1)}, u32[]{:S(2)}, u32[]{:S(2)}) %all-to-all-start.1) | async-done | bytes 655392 | tf_op jit(solution)/shard_map/all_to_all | solution.py:22
  110.6 1.4 gathered_sum.1
  112.0 4.1 %all-to-all-start.2 = ((bf16[32,8,2048]{2,1,0:T(8,128)(2,1)}), bf16[32,8,2048]{2,1,0:T(8,128)(2,1)S(1)}, u32[]{:S(2)}, u32[]{:S(2)}) async-start(bf16[32,8,2048]{2,1,0:T(8,128)(2,1)} %gathered_sum.1), calls=%async_computation.2 | async-start | bytes 2097152 | tf_op jit(solution)/shard_map/all_to_all | solution.py:22
  116.3 3.1 %collective-permute-start.8 = (bf16[1024,256]{1,0:T(8,128)(2,1)}, bf16[1024,256]{1,0:T(8,128)(2,1)S(1)}, u32[]{:S(2)}, u32[]{:S(2)}) collective-permute-start(bf16[1024,256]{1,0:T(8,128)(2,1)} %collective-permute-done.6.refs_1_.refs_8_), channel_id=1, source_target_pairs={{0,1},{1,2},{2,3},{3,4},{4,5},{5,6},{6,7},{7,0},{8,15},{9,8},{10,9... | collective-permute-start | bytes 1572872 | tf_op jit(solution)/shard_map/ppermute | solution.py:281
  119.8 13.5 %all-to-all-done.2 = bf16[32,8,2048]{2,1,0:T(8,128)(2,1)S(1)} async-done(((bf16[32,8,2048]{2,1,0:T(8,128)(2,1)}), bf16[32,8,2048]{2,1,0:T(8,128)(2,1)S(1)}, u32[]{:S(2)}, u32[]{:S(2)}) %all-to-all-start.2) | async-done | bytes 1048608 | tf_op jit(solution)/shard_map/all_to_all | solution.py:22
  134.5 4.3 %all-to-all-start.4 = ((bf16[8,86,256]{2,1,0:T(8,128)(2,1)}), bf16[8,86,256]{2,1,0:T(8,128)(2,1)S(1)}, u32[]{:S(2)}, u32[]{:S(2)}) async-start(bf16[8,86,256]{2,1,0:T(8,128)(2,1)} %broadcast_in_dim.10), calls=%async_computation.4 | async-start | bytes 720896 | tf_op jit(solution)/shard_map/all_to_all | solution.py:18
  138.8 2.7 %collective-permute-start.10 = (bf16[1024,256]{1,0:T(8,128)(2,1)S(1)}, bf16[1024,256]{1,0:T(8,128)(2,1)}, u32[]{:S(2)}, u32[]{:S(2)}) collective-permute-start(bf16[1024,256]{1,0:T(8,128)(2,1)S(1)} %collective-permute-done.8.refs_10_), channel_id=1, source_target_pairs={{0,1},{1,2},{2,3},{3,4},{4,5},{5,6},{6,7},{7,0},{8,15},{9,8},{10,9... | collective-permute-start | bytes 1572872 | tf_op jit(solution)/shard_map/ppermute | solution.py:281
  143.5 11.6 %collective-permute-done.10.refs_12_ = bf16[1024,256]{1,0:T(8,128)(2,1)} collective-permute-done((bf16[1024,256]{1,0:T(8,128)(2,1)S(1)}, bf16[1024,256]{1,0:T(8,128)(2,1)}, u32[]{:S(2)}, u32[]{:S(2)}) %collective-permute-start.10) | collective-permute-done | bytes 524320 | tf_op jit(solution)/shard_map/ppermute | solution.py:281
  156.1 4.7 %collective-permute-done.11.refs_13_ = bf16[1024,256]{1,0:T(8,128)(2,1)} collective-permute-done((bf16[1024,256]{1,0:T(8,128)(2,1)S(1)}, bf16[1024,256]{1,0:T(8,128)(2,1)}, u32[]{:S(2)}, u32[]{:S(2)}) %collective-permute-start.11) | collective-permute-done | bytes 524320 | tf_op jit(solution)/shard_map/ppermute | solution.py:281
  162.4 8.6 %rotated_cols.1 = (f32[2048,64]{1,0:T(8,128)}, bf16[32,64,128]{2,1,0:T(8,128)(2,1)}) custom-call(bf16[2048,2048]{1,0:T(8,128)(2,1)} %all-gather.2.cloned.1.call-done.basis_ref, bf16[8,86,256]{2,1,0:T(8,128)(2,1)} %copy-done.7, bf16[64,64]{1,0:T(8,128)(2,1)} %fusion.8.spread_ref), custom_call_target="tpu_custom_call" | custom-call | flops 536870912 | bytes 8388608 | tf_op jit(solution)/shard_map/rotated_cols/pallas_call | solution.py:165
  171.1 4.3 %all-to-all-start.5 = ((bf16[32,64,128]{2,1,0:T(8,128)(2,1)}), bf16[32,64,128]{2,1,0:T(8,128)(2,1)S(1)}, u32[]{:S(2)}, u32[]{:S(2)}) async-start(bf16[32,64,128]{2,1,0:T(8,128)(2,1)} %get-tuple-element.12), calls=%async_computation.5 | async-start | bytes 1048576 | tf_op jit(solution)/shard_map/all_to_all | solution.py:22
  176.9 8.3 %first_product.1 = (bf16[1024,2048]{1,0:T(8,128)(2,1)}, f32[1024,256]{1,0:T(8,128)}) custom-call(s32[8]{0:T(128)} %and_select_fusion.place_ref, f32[16,256]{1,0:T(8,128)} %reshape.44.told_ref, bf16[2048,256]{1,0:T(8,128)(2,1)} %whiten_ref.1, bf16[1024,256]{1,0:T(8,128)(2,1)} %refs_0_.1, bf16[1024,256]{1,0:T(8,128)(2,1)} %refs_1_.3, ...), custom_call_target="tpu_custom_call" | custom-call | flops 1073741824 | bytes 12582912 | tf_op jit(solution)/shard_map/first_product/pallas_call | solution.py:247
  186.9 2.6 %undone_copies.1 = bf16[32,64,256]{2,1,0:T(8,128)(2,1)} custom-call(f32[2048,64]{1,0:T(8,128)S(1)} %copy-done, bf16[32,64,128]{2,1,0:T(8,128)(2,1)S(1)} %all-to-all-done.5.back_ref, f32[64,64]{1,0:T(8,128)S(1)} %pad_maximum_fusion.1.spread_ref, f32[64,2048]{1,0:T(8,128)S(1)} %divide_select_fusion.kernel_ref, ...), custom_call_target="tpu_custom_call" | custom-call | flops 134217728 | bytes 2097152 | tf_op jit(solution)/shard_map/undone_copies/pallas_call | solution.py:215
  189.5 7.1 %all-to-all-start.6 = ((bf16[32,64,256]{2,1,0:T(8,128)(2,1)}), bf16[32,64,256]{2,1,0:T(8,128)(2,1)S(1)}, u32[]{:S(2)}, u32[]{:S(2)}) async-start(bf16[32,64,256]{2,1,0:T(8,128)(2,1)} %undone_copies.1), calls=%async_computation.6 | async-start | bytes 2097152 | tf_op jit(solution)/shard_map/all_to_all | solution.py:22
  196.6 14.0 %multiply_convert_fusion = bf16[1024,2048]{1,0:T(8,128)(2,1)} fusion(bf16[1024,2048]{1,0:T(8,128)(2,1)} %get-tuple-element.10, bf16[2048,2048]{1,0:T(8,128)(2,1)} %all-gather.2.cloned.1.call-done.basis_ref), kind=kOutput, calls=%fused_computation | convolution fusion | flops 8594128896 | bytes 16777216 | tf_op jit(solution)/shard_map/dot_general | solution.py:26
  210.5 3.1 %all-to-all-done.6 = bf16[32,64,256]{2,1,0:T(8,128)(2,1)S(1)} async-done(((bf16[32,64,256]{2,1,0:T(8,128)(2,1)}), bf16[32,64,256]{2,1,0:T(8,128)(2,1)S(1)}, u32[]{:S(2)}, u32[]{:S(2)}) %all-to-all-start.6) | async-done | bytes 1048608 | tf_op jit(solution)/shard_map/all_to_all | solution.py:22
  213.6 3.4 %fusion.11 = f32[1024,256]{1,0:T(8,128)S(1)} fusion(bf16[1024,2048]{1,0:T(8,128)(2,1)} %multiply_convert_fusion, bf16[2048,256]{1,0:T(8,128)(2,1)S(1)} %bitcast.27), kind=kOutput, calls=%fused_computation.41 | convolution fusion | flops 1073741824 | bytes 6291456 | tf_op jit(solution)/shard_map/dot_general | solution.py:30
  (84 shorter events, 20.8 us)
Async XLA Ops:
  6.5 73.2 %copy-start.1 = (bf16[1024,256]{1,0:T(8,128)(2,1)S(1)}, bf16[1024,256]{1,0:T(8,128)(2,1)}, u32[]{:S(2)}) copy-start(bf16[1024,256]{1,0:T(8,128)(2,1)} %refs_1_.3) | copy-start | bytes 1572868
  6.5 155.9 %all-gather.2.cloned.1.call-start = ((), (), s32[]{:S(2)}) async-start(), calls=%async_computation.7 | async-start | bytes 8650752 | tf_op jit(solution)/shard_map/all_gather | solution.py:298
  27.5 8.6 %collective-permute-start = (bf16[1024,256]{1,0:T(8,128)(2,1)}, bf16[1024,256]{1,0:T(8,128)(2,1)S(1)}, u32[]{:S(2)}, u32[]{:S(2)}) collective-permute-start(bf16[1024,256]{1,0:T(8,128)(2,1)} %refs_0_.1), channel_id=1, source_target_pairs={{0,1},{1,2},{2,3},{3,4},{4,5},{5,6},{6,7},{7,0},{8,15},{9,8},{10,9... | collective-permute-start | bytes 1572872 | tf_op jit(solution)/shard_map/ppermute | solution.py:281
  27.6 14.2 %collective-permute-start.1 = (bf16[1024,256]{1,0:T(8,128)(2,1)}, bf16[1024,256]{1,0:T(8,128)(2,1)S(1)}, u32[]{:S(2)}, u32[]{:S(2)}) collective-permute-start(bf16[1024,256]{1,0:T(8,128)(2,1)} %refs_1_.3), channel_id=1, source_target_pairs={{0,1},{1,2},{2,3},{3,4},{4,5},{5,6},{6,7},{7,0},{8,15},{9,8},{10,9... | collective-permute-start | bytes 1572872 | tf_op jit(solution)/shard_map/ppermute | solution.py:281
  36.1 47.0 %copy-start.2 = (bf16[1024,256]{1,0:T(8,128)(2,1)}, bf16[1024,256]{1,0:T(8,128)(2,1)S(1)}, u32[]{:S(2)}) copy-start(bf16[1024,256]{1,0:T(8,128)(2,1)S(1)} %collective-permute-done.refs_3_.refs_2_) | copy-start | bytes 1572868
  36.1 11.3 %collective-permute-start.2 = (bf16[1024,256]{1,0:T(8,128)(2,1)S(1)}, bf16[1024,256]{1,0:T(8,128)(2,1)S(1)}, u32[]{:S(2)}, u32[]{:S(2)}) collective-permute-start(bf16[1024,256]{1,0:T(8,128)(2,1)S(1)} %collective-permute-done.refs_3_.refs_2_), channel_id=1, source_target_pairs={{0,1},{1,2},{2,3},{3,4},{4,5},{5,6},{6,7},{7,0},{8,15},{9,8},{10,9... | collective-permute-start | bytes 1572872 | tf_op jit(solution)/shard_map/ppermute | solution.py:281
  41.8 41.2 %copy-start.3 = (bf16[1024,256]{1,0:T(8,128)(2,1)}, bf16[1024,256]{1,0:T(8,128)(2,1)S(1)}, u32[]{:S(2)}) copy-start(bf16[1024,256]{1,0:T(8,128)(2,1)S(1)} %collective-permute-done.1.refs_4_.refs_3_) | copy-start | bytes 1572868
  41.9 11.1 %collective-permute-start.3 = (bf16[1024,256]{1,0:T(8,128)(2,1)S(1)}, bf16[1024,256]{1,0:T(8,128)(2,1)S(1)}, u32[]{:S(2)}, u32[]{:S(2)}) collective-permute-start(bf16[1024,256]{1,0:T(8,128)(2,1)S(1)} %collective-permute-done.1.refs_4_.refs_3_), channel_id=1, source_target_pairs={{0,1},{1,2},{2,3},{3,4},{4,5},{5,6},{6,7},{7,0},{8,15},{9,8},{10,9... | collective-permute-start | bytes 1572872 | tf_op jit(solution)/shard_map/ppermute | solution.py:281
  47.5 35.6 %copy-start.4 = (bf16[1024,256]{1,0:T(8,128)(2,1)}, bf16[1024,256]{1,0:T(8,128)(2,1)S(1)}, u32[]{:S(2)}) copy-start(bf16[1024,256]{1,0:T(8,128)(2,1)S(1)} %collective-permute-done.2.refs_5_.refs_4_) | copy-start | bytes 1572868
  47.5 11.1 %collective-permute-start.4 = (bf16[1024,256]{1,0:T(8,128)(2,1)S(1)}, bf16[1024,256]{1,0:T(8,128)(2,1)S(1)}, u32[]{:S(2)}, u32[]{:S(2)}) collective-permute-start(bf16[1024,256]{1,0:T(8,128)(2,1)S(1)} %collective-permute-done.2.refs_5_.refs_4_), channel_id=1, source_target_pairs={{0,1},{1,2},{2,3},{3,4},{4,5},{5,6},{6,7},{7,0},{8,15},{9,8},{10,9... | collective-permute-start | bytes 1572872 | tf_op jit(solution)/shard_map/ppermute | solution.py:281
  53.0 30.1 %copy-start.5 = (bf16[1024,256]{1,0:T(8,128)(2,1)}, bf16[1024,256]{1,0:T(8,128)(2,1)S(1)}, u32[]{:S(2)}) copy-start(bf16[1024,256]{1,0:T(8,128)(2,1)S(1)} %collective-permute-done.3.refs_6_.refs_5_) | copy-start | bytes 1572868
  53.0 11.3 %collective-permute-start.5 = (bf16[1024,256]{1,0:T(8,128)(2,1)S(1)}, bf16[1024,256]{1,0:T(8,128)(2,1)}, u32[]{:S(2)}, u32[]{:S(2)}) collective-permute-start(bf16[1024,256]{1,0:T(8,128)(2,1)S(1)} %collective-permute-done.3.refs_6_.refs_5_), channel_id=1, source_target_pairs={{0,1},{1,2},{2,3},{3,4},{4,5},{5,6},{6,7},{7,0},{8,15},{9,8},{10,9... | collective-permute-start | bytes 1572872 | tf_op jit(solution)/shard_map/ppermute | solution.py:281
  58.6 24.5 %copy-start.6 = (bf16[1024,256]{1,0:T(8,128)(2,1)}, bf16[1024,256]{1,0:T(8,128)(2,1)S(1)}, u32[]{:S(2)}) copy-start(bf16[1024,256]{1,0:T(8,128)(2,1)S(1)} %collective-permute-done.4.refs_7_.refs_6_) | copy-start | bytes 1572868
  58.6 29.0 %collective-permute-start.6 = (bf16[1024,256]{1,0:T(8,128)(2,1)S(1)}, bf16[1024,256]{1,0:T(8,128)(2,1)}, u32[]{:S(2)}, u32[]{:S(2)}) collective-permute-start(bf16[1024,256]{1,0:T(8,128)(2,1)S(1)} %collective-permute-done.4.refs_7_.refs_6_), channel_id=1, source_target_pairs={{0,1},{1,2},{2,3},{3,4},{4,5},{5,6},{6,7},{7,0},{8,15},{9,8},{10,9... | collective-permute-start | bytes 1572872 | tf_op jit(solution)/shard_map/ppermute | solution.py:281
  64.3 23.3 %collective-permute-start.7 = (bf16[1024,256]{1,0:T(8,128)(2,1)}, bf16[1024,256]{1,0:T(8,128)(2,1)}, u32[]{:S(2)}, u32[]{:S(2)}) collective-permute-start(bf16[1024,256]{1,0:T(8,128)(2,1)} %collective-permute-done.5.refs_8_.refs_7_), channel_id=1, source_target_pairs={{0,1},{1,2},{2,3},{3,4},{4,5},{5,6},{6,7},{7,0},{8,15},{9,8},{10,9... | collective-permute-start | bytes 1572872 | tf_op jit(solution)/shard_map/ppermute | solution.py:281
  67.1 23.3 %all-to-all-start.3 = ((f32[32,2,256]{2,1,0:T(2,128)}), f32[32,2,256]{2,1,0:T(2,128)S(1)}, u32[]{:S(2)}, u32[]{:S(2)}) async-start(f32[32,2,256]{2,1,0:T(2,128)} %broadcast_in_dim.9), calls=%async_computation.3 | async-start | bytes 131072 | tf_op jit(solution)/shard_map/all_to_all | solution.py:18
  83.1 14.7 %copy-start.13 = (f32[2048]{0:T(1024)S(1)}, f32[2048]{0:T(1024)}, u32[]{:S(2)}) copy-start(f32[2048]{0:T(1024)} %param.8) | copy-start | bytes 24580
  87.6 28.5 %copy-start.12 = (f32[256,64]{0,1:T(8,128)S(1)}, f32[256,64]{0,1:T(8,128)}, u32[]{:S(2)}) copy-start(f32[256,64]{0,1:T(8,128)} %param.7) | copy-start | bytes 196612
  87.6 45.6 %copy-start.9 = (bf16[8,8,8,256]{3,2,0,1:T(8,128)(2,1)S(1)}, bf16[8,8,8,256]{3,2,0,1:T(8,128)(2,1)}, u32[]{:S(2)}) copy-start(bf16[8,8,8,256]{3,2,0,1:T(8,128)(2,1)} %copy.24) | copy-start | bytes 786436
  90.4 20.2 %all-to-all-start.1 = ((bf16[32,8,1280]{2,1,0:T(8,128)(2,1)}), bf16[32,8,1280]{2,1,0:T(8,128)(2,1)S(1)}, u32[]{:S(2)}, u32[]{:S(2)}) async-start(bf16[32,8,1280]{2,1,0:T(8,128)(2,1)} %bitcast.24), calls=%async_computation.1 | async-start | bytes 1310720 | tf_op jit(solution)/shard_map/all_to_all | solution.py:22
  112.0 21.2 %all-to-all-start.2 = ((bf16[32,8,2048]{2,1,0:T(8,128)(2,1)}), bf16[32,8,2048]{2,1,0:T(8,128)(2,1)S(1)}, u32[]{:S(2)}, u32[]{:S(2)}) async-start(bf16[32,8,2048]{2,1,0:T(8,128)(2,1)} %gathered_sum.1), calls=%async_computation.2 | async-start | bytes 2097152 | tf_op jit(solution)/shard_map/all_to_all | solution.py:22
  116.3 22.5 %collective-permute-start.8 = (bf16[1024,256]{1,0:T(8,128)(2,1)}, bf16[1024,256]{1,0:T(8,128)(2,1)S(1)}, u32[]{:S(2)}, u32[]{:S(2)}) collective-permute-start(bf16[1024,256]{1,0:T(8,128)(2,1)} %collective-permute-done.6.refs_1_.refs_8_), channel_id=1, source_target_pairs={{0,1},{1,2},{2,3},{3,4},{4,5},{5,6},{6,7},{7,0},{8,15},{9,8},{10,9... | collective-permute-start | bytes 1572872 | tf_op jit(solution)/shard_map/ppermute | solution.py:281
  119.4 22.1 %collective-permute-start.9 = (bf16[1024,256]{1,0:T(8,128)(2,1)}, bf16[1024,256]{1,0:T(8,128)(2,1)S(1)}, u32[]{:S(2)}, u32[]{:S(2)}) collective-permute-start(bf16[1024,256]{1,0:T(8,128)(2,1)} %collective-permute-done.7.refs_2_.refs_9_), channel_id=1, source_target_pairs={{0,1},{1,2},{2,3},{3,4},{4,5},{5,6},{6,7},{7,0},{8,15},{9,8},{10,9... | collective-permute-start | bytes 1572872 | tf_op jit(solution)/shard_map/ppermute | solution.py:281
  134.5 27.2 %all-to-all-start.4 = ((bf16[8,86,256]{2,1,0:T(8,128)(2,1)}), bf16[8,86,256]{2,1,0:T(8,128)(2,1)S(1)}, u32[]{:S(2)}, u32[]{:S(2)}) async-start(bf16[8,86,256]{2,1,0:T(8,128)(2,1)} %broadcast_in_dim.10), calls=%async_computation.4 | async-start | bytes 720896 | tf_op jit(solution)/shard_map/all_to_all | solution.py:18
  138.8 32.3 %copy-start.10 = (bf16[1024,256]{1,0:T(8,128)(2,1)}, bf16[1024,256]{1,0:T(8,128)(2,1)S(1)}, u32[]{:S(2)}) copy-start(bf16[1024,256]{1,0:T(8,128)(2,1)S(1)} %collective-permute-done.8.refs_10_) | copy-start | bytes 1572868
  138.8 16.3 %collective-permute-start.10 = (bf16[1024,256]{1,0:T(8,128)(2,1)S(1)}, bf16[1024,256]{1,0:T(8,128)(2,1)}, u32[]{:S(2)}, u32[]{:S(2)}) collective-permute-start(bf16[1024,256]{1,0:T(8,128)(2,1)S(1)} %collective-permute-done.8.refs_10_), channel_id=1, source_target_pairs={{0,1},{1,2},{2,3},{3,4},{4,5},{5,6},{6,7},{7,0},{8,15},{9,8},{10,9... | collective-permute-start | bytes 1572872 | tf_op jit(solution)/shard_map/ppermute | solution.py:281
  141.6 35.3 %copy-start.11 = (bf16[1024,256]{1,0:T(8,128)(2,1)}, bf16[1024,256]{1,0:T(8,128)(2,1)S(1)}, u32[]{:S(2)}) copy-start(bf16[1024,256]{1,0:T(8,128)(2,1)S(1)} %collective-permute-done.9.refs_11_) | copy-start | bytes 1572868
  141.6 19.2 %collective-permute-start.11 = (bf16[1024,256]{1,0:T(8,128)(2,1)S(1)}, bf16[1024,256]{1,0:T(8,128)(2,1)}, u32[]{:S(2)}, u32[]{:S(2)}) collective-permute-start(bf16[1024,256]{1,0:T(8,128)(2,1)S(1)} %collective-permute-done.9.refs_11_), channel_id=1, source_target_pairs={{0,1},{1,2},{2,3},{3,4},{4,5},{5,6},{6,7},{7,0},{8,15},{9,8},{10,9... | collective-permute-start | bytes 1572872 | tf_op jit(solution)/shard_map/ppermute | solution.py:281
  155.1 21.7 %collective-permute-start.12 = (bf16[1024,256]{1,0:T(8,128)(2,1)}, bf16[1024,256]{1,0:T(8,128)(2,1)}, u32[]{:S(2)}, u32[]{:S(2)}) collective-permute-start(bf16[1024,256]{1,0:T(8,128)(2,1)} %collective-permute-done.10.refs_12_), channel_id=1, source_target_pairs={{0,1},{1,2},{2,3},{3,4},{4,5},{5,6},{6,7},{7,0},{8,15},{9,8},{10,9... | collective-permute-start | bytes 1572872 | tf_op jit(solution)/shard_map/ppermute | solution.py:281
  160.8 16.1 %collective-permute-start.13 = (bf16[1024,256]{1,0:T(8,128)(2,1)}, bf16[1024,256]{1,0:T(8,128)(2,1)}, u32[]{:S(2)}, u32[]{:S(2)}) collective-permute-start(bf16[1024,256]{1,0:T(8,128)(2,1)} %collective-permute-done.11.refs_13_), channel_id=1, source_target_pairs={{0,1},{1,2},{2,3},{3,4},{4,5},{5,6},{6,7},{7,0},{8,15},{9,8},{10,9... | collective-permute-start | bytes 1572872 | tf_op jit(solution)/shard_map/ppermute | solution.py:281
  171.1 15.8 %all-to-all-start.5 = ((bf16[32,64,128]{2,1,0:T(8,128)(2,1)}), bf16[32,64,128]{2,1,0:T(8,128)(2,1)S(1)}, u32[]{:S(2)}, u32[]{:S(2)}) async-start(bf16[32,64,128]{2,1,0:T(8,128)(2,1)} %get-tuple-element.12), calls=%async_computation.5 | async-start | bytes 1048576 | tf_op jit(solution)/shard_map/all_to_all | solution.py:22
  189.5 24.1 %all-to-all-start.6 = ((bf16[32,64,256]{2,1,0:T(8,128)(2,1)}), bf16[32,64,256]{2,1,0:T(8,128)(2,1)S(1)}, u32[]{:S(2)}, u32[]{:S(2)}) async-start(bf16[32,64,256]{2,1,0:T(8,128)(2,1)} %undone_copies.1), calls=%async_computation.6 | async-start | bytes 2097152 | tf_op jit(solution)/shard_map/all_to_all | solution.py:22
  (3 other events, 17.3 us)
Sparse Core Ops, SparseCore 0:
  27.6 56.1 all-gather.1

commit v6 on v5

--- a/solution.py
+++ b/solution.py
@@ -179,7 +179,7 @@
             pl.BlockSpec((each, narrow, 2 * narrow), lambda i: (i, 0, 0)),
         ],
         scratch_shapes=[pltpu.VMEM((dim, narrow), BF16)],
-        compiler_params=params(),
+        compiler_params=params(SMALL),
         cost_estimate=cost(2 * dim * dim * narrow, 2 * dim * dim),
         name="rotated_cols",
     )(basis_t, shared, spread)
@@ -256,10 +256,32 @@
             in_specs=[full(told.shape), full(whiten.shape)] + [part(width)] * len(flat),
             out_specs=[part(dim), part(width)],
         ),
-        compiler_params=params(),
+        compiler_params=params(SMALL),
         cost_estimate=cost(2 * n * dim * width, 6 * n * dim),
         name="first_product",
     )(places, told, whiten, *flat)
+
+
+def last_product(turned, undone, running):
+    n, dim = turned.shape
+    width = undone.shape[1]
+    rows = 256
+
+    def body(turned_ref, undone_ref, running_ref, out_ref):
+        value = running_ref[...] + product(turned_ref[...], undone_ref[...])
+        out_ref[...] = value.astype(BF16)
+
+    part = lambda cols: pl.BlockSpec((rows, cols), lambda i: (i, 0))
+    return pl.pallas_call(
+        body,
+        out_shape=jax.ShapeDtypeStruct((n, width), BF16),
+        grid=(n // rows,),
+        in_specs=[part(dim), pl.BlockSpec((dim, width), lambda i: (0, 0)), part(width)],
+        out_specs=part(width),
+        compiler_params=params(SMALL),
+        cost_estimate=cost(2 * n * dim * width, 2 * n * dim + 2 * dim * width),
+        name="last_product",
+    )(turned, undone, running)
 
 
 def local(features, grad_out, eigvecs, eigvals, whiten):
@@ -282,7 +304,8 @@
 
     blocks = [(grad_out, features)]
     for _ in range(1, planes):
-        blocks.append(tuple(pass_on(b) for b in blocks[-1]))
+        grads = pass_on(blocks[-1][0])
+        blocks.append((grads, pass_on(blocks[-1][1])))
 
     sums = jnp.stack([jnp.sum(a, axis=0, dtype=F32) for a in (features, grad_out)])
     all_sums = copy_for_each(sums, "rows")
@@ -327,7 +350,7 @@
     told = jnp.sum(told, axis=1).reshape(2 * planes, width)
     centered, running = first_product(places, told, whiten, blocks)
     turned = (contract_last(centered, basis_t) * (1.0 / total)).astype(BF16)
-    return (running + product(lax.optimization_barrier(turned), undone)).astype(BF16)
+    return last_product(turned, undone, running)
 
 
 def solution(mesh):

time: 226 us -> 234 us (1.035)
  local copies, waits for them, and re-layouts: 7.37 us -> 25.2 us
  Pallas kernels: 28.2 us -> 23.8 us
  matrix products: 18 us -> 14.6 us
    unnamed x30 -> x66, local copies, waits for them, and re-layouts: 3.14 us -> 21.5 us
    pallas_call x1, Pallas kernels: 8.64 us -> 3.7 us  [rotated_cols(): pl.pallas_call(body, out_shape=[jax.ShapeDtypeStruct((dim, narrow), F32),...]
    dot_general x1 -> x0, matrix products: 3.44 us -> none  [product(): return jnp.dot(a, b, preferred_element_type=F32)]
    pallas_call x1, Pallas kernels: 8.32 us -> 5.25 us  [first_product(): pl.pallas_call(body, out_shape=[jax.ShapeDtypeStruct((n, dim), BF16), jax...]
    pallas_call x0 -> x1, Pallas kernels: none -> 2.64 us  [last_product(): pl.pallas_call(body, out_shape=jax.ShapeDtypeStruct((n, width), BF16), gr...]
  transfers between devices with their start and end apart: 21 -> 21, of which waited for: 12 -> 11; matrix products, arithmetic and copies ran while one was open for 13% -> 11% of each run, Pallas kernels for 11% -> 8%
where the time goes in v6:
time: 234 us; the launch traced here: 232 us
  waiting for transfers between devices  73.5 us (31%)
  starting transfers between devices  55.2 us (24%)
  local copies, waits for them, and re-layouts  25.2 us (11%)
  Pallas kernels  23.8 us (10%)
  blocking collectives  19.3 us (8%)
  matrix products  14.6 us (6%)
  between operations  13.8 us (6%)
  other arithmetic  6.91 us (3%)
    ppermute x14, waiting for transfers between devices, pass_on(): return lax.ppermute(value, ('rows', 'feat'), pairs)  44.3 us
    all_to_all x4, waiting for transfers between devices, exchange(): return lax.all_to_all(parts, axis, split_axis=0, concat_axis=0, tiled=True)  29.2 us
    all_to_all x4, starting transfers between devices, exchange(): return lax.all_to_all(parts, axis, split_axis=0, concat_axis=0, tiled=True)  23.8 us
    unnamed x66, local copies, waits for them, and re-layouts  21.5 us
    all_to_all x1, blocking collectives, copy_for_each(): return lax.all_to_all(copies, axis, split_axis=0, concat_axis=0, tiled=True)  19.3 us
    ppermute x14, starting transfers between devices, pass_on(): return lax.ppermute(value, ('rows', 'feat'), pairs)  16.5 us
    all_to_all x2, starting transfers between devices, copy_for_each(): return lax.all_to_all(copies, axis, split_axis=0, concat_axis=0, tiled=True)  14.9 us
    dot_general x2, matrix products, contract_last(): lax.dot_general(a, b, (((1,), (1,)), ((), ())), preferred_element_type=F32)  14.4 us
  transfers between devices with their start and end apart: 21, of which 11 were waited for; matrix products, arithmetic and copies ran while one was open for 11% of the time, Pallas kernels for 8%

profile of v6, /device:TPU:1, one launch (start us, length us, event | category | flops | bytes accessed | tf_op | source)
XLA Modules:
  0.0 232.4 jit_solution(2478358247614900553)
XLA Ops:
  7.5 19.3 %all_to_all.35 = bf16[8,64,256]{2,1,0:T(8,128)(2,1)S(1)} all-to-all(bf16[8,64,256]{2,1,0:T(8,128)(2,1)S(1)} %broadcast_in_dim.8), channel_id=1, replica_groups=mesh['rows'=32,'feat'=8] {'feat'}, dimensions={0} | all-to-all | bytes 524288 | tf_op jit(solution)/shard_map/all_to_all | solution.py:18
  29.2 6.9 %collective-permute-done.refs_3_.refs_2_ = bf16[1024,256]{1,0:T(8,128)(2,1)S(1)} collective-permute-done((bf16[1024,256]{1,0:T(8,128)(2,1)}, bf16[1024,256]{1,0:T(8,128)(2,1)S(1)}, u32[]{:S(2)}, u32[]{:S(2)}) %collective-permute-start) | collective-permute-done | bytes 524320 | tf_op jit(solution)/shard_map/ppermute | solution.py:303
  37.1 4.8 %collective-permute-done.1.refs_4_.refs_3_ = bf16[1024,256]{1,0:T(8,128)(2,1)S(1)} collective-permute-done((bf16[1024,256]{1,0:T(8,128)(2,1)}, bf16[1024,256]{1,0:T(8,128)(2,1)S(1)}, u32[]{:S(2)}, u32[]{:S(2)}) %collective-permute-start.1) | collective-permute-done | bytes 524320 | tf_op jit(solution)/shard_map/ppermute | solution.py:303
  42.7 4.8 %collective-permute-done.2.refs_5_.refs_4_ = bf16[1024,256]{1,0:T(8,128)(2,1)S(1)} collective-permute-done((bf16[1024,256]{1,0:T(8,128)(2,1)S(1)}, bf16[1024,256]{1,0:T(8,128)(2,1)S(1)}, u32[]{:S(2)}, u32[]{:S(2)}) %collective-permute-start.2) | collective-permute-done | bytes 524320 | tf_op jit(solution)/shard_map/ppermute | solution.py:303
  48.3 4.7 %collective-permute-done.3.refs_6_.refs_5_ = bf16[1024,256]{1,0:T(8,128)(2,1)S(1)} collective-permute-done((bf16[1024,256]{1,0:T(8,128)(2,1)S(1)}, bf16[1024,256]{1,0:T(8,128)(2,1)S(1)}, u32[]{:S(2)}, u32[]{:S(2)}) %collective-permute-start.3) | collective-permute-done | bytes 524320 | tf_op jit(solution)/shard_map/ppermute | solution.py:303
  55.5 3.1 %collective-permute-done.4.refs_7_.refs_6_ = bf16[1024,256]{1,0:T(8,128)(2,1)S(1)} collective-permute-done((bf16[1024,256]{1,0:T(8,128)(2,1)S(1)}, bf16[1024,256]{1,0:T(8,128)(2,1)S(1)}, u32[]{:S(2)}, u32[]{:S(2)}) %collective-permute-start.4) | collective-permute-done | bytes 524320 | tf_op jit(solution)/shard_map/ppermute | solution.py:303
  59.5 4.8 %collective-permute-done.5.refs_8_.refs_7_ = bf16[1024,256]{1,0:T(8,128)(2,1)} collective-permute-done((bf16[1024,256]{1,0:T(8,128)(2,1)S(1)}, bf16[1024,256]{1,0:T(8,128)(2,1)}, u32[]{:S(2)}, u32[]{:S(2)}) %collective-permute-start.5) | collective-permute-done | bytes 524320 | tf_op jit(solution)/shard_map/ppermute | solution.py:303
  67.1 10.6 %all-to-all-start.3 = ((f32[32,2,256]{2,1,0:T(2,128)}), f32[32,2,256]{2,1,0:T(2,128)S(1)}, u32[]{:S(2)}, u32[]{:S(2)}) async-start(f32[32,2,256]{2,1,0:T(2,128)} %broadcast_in_dim.9), calls=%async_computation.3 | async-start | bytes 131072 | tf_op jit(solution)/shard_map/all_to_all | solution.py:18
  77.7 2.1 copy.20
  80.8 2.3 pad_maximum_fusion.refs_0_
  83.1 4.5 %gram_first.1.partial_ref = bf16[256,1280]{1,0:T(8,128)(2,1)} custom-call(bf16[256,2048]{1,0:T(8,128)(2,1)} %pad_maximum_fusion.refs_0_, bf16[1024,256]{1,0:T(8,128)(2,1)} %refs_0_.1, bf16[1024,256]{1,0:T(8,128)(2,1)} %refs_1_.3, bf16[1024,256]{1,0:T(8,128)(2,1)} %copy-done.5, bf16[1024,256]{1,0:T(8,128)(2,1)} %copy-done.7, bf16[1024,256]{1,0:T(8,128)(2,1)} %copy-done.9, ...), custom_call_target="tpu_custom_call" | custom-call | flops 1073741824 | bytes 5242880 | tf_op jit(solution)/shard_map/gram_first/pallas_call | solution.py:83
  87.6 2.7 %gram_last.1 = bf16[256,1280]{1,0:T(8,128)(2,1)} custom-call(bf16[256,1280]{1,0:T(8,128)(2,1)} %gram_first.1.partial_ref, bf16[256,2048]{1,0:T(8,128)(2,1)} %pad_maximum_fusion.refs_0_, bf16[1024,256]{1,0:T(8,128)(2,1)} %collective-permute-done.6.refs_1_.refs_8_, bf16[1024,256]{1,0:T(8,128)(2,1)} %collective-permute-done.7.refs_2_.refs_9_), custom_call_target="tpu_custom_call", output_to_operand_aliasing={{}: (0, {})} | custom-call | flops 268435456 | bytes 2097152 | tf_op jit(solution)/shard_map/gram_last/pallas_call | solution.py:101
  90.3 7.4 %all-to-all-start.1 = ((bf16[32,8,1280]{2,1,0:T(8,128)(2,1)}), bf16[32,8,1280]{2,1,0:T(8,128)(2,1)S(1)}, u32[]{:S(2)}, u32[]{:S(2)}) async-start(bf16[32,8,1280]{2,1,0:T(8,128)(2,1)} %bitcast.23), calls=%async_computation.1 | async-start | bytes 1310720 | tf_op jit(solution)/shard_map/all_to_all | solution.py:22
  97.9 12.7 %all-to-all-done.1.got_ref = bf16[32,8,1280]{2,1,0:T(8,128)(2,1)S(1)} async-done(((bf16[32,8,1280]{2,1,0:T(8,128)(2,1)}), bf16[32,8,1280]{2,1,0:T(8,128)(2,1)S(1)}, u32[]{:S(2)}, u32[]{:S(2)}) %all-to-all-start.1) | async-done | bytes 655392 | tf_op jit(solution)/shard_map/all_to_all | solution.py:22
  111.9 4.1 %all-to-all-start.2 = ((bf16[32,8,2048]{2,1,0:T(8,128)(2,1)}), bf16[32,8,2048]{2,1,0:T(8,128)(2,1)S(1)}, u32[]{:S(2)}, u32[]{:S(2)}) async-start(bf16[32,8,2048]{2,1,0:T(8,128)(2,1)} %gathered_sum.1), calls=%async_computation.2 | async-start | bytes 2097152 | tf_op jit(solution)/shard_map/all_to_all | solution.py:22
  116.2 3.1 %collective-permute-start.8 = (bf16[1024,256]{1,0:T(8,128)(2,1)}, bf16[1024,256]{1,0:T(8,128)(2,1)S(1)}, u32[]{:S(2)}, u32[]{:S(2)}) collective-permute-start(bf16[1024,256]{1,0:T(8,128)(2,1)} %collective-permute-done.6.refs_1_.refs_8_), channel_id=1, source_target_pairs={{0,1},{1,2},{2,3},{3,4},{4,5},{5,6},{6,7},{7,0},{8,15},{9,8},{10,9... | collective-permute-start | bytes 1572872 | tf_op jit(solution)/shard_map/ppermute | solution.py:303
  119.6 13.5 %all-to-all-done.2 = bf16[32,8,2048]{2,1,0:T(8,128)(2,1)S(1)} async-done(((bf16[32,8,2048]{2,1,0:T(8,128)(2,1)}), bf16[32,8,2048]{2,1,0:T(8,128)(2,1)S(1)}, u32[]{:S(2)}, u32[]{:S(2)}) %all-to-all-start.2) | async-done | bytes 1048608 | tf_op jit(solution)/shard_map/all_to_all | solution.py:22
  134.3 4.3 %all-to-all-start.4 = ((bf16[8,86,256]{2,1,0:T(8,128)(2,1)}), bf16[8,86,256]{2,1,0:T(8,128)(2,1)S(1)}, u32[]{:S(2)}, u32[]{:S(2)}) async-start(bf16[8,86,256]{2,1,0:T(8,128)(2,1)} %broadcast_in_dim.10), calls=%async_computation.4 | async-start | bytes 720896 | tf_op jit(solution)/shard_map/all_to_all | solution.py:18
  138.7 2.7 %collective-permute-start.10 = (bf16[1024,256]{1,0:T(8,128)(2,1)S(1)}, bf16[1024,256]{1,0:T(8,128)(2,1)}, u32[]{:S(2)}, u32[]{:S(2)}) collective-permute-start(bf16[1024,256]{1,0:T(8,128)(2,1)S(1)} %collective-permute-done.8.refs_10_), channel_id=1, source_target_pairs={{0,1},{1,2},{2,3},{3,4},{4,5},{5,6},{6,7},{7,0},{8,15},{9,8},{10,9... | collective-permute-start | bytes 1572872 | tf_op jit(solution)/shard_map/ppermute | solution.py:303
  144.5 10.5 %collective-permute-done.10.refs_12_ = bf16[1024,256]{1,0:T(8,128)(2,1)} collective-permute-done((bf16[1024,256]{1,0:T(8,128)(2,1)S(1)}, bf16[1024,256]{1,0:T(8,128)(2,1)}, u32[]{:S(2)}, u32[]{:S(2)}) %collective-permute-start.10) | collective-permute-done | bytes 524320 | tf_op jit(solution)/shard_map/ppermute | solution.py:303
  155.9 4.7 %collective-permute-done.11.refs_13_ = bf16[1024,256]{1,0:T(8,128)(2,1)} collective-permute-done((bf16[1024,256]{1,0:T(8,128)(2,1)S(1)}, bf16[1024,256]{1,0:T(8,128)(2,1)}, u32[]{:S(2)}, u32[]{:S(2)}) %collective-permute-start.11) | collective-permute-done | bytes 524320 | tf_op jit(solution)/shard_map/ppermute | solution.py:303
  162.2 3.4 %copy-done = bf16[2048,2048]{1,0:T(8,128)(2,1)S(1)} copy-done((bf16[2048,2048]{1,0:T(8,128)(2,1)S(1)}, bf16[2048,2048]{1,0:T(8,128)(2,1)}, u32[]{:S(2)}) %copy-start) | copy-done | bytes 8388632
  165.6 3.7 %rotated_cols.1 = (f32[2048,64]{1,0:T(8,128)S(1)}, bf16[32,64,128]{2,1,0:T(8,128)(2,1)S(1)}) custom-call(bf16[2048,2048]{1,0:T(8,128)(2,1)S(1)} %copy-done, bf16[8,86,256]{2,1,0:T(8,128)(2,1)S(1)} %all-to-all-done.4.shared_ref, bf16[64,64]{1,0:T(8,128)(2,1)S(1)} %fusion.8.spread_ref), custom_call_target="tpu_custom_call" | custom-call | flops 536870912 | bytes 8388608 | tf_op jit(solution)/shard_map/rotated_cols/pallas_call | solution.py:165
  171.1 4.9 %all-to-all-start.5 = ((bf16[32,64,128]{2,1,0:T(8,128)(2,1)}), bf16[32,64,128]{2,1,0:T(8,128)(2,1)}, u32[]{:S(2)}, u32[]{:S(2)}) async-start(bf16[32,64,128]{2,1,0:T(8,128)(2,1)} %copy-done.25), calls=%async_computation.5 | async-start | bytes 1048576 | tf_op jit(solution)/shard_map/all_to_all | solution.py:22
  180.6 5.3 %first_product.1 = (bf16[1024,2048]{1,0:T(8,128)(2,1)S(1)}, f32[1024,256]{1,0:T(8,128)S(1)}) custom-call(s32[8]{0:T(128)S(1)} %and_select_fusion.place_ref, f32[16,256]{1,0:T(8,128)S(1)} %reshape.44.told_ref, bf16[2048,256]{1,0:T(8,128)(2,1)S(1)} %copy-done.16, bf16[1024,256]{1,0:T(8,128)(2,1)S(1)} %copy-done.1, bf16[1024,256]{1,0:T(8,128)(2,1)S(1)} %copy-done.3, ...), custom_call_target="tpu_custom_call" | custom-call | flops 1073741824 | bytes 12582912 | tf_op jit(solution)/shard_map/first_product/pallas_call | solution.py:247
  186.8 2.0 copy-done.26
  192.5 3.7 %undone_copies.1 = bf16[32,64,256]{2,1,0:T(8,128)(2,1)} custom-call(f32[2048,64]{1,0:T(8,128)S(1)} %copy-done.18, bf16[32,64,128]{2,1,0:T(8,128)(2,1)} %all-to-all-done.5.back_ref, f32[64,64]{1,0:T(8,128)S(1)} %pad_maximum_fusion.1.spread_ref, f32[64,2048]{1,0:T(8,128)S(1)} %copy-done.15, bf16[2048,256]{1,0:T(8,128)(2,1)S(1)} %constant_dynamic-slice_fusion.basis_ref), custom_call_target="tpu_custom_call" | custom-call | flops 134217728 | bytes 2097152 | tf_op jit(solution)/shard_map/undone_copies/pallas_call | solution.py:215
  196.2 7.5 %all-to-all-start.6 = ((bf16[32,64,256]{2,1,0:T(8,128)(2,1)}), bf16[32,64,256]{2,1,0:T(8,128)(2,1)S(1)}, u32[]{:S(2)}, u32[]{:S(2)}) async-start(bf16[32,64,256]{2,1,0:T(8,128)(2,1)} %undone_copies.1), calls=%async_computation.6 | async-start | bytes 2097152 | tf_op jit(solution)/shard_map/all_to_all | solution.py:22
  203.7 14.0 %multiply_convert_fusion.turned_ref = bf16[1024,2048]{1,0:T(8,128)(2,1)} fusion(bf16[1024,2048]{1,0:T(8,128)(2,1)} %copy-done.26, bf16[2048,2048]{1,0:T(8,128)(2,1)} %all-gather.2.cloned.1.call-done.basis_ref), kind=kOutput, calls=%fused_computation | convolution fusion | flops 8594128896 | bytes 16777216 | tf_op jit(solution)/shard_map/dot_general | solution.py:26
  217.7 3.0 %all-to-all-done.6 = bf16[32,64,256]{2,1,0:T(8,128)(2,1)S(1)} async-done(((bf16[32,64,256]{2,1,0:T(8,128)(2,1)}), bf16[32,64,256]{2,1,0:T(8,128)(2,1)S(1)}, u32[]{:S(2)}, u32[]{:S(2)}) %all-to-all-start.6) | async-done | bytes 1048608 | tf_op jit(solution)/shard_map/all_to_all | solution.py:22
  220.7 2.2 copy-done.4
  222.9 2.6 %last_product.1 = bf16[1024,256]{1,0:T(8,128)(2,1)} custom-call(bf16[1024,2048]{1,0:T(8,128)(2,1)S(1)} %copy-done.4, bf16[2048,256]{1,0:T(8,128)(2,1)S(1)} %bitcast.22, f32[1024,256]{1,0:T(8,128)S(1)} %copy-done.20), custom_call_target="tpu_custom_call" | custom-call | flops 1073741824 | bytes 5242880 | tf_op jit(solution)/shard_map/last_product/pallas_call | solution.py:275
  (119 shorter events, 32.8 us)
Async XLA Ops:
  6.5 73.2 %copy-start.2 = (bf16[1024,256]{1,0:T(8,128)(2,1)S(1)}, bf16[1024,256]{1,0:T(8,128)(2,1)}, u32[]{:S(2)}) copy-start(bf16[1024,256]{1,0:T(8,128)(2,1)} %refs_1_.3) | copy-start | bytes 1572868
  6.5 155.7 %all-gather.2.cloned.1.call-start = ((), (), s32[]{:S(2)}) async-start(), calls=%async_computation.7 | async-start | bytes 8650752 | tf_op jit(solution)/shard_map/all_gather | solution.py:321
  27.5 8.6 %collective-permute-start = (bf16[1024,256]{1,0:T(8,128)(2,1)}, bf16[1024,256]{1,0:T(8,128)(2,1)S(1)}, u32[]{:S(2)}, u32[]{:S(2)}) collective-permute-start(bf16[1024,256]{1,0:T(8,128)(2,1)} %refs_0_.1), channel_id=1, source_target_pairs={{0,1},{1,2},{2,3},{3,4},{4,5},{5,6},{6,7},{7,0},{8,15},{9,8},{10,9... | collective-permute-start | bytes 1572872 | tf_op jit(solution)/shard_map/ppermute | solution.py:303
  27.6 14.2 %collective-permute-start.1 = (bf16[1024,256]{1,0:T(8,128)(2,1)}, bf16[1024,256]{1,0:T(8,128)(2,1)S(1)}, u32[]{:S(2)}, u32[]{:S(2)}) collective-permute-start(bf16[1024,256]{1,0:T(8,128)(2,1)} %refs_1_.3), channel_id=1, source_target_pairs={{0,1},{1,2},{2,3},{3,4},{4,5},{5,6},{6,7},{7,0},{8,15},{9,8},{10,9... | collective-permute-start | bytes 1572872 | tf_op jit(solution)/shard_map/ppermute | solution.py:303
  36.1 46.9 %copy-start.5 = (bf16[1024,256]{1,0:T(8,128)(2,1)}, bf16[1024,256]{1,0:T(8,128)(2,1)S(1)}, u32[]{:S(2)}) copy-start(bf16[1024,256]{1,0:T(8,128)(2,1)S(1)} %collective-permute-done.refs_3_.refs_2_) | copy-start | bytes 1572868
  36.1 11.3 %collective-permute-start.2 = (bf16[1024,256]{1,0:T(8,128)(2,1)S(1)}, bf16[1024,256]{1,0:T(8,128)(2,1)S(1)}, u32[]{:S(2)}, u32[]{:S(2)}) collective-permute-start(bf16[1024,256]{1,0:T(8,128)(2,1)S(1)} %collective-permute-done.refs_3_.refs_2_), channel_id=1, source_target_pairs={{0,1},{1,2},{2,3},{3,4},{4,5},{5,6},{6,7},{7,0},{8,15},{9,8},{10,9... | collective-permute-start | bytes 1572872 | tf_op jit(solution)/shard_map/ppermute | solution.py:303
  41.9 41.2 %copy-start.7 = (bf16[1024,256]{1,0:T(8,128)(2,1)}, bf16[1024,256]{1,0:T(8,128)(2,1)S(1)}, u32[]{:S(2)}) copy-start(bf16[1024,256]{1,0:T(8,128)(2,1)S(1)} %collective-permute-done.1.refs_4_.refs_3_) | copy-start | bytes 1572868
  41.9 11.1 %collective-permute-start.3 = (bf16[1024,256]{1,0:T(8,128)(2,1)S(1)}, bf16[1024,256]{1,0:T(8,128)(2,1)S(1)}, u32[]{:S(2)}, u32[]{:S(2)}) collective-permute-start(bf16[1024,256]{1,0:T(8,128)(2,1)S(1)} %collective-permute-done.1.refs_4_.refs_3_), channel_id=1, source_target_pairs={{0,1},{1,2},{2,3},{3,4},{4,5},{5,6},{6,7},{7,0},{8,15},{9,8},{10,9... | collective-permute-start | bytes 1572872 | tf_op jit(solution)/shard_map/ppermute | solution.py:303
  47.5 35.6 %copy-start.9 = (bf16[1024,256]{1,0:T(8,128)(2,1)}, bf16[1024,256]{1,0:T(8,128)(2,1)S(1)}, u32[]{:S(2)}) copy-start(bf16[1024,256]{1,0:T(8,128)(2,1)S(1)} %collective-permute-done.2.refs_5_.refs_4_) | copy-start | bytes 1572868
  47.5 11.1 %collective-permute-start.4 = (bf16[1024,256]{1,0:T(8,128)(2,1)S(1)}, bf16[1024,256]{1,0:T(8,128)(2,1)S(1)}, u32[]{:S(2)}, u32[]{:S(2)}) collective-permute-start(bf16[1024,256]{1,0:T(8,128)(2,1)S(1)} %collective-permute-done.2.refs_5_.refs_4_), channel_id=1, source_target_pairs={{0,1},{1,2},{2,3},{3,4},{4,5},{5,6},{6,7},{7,0},{8,15},{9,8},{10,9... | collective-permute-start | bytes 1572872 | tf_op jit(solution)/shard_map/ppermute | solution.py:303
  53.0 30.1 %copy-start.11 = (bf16[1024,256]{1,0:T(8,128)(2,1)}, bf16[1024,256]{1,0:T(8,128)(2,1)S(1)}, u32[]{:S(2)}) copy-start(bf16[1024,256]{1,0:T(8,128)(2,1)S(1)} %collective-permute-done.3.refs_6_.refs_5_) | copy-start | bytes 1572868
  53.0 11.3 %collective-permute-start.5 = (bf16[1024,256]{1,0:T(8,128)(2,1)S(1)}, bf16[1024,256]{1,0:T(8,128)(2,1)}, u32[]{:S(2)}, u32[]{:S(2)}) collective-permute-start(bf16[1024,256]{1,0:T(8,128)(2,1)S(1)} %collective-permute-done.3.refs_6_.refs_5_), channel_id=1, source_target_pairs={{0,1},{1,2},{2,3},{3,4},{4,5},{5,6},{6,7},{7,0},{8,15},{9,8},{10,9... | collective-permute-start | bytes 1572872 | tf_op jit(solution)/shard_map/ppermute | solution.py:303
  58.6 24.5 %copy-start.13 = (bf16[1024,256]{1,0:T(8,128)(2,1)}, bf16[1024,256]{1,0:T(8,128)(2,1)S(1)}, u32[]{:S(2)}) copy-start(bf16[1024,256]{1,0:T(8,128)(2,1)S(1)} %collective-permute-done.4.refs_7_.refs_6_) | copy-start | bytes 1572868
  58.6 29.0 %collective-permute-start.6 = (bf16[1024,256]{1,0:T(8,128)(2,1)S(1)}, bf16[1024,256]{1,0:T(8,128)(2,1)}, u32[]{:S(2)}, u32[]{:S(2)}) collective-permute-start(bf16[1024,256]{1,0:T(8,128)(2,1)S(1)} %collective-permute-done.4.refs_7_.refs_6_), channel_id=1, source_target_pairs={{0,1},{1,2},{2,3},{3,4},{4,5},{5,6},{6,7},{7,0},{8,15},{9,8},{10,9... | collective-permute-start | bytes 1572872 | tf_op jit(solution)/shard_map/ppermute | solution.py:303
  64.3 23.3 %collective-permute-start.7 = (bf16[1024,256]{1,0:T(8,128)(2,1)}, bf16[1024,256]{1,0:T(8,128)(2,1)}, u32[]{:S(2)}, u32[]{:S(2)}) collective-permute-start(bf16[1024,256]{1,0:T(8,128)(2,1)} %collective-permute-done.5.refs_8_.refs_7_), channel_id=1, source_target_pairs={{0,1},{1,2},{2,3},{3,4},{4,5},{5,6},{6,7},{7,0},{8,15},{9,8},{10,9... | collective-permute-start | bytes 1572872 | tf_op jit(solution)/shard_map/ppermute | solution.py:303
  67.1 23.2 %all-to-all-start.3 = ((f32[32,2,256]{2,1,0:T(2,128)}), f32[32,2,256]{2,1,0:T(2,128)S(1)}, u32[]{:S(2)}, u32[]{:S(2)}) async-start(f32[32,2,256]{2,1,0:T(2,128)} %broadcast_in_dim.9), calls=%async_computation.3 | async-start | bytes 131072 | tf_op jit(solution)/shard_map/all_to_all | solution.py:18
  83.1 14.7 %copy-start.31 = (f32[2048]{0:T(1024)S(1)}, f32[2048]{0:T(1024)}, u32[]{:S(2)}) copy-start(f32[2048]{0:T(1024)} %param.8) | copy-start | bytes 24580
  87.6 28.4 %copy-start.28 = (f32[256,64]{0,1:T(8,128)S(1)}, f32[256,64]{0,1:T(8,128)}, u32[]{:S(2)}) copy-start(f32[256,64]{0,1:T(8,128)} %param.7) | copy-start | bytes 196612
  87.6 45.5 %copy-start.27 = (bf16[8,8,8,256]{3,2,0,1:T(8,128)(2,1)S(1)}, bf16[8,8,8,256]{3,2,0,1:T(8,128)(2,1)}, u32[]{:S(2)}) copy-start(bf16[8,8,8,256]{3,2,0,1:T(8,128)(2,1)} %copy.24) | copy-start | bytes 786436
  90.3 20.2 %all-to-all-start.1 = ((bf16[32,8,1280]{2,1,0:T(8,128)(2,1)}), bf16[32,8,1280]{2,1,0:T(8,128)(2,1)S(1)}, u32[]{:S(2)}, u32[]{:S(2)}) async-start(bf16[32,8,1280]{2,1,0:T(8,128)(2,1)} %bitcast.23), calls=%async_computation.1 | async-start | bytes 1310720 | tf_op jit(solution)/shard_map/all_to_all | solution.py:22
  111.9 21.2 %all-to-all-start.2 = ((bf16[32,8,2048]{2,1,0:T(8,128)(2,1)}), bf16[32,8,2048]{2,1,0:T(8,128)(2,1)S(1)}, u32[]{:S(2)}, u32[]{:S(2)}) async-start(bf16[32,8,2048]{2,1,0:T(8,128)(2,1)} %gathered_sum.1), calls=%async_computation.2 | async-start | bytes 2097152 | tf_op jit(solution)/shard_map/all_to_all | solution.py:22
  116.2 22.5 %collective-permute-start.8 = (bf16[1024,256]{1,0:T(8,128)(2,1)}, bf16[1024,256]{1,0:T(8,128)(2,1)S(1)}, u32[]{:S(2)}, u32[]{:S(2)}) collective-permute-start(bf16[1024,256]{1,0:T(8,128)(2,1)} %collective-permute-done.6.refs_1_.refs_8_), channel_id=1, source_target_pairs={{0,1},{1,2},{2,3},{3,4},{4,5},{5,6},{6,7},{7,0},{8,15},{9,8},{10,9... | collective-permute-start | bytes 1572872 | tf_op jit(solution)/shard_map/ppermute | solution.py:303
  119.3 22.1 %collective-permute-start.9 = (bf16[1024,256]{1,0:T(8,128)(2,1)}, bf16[1024,256]{1,0:T(8,128)(2,1)S(1)}, u32[]{:S(2)}, u32[]{:S(2)}) collective-permute-start(bf16[1024,256]{1,0:T(8,128)(2,1)} %collective-permute-done.7.refs_2_.refs_9_), channel_id=1, source_target_pairs={{0,1},{1,2},{2,3},{3,4},{4,5},{5,6},{6,7},{7,0},{8,15},{9,8},{10,9... | collective-permute-start | bytes 1572872 | tf_op jit(solution)/shard_map/ppermute | solution.py:303
  134.3 27.2 %all-to-all-start.4 = ((bf16[8,86,256]{2,1,0:T(8,128)(2,1)}), bf16[8,86,256]{2,1,0:T(8,128)(2,1)S(1)}, u32[]{:S(2)}, u32[]{:S(2)}) async-start(bf16[8,86,256]{2,1,0:T(8,128)(2,1)} %broadcast_in_dim.10), calls=%async_computation.4 | async-start | bytes 720896 | tf_op jit(solution)/shard_map/all_to_all | solution.py:18
  138.7 23.0 %copy-start.21 = (bf16[1024,256]{1,0:T(8,128)(2,1)}, bf16[1024,256]{1,0:T(8,128)(2,1)S(1)}, u32[]{:S(2)}) copy-start(bf16[1024,256]{1,0:T(8,128)(2,1)S(1)} %collective-permute-done.8.refs_10_) | copy-start | bytes 1572868
  138.7 16.3 %collective-permute-start.10 = (bf16[1024,256]{1,0:T(8,128)(2,1)S(1)}, bf16[1024,256]{1,0:T(8,128)(2,1)}, u32[]{:S(2)}, u32[]{:S(2)}) collective-permute-start(bf16[1024,256]{1,0:T(8,128)(2,1)S(1)} %collective-permute-done.8.refs_10_), channel_id=1, source_target_pairs={{0,1},{1,2},{2,3},{3,4},{4,5},{5,6},{6,7},{7,0},{8,15},{9,8},{10,9... | collective-permute-start | bytes 1572872 | tf_op jit(solution)/shard_map/ppermute | solution.py:303
  141.4 19.2 %collective-permute-start.11 = (bf16[1024,256]{1,0:T(8,128)(2,1)S(1)}, bf16[1024,256]{1,0:T(8,128)(2,1)}, u32[]{:S(2)}, u32[]{:S(2)}) collective-permute-start(bf16[1024,256]{1,0:T(8,128)(2,1)S(1)} %collective-permute-done.9.refs_11_), channel_id=1, source_target_pairs={{0,1},{1,2},{2,3},{3,4},{4,5},{5,6},{6,7},{7,0},{8,15},{9,8},{10,9... | collective-permute-start | bytes 1572872 | tf_op jit(solution)/shard_map/ppermute | solution.py:303
  155.0 21.1 %collective-permute-start.12 = (bf16[1024,256]{1,0:T(8,128)(2,1)}, bf16[1024,256]{1,0:T(8,128)(2,1)}, u32[]{:S(2)}, u32[]{:S(2)}) collective-permute-start(bf16[1024,256]{1,0:T(8,128)(2,1)} %collective-permute-done.10.refs_12_), channel_id=1, source_target_pairs={{0,1},{1,2},{2,3},{3,4},{4,5},{5,6},{6,7},{7,0},{8,15},{9,8},{10,9... | collective-permute-start | bytes 1572872 | tf_op jit(solution)/shard_map/ppermute | solution.py:303
  160.6 15.5 %collective-permute-start.13 = (bf16[1024,256]{1,0:T(8,128)(2,1)}, bf16[1024,256]{1,0:T(8,128)(2,1)}, u32[]{:S(2)}, u32[]{:S(2)}) collective-permute-start(bf16[1024,256]{1,0:T(8,128)(2,1)} %collective-permute-done.11.refs_13_), channel_id=1, source_target_pairs={{0,1},{1,2},{2,3},{3,4},{4,5},{5,6},{6,7},{7,0},{8,15},{9,8},{10,9... | collective-permute-start | bytes 1572872 | tf_op jit(solution)/shard_map/ppermute | solution.py:303
  171.1 19.1 %all-to-all-start.5 = ((bf16[32,64,128]{2,1,0:T(8,128)(2,1)}), bf16[32,64,128]{2,1,0:T(8,128)(2,1)}, u32[]{:S(2)}, u32[]{:S(2)}) async-start(bf16[32,64,128]{2,1,0:T(8,128)(2,1)} %copy-done.25), calls=%async_computation.5 | async-start | bytes 1048576 | tf_op jit(solution)/shard_map/all_to_all | solution.py:22
  196.2 24.5 %all-to-all-start.6 = ((bf16[32,64,256]{2,1,0:T(8,128)(2,1)}), bf16[32,64,256]{2,1,0:T(8,128)(2,1)S(1)}, u32[]{:S(2)}, u32[]{:S(2)}) async-start(bf16[32,64,256]{2,1,0:T(8,128)(2,1)} %undone_copies.1), calls=%async_computation.6 | async-start | bytes 2097152 | tf_op jit(solution)/shard_map/all_to_all | solution.py:22
  203.6 17.1 %copy-start.20 = (f32[1024,256]{1,0:T(8,128)S(1)}, f32[1024,256]{1,0:T(8,128)}, u32[]{:S(2)}) copy-start(f32[1024,256]{1,0:T(8,128)} %copy-done.19) | copy-start | bytes 3145732
  (21 other events, 94.6 us)
Sparse Core Ops, SparseCore 0:
  27.6 56.1 all-gather.1

commit v7 on v6

--- a/solution.py
+++ b/solution.py
@@ -147,20 +147,28 @@
 def rotated_cols(basis_t, shared, spread):
     dim, narrow = basis_t.shape[0], spread.shape[0]
     planes, _, width = shared.shape
-    rows = 256
+    steps = 8
+    rows = dim // steps
     each = rows // narrow
 
-    def body(basis_ref, shared_ref, spread_ref, out_ref, low_ref, right_ref):
-        @pl.when(pl.program_id(0) == 0)
-        def _():
-            for p in range(planes):
-                right_ref[p * width : (p + 1) * width, :] = shared_ref[p, :narrow, :].T
-
-        value = product(basis_ref[...], right_ref[...])
-        out_ref[...] = value
-        for k in range(each):
-            piece = value[k * narrow : (k + 1) * narrow].astype(BF16)
-            low_ref[k] = jnp.concatenate([piece, spread_ref[...]], axis=1)
+    def body(basis_ref, shared_ref, spread_ref, out_ref, low_ref, held_ref, right_ref, sems):
+        copies = [
+            pltpu.make_async_copy(
+                basis_ref.at[pl.ds(i * rows, rows), :], held_ref.at[i], sems.at[i]
+            )
+            for i in range(steps)
+        ]
+        for copy in copies:
+            copy.start()
+        for p in range(planes):
+            right_ref[p * width : (p + 1) * width, :] = shared_ref[p, :narrow, :].T
+        for i in range(steps):
+            copies[i].wait()
+            value = product(held_ref[i], right_ref[...])
+            out_ref[i * rows : (i + 1) * rows, :] = value
+            for k in range(each):
+                piece = value[k * narrow : (k + 1) * narrow].astype(BF16)
+                low_ref[i * each + k] = jnp.concatenate([piece, spread_ref[...]], axis=1)
 
     return pl.pallas_call(
         body,
@@ -168,18 +176,14 @@
             jax.ShapeDtypeStruct((dim, narrow), F32),
             jax.ShapeDtypeStruct((dim // narrow, narrow, 2 * narrow), BF16),
         ],
-        grid=(dim // rows,),
-        in_specs=[
-            pl.BlockSpec((rows, dim), lambda i: (i, 0)),
-            pl.BlockSpec(shared.shape, lambda i: (0, 0, 0)),
-            pl.BlockSpec(spread.shape, lambda i: (0, 0)),
+        in_specs=[pl.BlockSpec(memory_space=pl.ANY), VMEM, VMEM],
+        out_specs=[VMEM, VMEM],
+        scratch_shapes=[
+            pltpu.VMEM((steps, rows, dim), BF16),
+            pltpu.VMEM((dim, narrow), BF16),
+            pltpu.SemaphoreType.DMA((steps,)),
         ],
-        out_specs=[
-            pl.BlockSpec((rows, narrow), lambda i: (i, 0)),
-            pl.BlockSpec((each, narrow, 2 * narrow), lambda i: (i, 0, 0)),
-        ],
-        scratch_shapes=[pltpu.VMEM((dim, narrow), BF16)],
-        compiler_params=params(SMALL),
+        compiler_params=params(),
         cost_estimate=cost(2 * dim * dim * narrow, 2 * dim * dim),
         name="rotated_cols",
     )(basis_t, shared, spread)
@@ -217,7 +221,7 @@
         out_shape=jax.ShapeDtypeStruct((groups, narrow, width), BF16),
         in_specs=[VMEM] * 5,
         out_specs=VMEM,
-        compiler_params=params(SMALL),
+        compiler_params=params(),
         cost_estimate=cost(4 * dim * narrow * width, 4 * dim * width),
         name="undone_copies",
     )(rot, back, spread, kernel_t, basis)
@@ -256,7 +260,7 @@
             in_specs=[full(told.shape), full(whiten.shape)] + [part(width)] * len(flat),
             out_specs=[part(dim), part(width)],
         ),
-        compiler_params=params(SMALL),
+        compiler_params=params(),
         cost_estimate=cost(2 * n * dim * width, 6 * n * dim),
         name="first_product",
     )(places, told, whiten, *flat)
@@ -278,7 +282,7 @@
         grid=(n // rows,),
         in_specs=[part(dim), pl.BlockSpec((dim, width), lambda i: (0, 0)), part(width)],
         out_specs=part(width),
-        compiler_params=params(SMALL),
+        compiler_params=params(),
         cost_estimate=cost(2 * n * dim * width, 2 * n * dim + 2 * dim * width),
         name="last_product",
     )(turned, undone, running)

time: 234 us -> 230 us (0.983)
  local copies, waits for them, and re-layouts: 25.2 us -> 10 us
  Pallas kernels: 23.8 us -> 33.3 us
  other arithmetic: 6.91 us -> 9.51 us
    unnamed x66 -> x34, local copies, waits for them, and re-layouts: 21.5 us -> 4.89 us
    pallas_call x1, Pallas kernels: 3.7 us -> 6.87 us  [rotated_cols(): pl.pallas_call(body, out_shape=[jax.ShapeDtypeStruct((dim, narrow), F32),...]
    pallas_call x1, Pallas kernels: 5.25 us -> 8.2 us  [first_product(): pl.pallas_call(body, out_shape=[jax.ShapeDtypeStruct((n, dim), BF16), jax...]
    pallas_call x1, Pallas kernels: 2.64 us -> 5.18 us  [last_product(): pl.pallas_call(body, out_shape=jax.ShapeDtypeStruct((n, width), BF16), gr...]
  transfers between devices with their start and end apart: 21 -> 21, of which waited for: 11 -> 11; matrix products, arithmetic and copies ran while one was open for 11% -> 13% of each run, Pallas kernels for 8% -> 10%
where the time goes in v7:
time: 230 us; the launch traced here: 229 us
  waiting for transfers between devices  73.8 us (32%)
  starting transfers between devices  54.7 us (24%)
  Pallas kernels  33.3 us (14%)
  blocking collectives  19.3 us (8%)
  matrix products  14.6 us (6%)
  between operations  13.7 us (6%)
  local copies, waits for them, and re-layouts  10 us (4%)
  other arithmetic  9.51 us (4%)
    ppermute x14, waiting for transfers between devices, pass_on(): return lax.ppermute(value, ('rows', 'feat'), pairs)  44.5 us
    all_to_all x4, waiting for transfers between devices, exchange(): return lax.all_to_all(parts, axis, split_axis=0, concat_axis=0, tiled=True)  29.2 us
    all_to_all x4, starting transfers between devices, exchange(): return lax.all_to_all(parts, axis, split_axis=0, concat_axis=0, tiled=True)  23.3 us
    all_to_all x1, blocking collectives, copy_for_each(): return lax.all_to_all(copies, axis, split_axis=0, concat_axis=0, tiled=True)  19.3 us
    ppermute x14, starting transfers between devices, pass_on(): return lax.ppermute(value, ('rows', 'feat'), pairs)  16.5 us
    all_to_all x2, starting transfers between devices, copy_for_each(): return lax.all_to_all(copies, axis, split_axis=0, concat_axis=0, tiled=True)  14.9 us
    dot_general x2, matrix products, contract_last(): lax.dot_general(a, b, (((1,), (1,)), ((), ())), preferred_element_type=F32)  14.4 us
    pallas_call x1, Pallas kernels, first_product(): pl.pallas_call(body, out_shape=[jax.ShapeDtypeStruct((n, dim), BF16), jax...  8.2 us
  transfers between devices with their start and end apart: 21, of which 11 were waited for; matrix products, arithmetic and copies ran while one was open for 13% of the time, Pallas kernels for 10%

profile of v7, /device:TPU:1, one launch (start us, length us, event | category | flops | bytes accessed | tf_op | source)
XLA Modules:
  0.0 228.9 jit_solution(306870366301155192)
XLA Ops:
  7.5 19.3 %all_to_all.35 = bf16[8,64,256]{2,1,0:T(8,128)(2,1)S(1)} all-to-all(bf16[8,64,256]{2,1,0:T(8,128)(2,1)S(1)} %broadcast_in_dim.8), channel_id=1, replica_groups=mesh['rows'=32,'feat'=8] {'feat'}, dimensions={0} | all-to-all | bytes 524288 | tf_op jit(solution)/shard_map/all_to_all | solution.py:18
  27.6 1.6 collective-permute-start.1
  29.2 6.9 %collective-permute-done.refs_3_.refs_2_ = bf16[1024,256]{1,0:T(8,128)(2,1)S(1)} collective-permute-done((bf16[1024,256]{1,0:T(8,128)(2,1)}, bf16[1024,256]{1,0:T(8,128)(2,1)S(1)}, u32[]{:S(2)}, u32[]{:S(2)}) %collective-permute-start) | collective-permute-done | bytes 524320 | tf_op jit(solution)/shard_map/ppermute | solution.py:307
  37.0 4.8 %collective-permute-done.1.refs_4_.refs_3_ = bf16[1024,256]{1,0:T(8,128)(2,1)S(1)} collective-permute-done((bf16[1024,256]{1,0:T(8,128)(2,1)}, bf16[1024,256]{1,0:T(8,128)(2,1)S(1)}, u32[]{:S(2)}, u32[]{:S(2)}) %collective-permute-start.1) | collective-permute-done | bytes 524320 | tf_op jit(solution)/shard_map/ppermute | solution.py:307
  42.7 4.8 %collective-permute-done.2.refs_5_.refs_4_ = bf16[1024,256]{1,0:T(8,128)(2,1)S(1)} collective-permute-done((bf16[1024,256]{1,0:T(8,128)(2,1)S(1)}, bf16[1024,256]{1,0:T(8,128)(2,1)S(1)}, u32[]{:S(2)}, u32[]{:S(2)}) %collective-permute-start.2) | collective-permute-done | bytes 524320 | tf_op jit(solution)/shard_map/ppermute | solution.py:307
  48.3 4.7 %collective-permute-done.3.refs_6_.refs_5_ = bf16[1024,256]{1,0:T(8,128)(2,1)S(1)} collective-permute-done((bf16[1024,256]{1,0:T(8,128)(2,1)S(1)}, bf16[1024,256]{1,0:T(8,128)(2,1)S(1)}, u32[]{:S(2)}, u32[]{:S(2)}) %collective-permute-start.3) | collective-permute-done | bytes 524320 | tf_op jit(solution)/shard_map/ppermute | solution.py:307
  55.5 3.1 %collective-permute-done.4.refs_7_.refs_6_ = bf16[1024,256]{1,0:T(8,128)(2,1)S(1)} collective-permute-done((bf16[1024,256]{1,0:T(8,128)(2,1)S(1)}, bf16[1024,256]{1,0:T(8,128)(2,1)S(1)}, u32[]{:S(2)}, u32[]{:S(2)}) %collective-permute-start.4) | collective-permute-done | bytes 524320 | tf_op jit(solution)/shard_map/ppermute | solution.py:307
  59.5 4.8 %collective-permute-done.5.refs_8_.refs_7_ = bf16[1024,256]{1,0:T(8,128)(2,1)} collective-permute-done((bf16[1024,256]{1,0:T(8,128)(2,1)S(1)}, bf16[1024,256]{1,0:T(8,128)(2,1)}, u32[]{:S(2)}, u32[]{:S(2)}) %collective-permute-start.5) | collective-permute-done | bytes 524320 | tf_op jit(solution)/shard_map/ppermute | solution.py:307
  67.1 10.6 %all-to-all-start.3 = ((f32[32,2,256]{2,1,0:T(2,128)}), f32[32,2,256]{2,1,0:T(2,128)S(1)}, u32[]{:S(2)}, u32[]{:S(2)}) async-start(f32[32,2,256]{2,1,0:T(2,128)} %broadcast_in_dim.9), calls=%async_computation.3 | async-start | bytes 131072 | tf_op jit(solution)/shard_map/all_to_all | solution.py:18
  77.7 2.1 copy.20
  80.7 2.3 %pad_maximum_fusion.refs_0_ = bf16[256,2048]{1,0:T(8,128)(2,1)} fusion(bf16[256,1024]{1,0:T(8,128)(2,1)} %bitcast.24, bf16[256,1024]{1,0:T(8,128)(2,1)} %bitcast.25), kind=kLoop, calls=%fused_computation.3 | loop fusion | flops 2097152 | bytes 2097152 | tf_op jit(solution)/shard_map/concatenate | solution.py:327
  83.1 4.5 %gram_first.1.partial_ref = bf16[256,1280]{1,0:T(8,128)(2,1)} custom-call(bf16[256,2048]{1,0:T(8,128)(2,1)} %pad_maximum_fusion.refs_0_, bf16[1024,256]{1,0:T(8,128)(2,1)} %refs_0_.1, bf16[1024,256]{1,0:T(8,128)(2,1)} %refs_1_.3, bf16[1024,256]{1,0:T(8,128)(2,1)} %copy-done.2, bf16[1024,256]{1,0:T(8,128)(2,1)} %copy-done.3, bf16[1024,256]{1,0:T(8,128)(2,1)} %copy-done.4, ...), custom_call_target="tpu_custom_call" | custom-call | flops 1073741824 | bytes 5242880 | tf_op jit(solution)/shard_map/gram_first/pallas_call | solution.py:83
  87.6 2.7 %gram_last.1 = bf16[256,1280]{1,0:T(8,128)(2,1)} custom-call(bf16[256,1280]{1,0:T(8,128)(2,1)} %gram_first.1.partial_ref, bf16[256,2048]{1,0:T(8,128)(2,1)} %pad_maximum_fusion.refs_0_, bf16[1024,256]{1,0:T(8,128)(2,1)} %collective-permute-done.6.refs_1_.refs_8_, bf16[1024,256]{1,0:T(8,128)(2,1)} %collective-permute-done.7.refs_2_.refs_9_), custom_call_target="tpu_custom_call", output_to_operand_aliasing={{}: (0, {})} | custom-call | flops 268435456 | bytes 2097152 | tf_op jit(solution)/shard_map/gram_last/pallas_call | solution.py:101
  90.3 7.4 %all-to-all-start.1 = ((bf16[32,8,1280]{2,1,0:T(8,128)(2,1)}), bf16[32,8,1280]{2,1,0:T(8,128)(2,1)S(1)}, u32[]{:S(2)}, u32[]{:S(2)}) async-start(bf16[32,8,1280]{2,1,0:T(8,128)(2,1)} %bitcast.22), calls=%async_computation.1 | async-start | bytes 1310720 | tf_op jit(solution)/shard_map/all_to_all | solution.py:22
  97.9 12.7 %all-to-all-done.1.got_ref = bf16[32,8,1280]{2,1,0:T(8,128)(2,1)S(1)} async-done(((bf16[32,8,1280]{2,1,0:T(8,128)(2,1)}), bf16[32,8,1280]{2,1,0:T(8,128)(2,1)S(1)}, u32[]{:S(2)}, u32[]{:S(2)}) %all-to-all-start.1) | async-done | bytes 655392 | tf_op jit(solution)/shard_map/all_to_all | solution.py:22
  110.6 1.4 gathered_sum.1
  112.0 4.1 %all-to-all-start.2 = ((bf16[32,8,2048]{2,1,0:T(8,128)(2,1)}), bf16[32,8,2048]{2,1,0:T(8,128)(2,1)S(1)}, u32[]{:S(2)}, u32[]{:S(2)}) async-start(bf16[32,8,2048]{2,1,0:T(8,128)(2,1)} %gathered_sum.1), calls=%async_computation.2 | async-start | bytes 2097152 | tf_op jit(solution)/shard_map/all_to_all | solution.py:22
  116.3 3.1 %collective-permute-start.8 = (bf16[1024,256]{1,0:T(8,128)(2,1)}, bf16[1024,256]{1,0:T(8,128)(2,1)S(1)}, u32[]{:S(2)}, u32[]{:S(2)}) collective-permute-start(bf16[1024,256]{1,0:T(8,128)(2,1)} %collective-permute-done.6.refs_1_.refs_8_), channel_id=1, source_target_pairs={{0,1},{1,2},{2,3},{3,4},{4,5},{5,6},{6,7},{7,0},{8,15},{9,8},{10,9... | collective-permute-start | bytes 1572872 | tf_op jit(solution)/shard_map/ppermute | solution.py:307
  119.7 13.5 %all-to-all-done.2 = bf16[32,8,2048]{2,1,0:T(8,128)(2,1)S(1)} async-done(((bf16[32,8,2048]{2,1,0:T(8,128)(2,1)}), bf16[32,8,2048]{2,1,0:T(8,128)(2,1)S(1)}, u32[]{:S(2)}, u32[]{:S(2)}) %all-to-all-start.2) | async-done | bytes 1048608 | tf_op jit(solution)/shard_map/all_to_all | solution.py:22
  134.4 4.3 %all-to-all-start.4 = ((bf16[8,86,256]{2,1,0:T(8,128)(2,1)}), bf16[8,86,256]{2,1,0:T(8,128)(2,1)S(1)}, u32[]{:S(2)}, u32[]{:S(2)}) async-start(bf16[8,86,256]{2,1,0:T(8,128)(2,1)} %broadcast_in_dim.10), calls=%async_computation.4 | async-start | bytes 720896 | tf_op jit(solution)/shard_map/all_to_all | solution.py:18
  138.8 2.7 %collective-permute-start.10 = (bf16[1024,256]{1,0:T(8,128)(2,1)S(1)}, bf16[1024,256]{1,0:T(8,128)(2,1)S(1)}, u32[]{:S(2)}, u32[]{:S(2)}) collective-permute-start(bf16[1024,256]{1,0:T(8,128)(2,1)S(1)} %collective-permute-done.8.refs_10_), channel_id=1, source_target_pairs={{0,1},{1,2},{2,3},{3,4},{4,5},{5,6},{6,7},{7,0},{8,15},{9,8},{10,9... | collective-permute-start | bytes 1572872 | tf_op jit(solution)/shard_map/ppermute | solution.py:307
  144.3 10.7 %collective-permute-done.10.refs_12_ = bf16[1024,256]{1,0:T(8,128)(2,1)S(1)} collective-permute-done((bf16[1024,256]{1,0:T(8,128)(2,1)S(1)}, bf16[1024,256]{1,0:T(8,128)(2,1)S(1)}, u32[]{:S(2)}, u32[]{:S(2)}) %collective-permute-start.10) | collective-permute-done | bytes 524320 | tf_op jit(solution)/shard_map/ppermute | solution.py:307
  155.9 4.7 %collective-permute-done.11.refs_13_ = bf16[1024,256]{1,0:T(8,128)(2,1)S(1)} collective-permute-done((bf16[1024,256]{1,0:T(8,128)(2,1)S(1)}, bf16[1024,256]{1,0:T(8,128)(2,1)S(1)}, u32[]{:S(2)}, u32[]{:S(2)}) %collective-permute-start.11) | collective-permute-done | bytes 524320 | tf_op jit(solution)/shard_map/ppermute | solution.py:307
  162.3 6.9 %rotated_cols.1 = (f32[2048,64]{1,0:T(8,128)}, bf16[32,64,128]{2,1,0:T(8,128)(2,1)}) custom-call(bf16[2048,2048]{1,0:T(8,128)(2,1)} %all-gather.2.cloned.1.call-done.basis_ref, bf16[8,86,256]{2,1,0:T(8,128)(2,1)} %copy-done.8, bf16[64,64]{1,0:T(8,128)(2,1)} %fusion.8.spread_ref), custom_call_target="tpu_custom_call" | custom-call | flops 536870912 | bytes 8388608 | tf_op jit(solution)/shard_map/rotated_cols/pallas_call | solution.py:173
  169.2 4.5 %all-to-all-start.5 = ((bf16[32,64,128]{2,1,0:T(8,128)(2,1)}), bf16[32,64,128]{2,1,0:T(8,128)(2,1)S(1)}, u32[]{:S(2)}, u32[]{:S(2)}) async-start(bf16[32,64,128]{2,1,0:T(8,128)(2,1)} %get-tuple-element.11), calls=%async_computation.5 | async-start | bytes 1048576 | tf_op jit(solution)/shard_map/all_to_all | solution.py:22
  175.1 8.2 %first_product.1 = (bf16[1024,2048]{1,0:T(8,128)(2,1)}, f32[1024,256]{1,0:T(8,128)}) custom-call(s32[8]{0:T(128)} %and_select_fusion.place_ref, f32[16,256]{1,0:T(8,128)} %reshape.44.told_ref, bf16[2048,256]{1,0:T(8,128)(2,1)} %whiten_ref.1, bf16[1024,256]{1,0:T(8,128)(2,1)} %refs_0_.1, bf16[1024,256]{1,0:T(8,128)(2,1)} %refs_1_.3, ...), custom_call_target="tpu_custom_call" | custom-call | flops 1073741824 | bytes 12582912 | tf_op jit(solution)/shard_map/first_product/pallas_call | solution.py:251
  183.9 2.3 constant_dynamic-slice_fusion.basis_ref
  187.0 4.5 %undone_copies.1 = bf16[32,64,256]{2,1,0:T(8,128)(2,1)} custom-call(f32[2048,64]{1,0:T(8,128)} %get-tuple-element.10.rot_ref, bf16[32,64,128]{2,1,0:T(8,128)(2,1)} %copy-done.7, f32[64,64]{1,0:T(8,128)} %pad_maximum_fusion.1.spread_ref, f32[64,2048]{1,0:T(8,128)} %divide_select_fusion.kernel_ref, bf16[2048,256]{1,0:T(8,128)(2,1)} %constant_dynamic-slice_fusion.basis_ref), custom_call_target="tpu_custom_call" | custom-call | flops 134217728 | bytes 2097152 | tf_op jit(solution)/shard_map/undone_copies/pallas_call | solution.py:219
  191.5 7.4 %all-to-all-start.6 = ((bf16[32,64,256]{2,1,0:T(8,128)(2,1)}), bf16[32,64,256]{2,1,0:T(8,128)(2,1)S(1)}, u32[]{:S(2)}, u32[]{:S(2)}) async-start(bf16[32,64,256]{2,1,0:T(8,128)(2,1)} %undone_copies.1), calls=%async_computation.6 | async-start | bytes 2097152 | tf_op jit(solution)/shard_map/all_to_all | solution.py:22
  198.9 14.0 %multiply_convert_fusion.turned_ref = bf16[1024,2048]{1,0:T(8,128)(2,1)} fusion(bf16[1024,2048]{1,0:T(8,128)(2,1)} %get-tuple-element.9, bf16[2048,2048]{1,0:T(8,128)(2,1)} %all-gather.2.cloned.1.call-done.basis_ref), kind=kOutput, calls=%fused_computation | convolution fusion | flops 8594128896 | bytes 16777216 | tf_op jit(solution)/shard_map/dot_general | solution.py:26
  212.8 3.1 %all-to-all-done.6 = bf16[32,64,256]{2,1,0:T(8,128)(2,1)S(1)} async-done(((bf16[32,64,256]{2,1,0:T(8,128)(2,1)}), bf16[32,64,256]{2,1,0:T(8,128)(2,1)S(1)}, u32[]{:S(2)}, u32[]{:S(2)}) %all-to-all-start.6) | async-done | bytes 1048608 | tf_op jit(solution)/shard_map/all_to_all | solution.py:22
  216.9 5.2 %last_product.1 = bf16[1024,256]{1,0:T(8,128)(2,1)} custom-call(bf16[1024,2048]{1,0:T(8,128)(2,1)} %multiply_convert_fusion.turned_ref, bf16[2048,256]{1,0:T(8,128)(2,1)} %bitcast.23, f32[1024,256]{1,0:T(8,128)} %get-tuple-element.12.running_ref), custom_call_target="tpu_custom_call" | custom-call | flops 1073741824 | bytes 5242880 | tf_op jit(solution)/shard_map/last_product/pallas_call | solution.py:279
  (87 shorter events, 22.7 us)
Async XLA Ops:
  6.5 73.2 %copy-start = (bf16[1024,256]{1,0:T(8,128)(2,1)S(1)}, bf16[1024,256]{1,0:T(8,128)(2,1)}, u32[]{:S(2)}) copy-start(bf16[1024,256]{1,0:T(8,128)(2,1)} %refs_1_.3) | copy-start | bytes 1572868
  6.5 155.7 %all-gather.2.cloned.1.call-start = ((), (), s32[]{:S(2)}) async-start(), calls=%async_computation.7 | async-start | bytes 8650752 | tf_op jit(solution)/shard_map/all_gather | solution.py:325
  27.5 8.6 %collective-permute-start = (bf16[1024,256]{1,0:T(8,128)(2,1)}, bf16[1024,256]{1,0:T(8,128)(2,1)S(1)}, u32[]{:S(2)}, u32[]{:S(2)}) collective-permute-start(bf16[1024,256]{1,0:T(8,128)(2,1)} %refs_0_.1), channel_id=1, source_target_pairs={{0,1},{1,2},{2,3},{3,4},{4,5},{5,6},{6,7},{7,0},{8,15},{9,8},{10,9... | collective-permute-start | bytes 1572872 | tf_op jit(solution)/shard_map/ppermute | solution.py:307
  27.6 14.2 %collective-permute-start.1 = (bf16[1024,256]{1,0:T(8,128)(2,1)}, bf16[1024,256]{1,0:T(8,128)(2,1)S(1)}, u32[]{:S(2)}, u32[]{:S(2)}) collective-permute-start(bf16[1024,256]{1,0:T(8,128)(2,1)} %refs_1_.3), channel_id=1, source_target_pairs={{0,1},{1,2},{2,3},{3,4},{4,5},{5,6},{6,7},{7,0},{8,15},{9,8},{10,9... | collective-permute-start | bytes 1572872 | tf_op jit(solution)/shard_map/ppermute | solution.py:307
  36.1 46.9 %copy-start.2 = (bf16[1024,256]{1,0:T(8,128)(2,1)}, bf16[1024,256]{1,0:T(8,128)(2,1)S(1)}, u32[]{:S(2)}) copy-start(bf16[1024,256]{1,0:T(8,128)(2,1)S(1)} %collective-permute-done.refs_3_.refs_2_) | copy-start | bytes 1572868
  36.1 11.3 %collective-permute-start.2 = (bf16[1024,256]{1,0:T(8,128)(2,1)S(1)}, bf16[1024,256]{1,0:T(8,128)(2,1)S(1)}, u32[]{:S(2)}, u32[]{:S(2)}) collective-permute-start(bf16[1024,256]{1,0:T(8,128)(2,1)S(1)} %collective-permute-done.refs_3_.refs_2_), channel_id=1, source_target_pairs={{0,1},{1,2},{2,3},{3,4},{4,5},{5,6},{6,7},{7,0},{8,15},{9,8},{10,9... | collective-permute-start | bytes 1572872 | tf_op jit(solution)/shard_map/ppermute | solution.py:307
  41.8 41.2 %copy-start.3 = (bf16[1024,256]{1,0:T(8,128)(2,1)}, bf16[1024,256]{1,0:T(8,128)(2,1)S(1)}, u32[]{:S(2)}) copy-start(bf16[1024,256]{1,0:T(8,128)(2,1)S(1)} %collective-permute-done.1.refs_4_.refs_3_) | copy-start | bytes 1572868
  41.8 11.1 %collective-permute-start.3 = (bf16[1024,256]{1,0:T(8,128)(2,1)S(1)}, bf16[1024,256]{1,0:T(8,128)(2,1)S(1)}, u32[]{:S(2)}, u32[]{:S(2)}) collective-permute-start(bf16[1024,256]{1,0:T(8,128)(2,1)S(1)} %collective-permute-done.1.refs_4_.refs_3_), channel_id=1, source_target_pairs={{0,1},{1,2},{2,3},{3,4},{4,5},{5,6},{6,7},{7,0},{8,15},{9,8},{10,9... | collective-permute-start | bytes 1572872 | tf_op jit(solution)/shard_map/ppermute | solution.py:307
  47.5 35.6 %copy-start.4 = (bf16[1024,256]{1,0:T(8,128)(2,1)}, bf16[1024,256]{1,0:T(8,128)(2,1)S(1)}, u32[]{:S(2)}) copy-start(bf16[1024,256]{1,0:T(8,128)(2,1)S(1)} %collective-permute-done.2.refs_5_.refs_4_) | copy-start | bytes 1572868
  47.5 11.1 %collective-permute-start.4 = (bf16[1024,256]{1,0:T(8,128)(2,1)S(1)}, bf16[1024,256]{1,0:T(8,128)(2,1)S(1)}, u32[]{:S(2)}, u32[]{:S(2)}) collective-permute-start(bf16[1024,256]{1,0:T(8,128)(2,1)S(1)} %collective-permute-done.2.refs_5_.refs_4_), channel_id=1, source_target_pairs={{0,1},{1,2},{2,3},{3,4},{4,5},{5,6},{6,7},{7,0},{8,15},{9,8},{10,9... | collective-permute-start | bytes 1572872 | tf_op jit(solution)/shard_map/ppermute | solution.py:307
  53.0 30.1 %copy-start.5 = (bf16[1024,256]{1,0:T(8,128)(2,1)}, bf16[1024,256]{1,0:T(8,128)(2,1)S(1)}, u32[]{:S(2)}) copy-start(bf16[1024,256]{1,0:T(8,128)(2,1)S(1)} %collective-permute-done.3.refs_6_.refs_5_) | copy-start | bytes 1572868
  53.0 11.3 %collective-permute-start.5 = (bf16[1024,256]{1,0:T(8,128)(2,1)S(1)}, bf16[1024,256]{1,0:T(8,128)(2,1)}, u32[]{:S(2)}, u32[]{:S(2)}) collective-permute-start(bf16[1024,256]{1,0:T(8,128)(2,1)S(1)} %collective-permute-done.3.refs_6_.refs_5_), channel_id=1, source_target_pairs={{0,1},{1,2},{2,3},{3,4},{4,5},{5,6},{6,7},{7,0},{8,15},{9,8},{10,9... | collective-permute-start | bytes 1572872 | tf_op jit(solution)/shard_map/ppermute | solution.py:307
  58.6 24.5 %copy-start.6 = (bf16[1024,256]{1,0:T(8,128)(2,1)}, bf16[1024,256]{1,0:T(8,128)(2,1)S(1)}, u32[]{:S(2)}) copy-start(bf16[1024,256]{1,0:T(8,128)(2,1)S(1)} %collective-permute-done.4.refs_7_.refs_6_) | copy-start | bytes 1572868
  58.6 29.0 %collective-permute-start.6 = (bf16[1024,256]{1,0:T(8,128)(2,1)S(1)}, bf16[1024,256]{1,0:T(8,128)(2,1)}, u32[]{:S(2)}, u32[]{:S(2)}) collective-permute-start(bf16[1024,256]{1,0:T(8,128)(2,1)S(1)} %collective-permute-done.4.refs_7_.refs_6_), channel_id=1, source_target_pairs={{0,1},{1,2},{2,3},{3,4},{4,5},{5,6},{6,7},{7,0},{8,15},{9,8},{10,9... | collective-permute-start | bytes 1572872 | tf_op jit(solution)/shard_map/ppermute | solution.py:307
  64.3 23.3 %collective-permute-start.7 = (bf16[1024,256]{1,0:T(8,128)(2,1)}, bf16[1024,256]{1,0:T(8,128)(2,1)}, u32[]{:S(2)}, u32[]{:S(2)}) collective-permute-start(bf16[1024,256]{1,0:T(8,128)(2,1)} %collective-permute-done.5.refs_8_.refs_7_), channel_id=1, source_target_pairs={{0,1},{1,2},{2,3},{3,4},{4,5},{5,6},{6,7},{7,0},{8,15},{9,8},{10,9... | collective-permute-start | bytes 1572872 | tf_op jit(solution)/shard_map/ppermute | solution.py:307
  67.1 23.3 %all-to-all-start.3 = ((f32[32,2,256]{2,1,0:T(2,128)}), f32[32,2,256]{2,1,0:T(2,128)S(1)}, u32[]{:S(2)}, u32[]{:S(2)}) async-start(f32[32,2,256]{2,1,0:T(2,128)} %broadcast_in_dim.9), calls=%async_computation.3 | async-start | bytes 131072 | tf_op jit(solution)/shard_map/all_to_all | solution.py:18
  87.6 28.5 %copy-start.14 = (f32[256,64]{0,1:T(8,128)S(1)}, f32[256,64]{0,1:T(8,128)}, u32[]{:S(2)}) copy-start(f32[256,64]{0,1:T(8,128)} %param.7) | copy-start | bytes 196612
  87.6 45.6 %copy-start.9 = (bf16[8,8,8,256]{3,2,0,1:T(8,128)(2,1)S(1)}, bf16[8,8,8,256]{3,2,0,1:T(8,128)(2,1)}, u32[]{:S(2)}) copy-start(bf16[8,8,8,256]{3,2,0,1:T(8,128)(2,1)} %copy.24) | copy-start | bytes 786436
  90.3 20.2 %all-to-all-start.1 = ((bf16[32,8,1280]{2,1,0:T(8,128)(2,1)}), bf16[32,8,1280]{2,1,0:T(8,128)(2,1)S(1)}, u32[]{:S(2)}, u32[]{:S(2)}) async-start(bf16[32,8,1280]{2,1,0:T(8,128)(2,1)} %bitcast.22), calls=%async_computation.1 | async-start | bytes 1310720 | tf_op jit(solution)/shard_map/all_to_all | solution.py:22
  112.0 21.2 %all-to-all-start.2 = ((bf16[32,8,2048]{2,1,0:T(8,128)(2,1)}), bf16[32,8,2048]{2,1,0:T(8,128)(2,1)S(1)}, u32[]{:S(2)}, u32[]{:S(2)}) async-start(bf16[32,8,2048]{2,1,0:T(8,128)(2,1)} %gathered_sum.1), calls=%async_computation.2 | async-start | bytes 2097152 | tf_op jit(solution)/shard_map/all_to_all | solution.py:22
  116.3 22.4 %collective-permute-start.8 = (bf16[1024,256]{1,0:T(8,128)(2,1)}, bf16[1024,256]{1,0:T(8,128)(2,1)S(1)}, u32[]{:S(2)}, u32[]{:S(2)}) collective-permute-start(bf16[1024,256]{1,0:T(8,128)(2,1)} %collective-permute-done.6.refs_1_.refs_8_), channel_id=1, source_target_pairs={{0,1},{1,2},{2,3},{3,4},{4,5},{5,6},{6,7},{7,0},{8,15},{9,8},{10,9... | collective-permute-start | bytes 1572872 | tf_op jit(solution)/shard_map/ppermute | solution.py:307
  119.4 22.1 %collective-permute-start.9 = (bf16[1024,256]{1,0:T(8,128)(2,1)}, bf16[1024,256]{1,0:T(8,128)(2,1)S(1)}, u32[]{:S(2)}, u32[]{:S(2)}) collective-permute-start(bf16[1024,256]{1,0:T(8,128)(2,1)} %collective-permute-done.7.refs_2_.refs_9_), channel_id=1, source_target_pairs={{0,1},{1,2},{2,3},{3,4},{4,5},{5,6},{6,7},{7,0},{8,15},{9,8},{10,9... | collective-permute-start | bytes 1572872 | tf_op jit(solution)/shard_map/ppermute | solution.py:307
  134.4 27.1 %all-to-all-start.4 = ((bf16[8,86,256]{2,1,0:T(8,128)(2,1)}), bf16[8,86,256]{2,1,0:T(8,128)(2,1)S(1)}, u32[]{:S(2)}, u32[]{:S(2)}) async-start(bf16[8,86,256]{2,1,0:T(8,128)(2,1)} %broadcast_in_dim.10), calls=%async_computation.4 | async-start | bytes 720896 | tf_op jit(solution)/shard_map/all_to_all | solution.py:18
  138.8 30.4 %copy-start.10 = (bf16[1024,256]{1,0:T(8,128)(2,1)}, bf16[1024,256]{1,0:T(8,128)(2,1)S(1)}, u32[]{:S(2)}) copy-start(bf16[1024,256]{1,0:T(8,128)(2,1)S(1)} %collective-permute-done.8.refs_10_) | copy-start | bytes 1572868
  138.8 16.2 %collective-permute-start.10 = (bf16[1024,256]{1,0:T(8,128)(2,1)S(1)}, bf16[1024,256]{1,0:T(8,128)(2,1)S(1)}, u32[]{:S(2)}, u32[]{:S(2)}) collective-permute-start(bf16[1024,256]{1,0:T(8,128)(2,1)S(1)} %collective-permute-done.8.refs_10_), channel_id=1, source_target_pairs={{0,1},{1,2},{2,3},{3,4},{4,5},{5,6},{6,7},{7,0},{8,15},{9,8},{10,9... | collective-permute-start | bytes 1572872 | tf_op jit(solution)/shard_map/ppermute | solution.py:307
  141.5 33.6 %copy-start.11 = (bf16[1024,256]{1,0:T(8,128)(2,1)}, bf16[1024,256]{1,0:T(8,128)(2,1)S(1)}, u32[]{:S(2)}) copy-start(bf16[1024,256]{1,0:T(8,128)(2,1)S(1)} %collective-permute-done.9.refs_11_) | copy-start | bytes 1572868
  141.5 19.1 %collective-permute-start.11 = (bf16[1024,256]{1,0:T(8,128)(2,1)S(1)}, bf16[1024,256]{1,0:T(8,128)(2,1)S(1)}, u32[]{:S(2)}, u32[]{:S(2)}) collective-permute-start(bf16[1024,256]{1,0:T(8,128)(2,1)S(1)} %collective-permute-done.9.refs_11_), channel_id=1, source_target_pairs={{0,1},{1,2},{2,3},{3,4},{4,5},{5,6},{6,7},{7,0},{8,15},{9,8},{10,9... | collective-permute-start | bytes 1572872 | tf_op jit(solution)/shard_map/ppermute | solution.py:307
  155.0 20.1 %copy-start.12 = (bf16[1024,256]{1,0:T(8,128)(2,1)}, bf16[1024,256]{1,0:T(8,128)(2,1)S(1)}, u32[]{:S(2)}) copy-start(bf16[1024,256]{1,0:T(8,128)(2,1)S(1)} %collective-permute-done.10.refs_12_) | copy-start | bytes 1572868
  155.0 20.1 %collective-permute-start.12 = (bf16[1024,256]{1,0:T(8,128)(2,1)S(1)}, bf16[1024,256]{1,0:T(8,128)(2,1)}, u32[]{:S(2)}, u32[]{:S(2)}) collective-permute-start(bf16[1024,256]{1,0:T(8,128)(2,1)S(1)} %collective-permute-done.10.refs_12_), channel_id=1, source_target_pairs={{0,1},{1,2},{2,3},{3,4},{4,5},{5,6},{6,7},{7,0},{8,15},{9,8},{10,9... | collective-permute-start | bytes 1572872 | tf_op jit(solution)/shard_map/ppermute | solution.py:307
  160.6 14.5 %collective-permute-start.13 = (bf16[1024,256]{1,0:T(8,128)(2,1)S(1)}, bf16[1024,256]{1,0:T(8,128)(2,1)}, u32[]{:S(2)}, u32[]{:S(2)}) collective-permute-start(bf16[1024,256]{1,0:T(8,128)(2,1)S(1)} %collective-permute-done.11.refs_13_), channel_id=1, source_target_pairs={{0,1},{1,2},{2,3},{3,4},{4,5},{5,6},{6,7},{7,0},{8,15},{9,8},{10,9... | collective-permute-start | bytes 1572872 | tf_op jit(solution)/shard_map/ppermute | solution.py:307
  169.2 17.0 %all-to-all-start.5 = ((bf16[32,64,128]{2,1,0:T(8,128)(2,1)}), bf16[32,64,128]{2,1,0:T(8,128)(2,1)S(1)}, u32[]{:S(2)}, u32[]{:S(2)}) async-start(bf16[32,64,128]{2,1,0:T(8,128)(2,1)} %get-tuple-element.11), calls=%async_computation.5 | async-start | bytes 1048576 | tf_op jit(solution)/shard_map/all_to_all | solution.py:22
  191.5 24.4 %all-to-all-start.6 = ((bf16[32,64,256]{2,1,0:T(8,128)(2,1)}), bf16[32,64,256]{2,1,0:T(8,128)(2,1)S(1)}, u32[]{:S(2)}, u32[]{:S(2)}) async-start(bf16[32,64,256]{2,1,0:T(8,128)(2,1)} %undone_copies.1), calls=%async_computation.6 | async-start | bytes 2097152 | tf_op jit(solution)/shard_map/all_to_all | solution.py:22
  (5 other events, 31.7 us)
Sparse Core Ops, SparseCore 0:
  27.6 56.1 all-gather.1

commit v8 on v7

--- a/solution.py
+++ b/solution.py
@@ -128,14 +128,15 @@
         value = jnp.concatenate(pair, axis=1).astype(BF16)
 
         def store(i, carry):
-            out_ref[i] = value
+            out_ref[2 * i] = value[:, : half * width]
+            out_ref[2 * i + 1] = value[:, half * width :]
             return carry
 
-        lax.fori_loop(0, groups, store, 0)
-
-    return pl.pallas_call(
-        body,
-        out_shape=jax.ShapeDtypeStruct((groups, few, 2 * half * width), BF16),
+        lax.fori_loop(0, groups // 2, store, 0)
+
+    return pl.pallas_call(
+        body,
+        out_shape=jax.ShapeDtypeStruct((groups, few, half * width), BF16),
         in_specs=[VMEM],
         out_specs=VMEM,
         compiler_params=params(SMALL),
@@ -193,7 +194,14 @@
     dim, narrow = rot.shape
     groups, width = back.shape[0], basis.shape[1]
 
-    def body(rot_ref, back_ref, spread_ref, kernel_ref, basis_ref, out_ref):
+    def body(*refs):
+        out_ref, held, sems = refs[5], refs[6:11], refs[11]
+        copies = [pltpu.make_async_copy(refs[k], held[k], sems.at[k]) for k in range(5)]
+        for copy in copies:
+            copy.start()
+        for copy in copies:
+            copy.wait()
+        rot_ref, back_ref, spread_ref, kernel_ref, basis_ref = held
         halfway = narrow // 2
         crossed = jnp.concatenate([spread_ref[halfway:, :], spread_ref[:halfway, :]], axis=0)
         crossed = crossed.T.astype(BF16)
@@ -219,8 +227,10 @@
     return pl.pallas_call(
         body,
         out_shape=jax.ShapeDtypeStruct((groups, narrow, width), BF16),
-        in_specs=[VMEM] * 5,
+        in_specs=[pl.BlockSpec(memory_space=pl.ANY)] * 5,
         out_specs=VMEM,
+        scratch_shapes=[pltpu.VMEM(a.shape, a.dtype) for a in (rot, back, spread, kernel_t, basis)]
+        + [pltpu.SemaphoreType.DMA((5,))],
         compiler_params=params(),
         cost_estimate=cost(4 * dim * narrow * width, 4 * dim * width),
         name="undone_copies",
@@ -269,19 +279,41 @@
 def last_product(turned, undone, running):
     n, dim = turned.shape
     width = undone.shape[1]
-    rows = 256
-
-    def body(turned_ref, undone_ref, running_ref, out_ref):
-        value = running_ref[...] + product(turned_ref[...], undone_ref[...])
-        out_ref[...] = value.astype(BF16)
-
-    part = lambda cols: pl.BlockSpec((rows, cols), lambda i: (i, 0))
+    steps = 4
+    rows = n // steps
+
+    def body(turned_ref, undone_ref, running_ref, out_ref, left_ref, right_ref, added_ref, sems):
+        first = pltpu.make_async_copy(undone_ref, right_ref, sems.at[steps])
+        first.start()
+        copies = [
+            pltpu.make_async_copy(
+                turned_ref.at[pl.ds(i * rows, rows), :], left_ref.at[i], sems.at[i]
+            )
+            for i in range(steps)
+        ]
+        for copy in copies:
+            copy.start()
+        last = pltpu.make_async_copy(running_ref, added_ref, sems.at[steps + 1])
+        last.start()
+        first.wait()
+        last.wait()
+        for i in range(steps):
+            copies[i].wait()
+            at = slice(i * rows, (i + 1) * rows)
+            value = added_ref[at, :] + product(left_ref[i], right_ref[...])
+            out_ref[at, :] = value.astype(BF16)
+
     return pl.pallas_call(
         body,
         out_shape=jax.ShapeDtypeStruct((n, width), BF16),
-        grid=(n // rows,),
-        in_specs=[part(dim), pl.BlockSpec((dim, width), lambda i: (0, 0)), part(width)],
-        out_specs=part(width),
+        in_specs=[pl.BlockSpec(memory_space=pl.ANY)] * 3,
+        out_specs=VMEM,
+        scratch_shapes=[
+            pltpu.VMEM((steps, rows, dim), BF16),
+            pltpu.VMEM((dim, width), BF16),
+            pltpu.VMEM((n, width), F32),
+            pltpu.SemaphoreType.DMA((steps + 2,)),
+        ],
         compiler_params=params(),
         cost_estimate=cost(2 * n * dim * width, 2 * n * dim + 2 * dim * width),
         name="last_product",
@@ -306,6 +338,10 @@
         ]
         return lax.ppermute(value, ("rows", "feat"), pairs)
 
+    def swap(value):
+        pairs = [(a * planes + b, (a ^ 1) * planes + b) for a in range(groups) for b in range(planes)]
+        return lax.ppermute(value, ("rows", "feat"), pairs)
+
     blocks = [(grad_out, features)]
     for _ in range(1, planes):
         grads = pass_on(blocks[-1][0])
@@ -322,6 +358,7 @@
 
     basis_rt = copy_for_each(eigvecs.astype(BF16).T, "feat")
     basis_rt = jnp.swapaxes(basis_rt, 0, 1).reshape(narrow, dim)
+    both = jnp.concatenate([basis_rt, swap(basis_rt)])
     basis_t = lax.all_gather(basis_rt, "rows", axis=0, tiled=True)
 
     own = jnp.concatenate([features.T, grad_out.T], axis=1)
@@ -330,11 +367,12 @@
 
     got = exchange(mixed.reshape(groups, width // groups, -1), "rows")
     copies = gathered_sum(got, width, half)
-    gram = exchange(copies, "rows").reshape(width, dim)
-
-    twice = jnp.concatenate([basis_rt, basis_rt], axis=1)
-    turned = lax.dynamic_slice_in_dim(twice, f * width, dim, axis=1)
-    right = contract_last(turned, gram).astype(BF16)
+    gram = exchange(copies, "rows").reshape(width, half * width)
+
+    twice = jnp.concatenate([both, both], axis=1)
+    turned = lax.dynamic_slice_in_dim(twice, f * width + (r % 2) * half * width, half * width, axis=1)
+    right = contract_last(turned, gram)
+    right = (right[:narrow] + swap(right[narrow:])).astype(BF16)
     shared = copy_for_each(jnp.concatenate([right, spread, *three_parts(means)]), "feat")
     spread = jnp.sum(shared[:, narrow : narrow + few].astype(F32), axis=0)
     spread = jnp.concatenate(

time: 230 us -> 226 us (0.983)
  waiting for transfers between devices: 73.8 us -> 67.5 us
    all_to_all x4, waiting for transfers between devices: 29.2 us -> 23.4 us  [exchange(): return lax.all_to_all(parts, axis, split_axis=0, concat_axis=0, tiled=True)]
  transfers between devices with their start and end apart: 21 -> 23, of which waited for: 11 -> 12; matrix products, arithmetic and copies ran while one was open for 13% -> 14% of each run, Pallas kernels for 10% -> 10%
where the time goes in v8:
time: 226 us; the launch traced here: 225 us
  waiting for transfers between devices  67.5 us (30%)
  starting transfers between devices  55.4 us (25%)
  Pallas kernels  34.4 us (15%)
  blocking collectives  19.3 us (9%)
  matrix products  15.2 us (7%)
  between operations  13.7 us (6%)
  local copies, waits for them, and re-layouts  10.1 us (4%)
  other arithmetic  9.52 us (4%)
    ppermute x14, waiting for transfers between devices, pass_on(): return lax.ppermute(value, ('rows', 'feat'), pairs)  43.3 us
    all_to_all x4, waiting for transfers between devices, exchange(): return lax.all_to_all(parts, axis, split_axis=0, concat_axis=0, tiled=True)  23.4 us
    all_to_all x4, starting transfers between devices, exchange(): return lax.all_to_all(parts, axis, split_axis=0, concat_axis=0, tiled=True)  23.3 us
    all_to_all x1, blocking collectives, copy_for_each(): return lax.all_to_all(copies, axis, split_axis=0, concat_axis=0, tiled=True)  19.3 us
    ppermute x14, starting transfers between devices, pass_on(): return lax.ppermute(value, ('rows', 'feat'), pairs)  16.4 us
    dot_general x2, matrix products, contract_last(): lax.dot_general(a, b, (((1,), (1,)), ((), ())), preferred_element_type=F32)  15 us
    all_to_all x2, starting transfers between devices, copy_for_each(): return lax.all_to_all(copies, axis, split_axis=0, concat_axis=0, tiled=True)  14.8 us
    pallas_call x1, Pallas kernels, first_product(): pl.pallas_call(body, out_shape=[jax.ShapeDtypeStruct((n, dim), BF16), jax...  8.21 us
  transfers between devices with their start and end apart: 23, of which 12 were waited for; matrix products, arithmetic and copies ran while one was open for 14% of the time, Pallas kernels for 10%

profile of v8, /device:TPU:1, one launch (start us, length us, event | category | flops | bytes accessed | tf_op | source)
XLA Modules:
  0.0 225.2 jit_solution(1528999590236664263)
XLA Ops:
  7.5 19.3 %all_to_all.35 = bf16[8,64,256]{2,1,0:T(8,128)(2,1)S(1)} all-to-all(bf16[8,64,256]{2,1,0:T(8,128)(2,1)S(1)} %broadcast_in_dim.8), channel_id=1, replica_groups=mesh['rows'=32,'feat'=8] {'feat'}, dimensions={0} | all-to-all | bytes 524288 | tf_op jit(solution)/shard_map/all_to_all | solution.py:18
  27.6 1.6 collective-permute-start.2
  29.2 6.9 %collective-permute-done.1.refs_3_.refs_2_ = bf16[1024,256]{1,0:T(8,128)(2,1)S(1)} collective-permute-done((bf16[1024,256]{1,0:T(8,128)(2,1)}, bf16[1024,256]{1,0:T(8,128)(2,1)S(1)}, u32[]{:S(2)}, u32[]{:S(2)}) %collective-permute-start.1) | collective-permute-done | bytes 524320 | tf_op jit(solution)/shard_map/ppermute | solution.py:339
  37.1 4.8 %collective-permute-done.2.refs_4_.refs_3_ = bf16[1024,256]{1,0:T(8,128)(2,1)S(1)} collective-permute-done((bf16[1024,256]{1,0:T(8,128)(2,1)}, bf16[1024,256]{1,0:T(8,128)(2,1)S(1)}, u32[]{:S(2)}, u32[]{:S(2)}) %collective-permute-start.2) | collective-permute-done | bytes 524320 | tf_op jit(solution)/shard_map/ppermute | solution.py:339
  42.7 4.8 %collective-permute-done.3.refs_5_.refs_4_ = bf16[1024,256]{1,0:T(8,128)(2,1)S(1)} collective-permute-done((bf16[1024,256]{1,0:T(8,128)(2,1)S(1)}, bf16[1024,256]{1,0:T(8,128)(2,1)S(1)}, u32[]{:S(2)}, u32[]{:S(2)}) %collective-permute-start.3) | collective-permute-done | bytes 524320 | tf_op jit(solution)/shard_map/ppermute | solution.py:339
  48.3 4.7 %collective-permute-done.4.refs_6_.refs_5_ = bf16[1024,256]{1,0:T(8,128)(2,1)S(1)} collective-permute-done((bf16[1024,256]{1,0:T(8,128)(2,1)S(1)}, bf16[1024,256]{1,0:T(8,128)(2,1)S(1)}, u32[]{:S(2)}, u32[]{:S(2)}) %collective-permute-start.4) | collective-permute-done | bytes 524320 | tf_op jit(solution)/shard_map/ppermute | solution.py:339
  53.0 1.3 collective-permute-start.6
  56.7 1.9 collective-permute-done.5.refs_7_.refs_6_
  59.5 4.8 %collective-permute-done.6.refs_8_.refs_7_ = bf16[1024,256]{1,0:T(8,128)(2,1)} collective-permute-done((bf16[1024,256]{1,0:T(8,128)(2,1)S(1)}, bf16[1024,256]{1,0:T(8,128)(2,1)}, u32[]{:S(2)}, u32[]{:S(2)}) %collective-permute-start.6) | collective-permute-done | bytes 524320 | tf_op jit(solution)/shard_map/ppermute | solution.py:339
  65.9 10.6 %all-to-all-start.3 = ((f32[32,2,256]{2,1,0:T(2,128)}), f32[32,2,256]{2,1,0:T(2,128)S(1)}, u32[]{:S(2)}, u32[]{:S(2)}) async-start(f32[32,2,256]{2,1,0:T(2,128)} %broadcast_in_dim.9), calls=%async_computation.3 | async-start | bytes 131072 | tf_op jit(solution)/shard_map/all_to_all | solution.py:18
  76.5 2.1 copy.20
  79.6 2.3 %pad_maximum_fusion.refs_0_ = bf16[256,2048]{1,0:T(8,128)(2,1)} fusion(bf16[256,1024]{1,0:T(8,128)(2,1)} %bitcast.24, bf16[256,1024]{1,0:T(8,128)(2,1)} %bitcast.25), kind=kLoop, calls=%fused_computation.6 | loop fusion | flops 2097152 | bytes 2097152 | tf_op jit(solution)/shard_map/concatenate | solution.py:364
  82.0 4.6 %gram_first.1.partial_ref = bf16[256,1280]{1,0:T(8,128)(2,1)} custom-call(bf16[256,2048]{1,0:T(8,128)(2,1)} %pad_maximum_fusion.refs_0_, bf16[1024,256]{1,0:T(8,128)(2,1)} %refs_0_.1, bf16[1024,256]{1,0:T(8,128)(2,1)} %refs_1_.3, bf16[1024,256]{1,0:T(8,128)(2,1)} %copy-done.2, bf16[1024,256]{1,0:T(8,128)(2,1)} %copy-done.3, bf16[1024,256]{1,0:T(8,128)(2,1)} %copy-done.4, ...), custom_call_target="tpu_custom_call" | custom-call | flops 1073741824 | bytes 5242880 | tf_op jit(solution)/shard_map/gram_first/pallas_call | solution.py:83
  86.6 2.7 %gram_last.1 = bf16[256,1280]{1,0:T(8,128)(2,1)} custom-call(bf16[256,1280]{1,0:T(8,128)(2,1)} %gram_first.1.partial_ref, bf16[256,2048]{1,0:T(8,128)(2,1)} %pad_maximum_fusion.refs_0_, bf16[1024,256]{1,0:T(8,128)(2,1)} %collective-permute-done.7.refs_1_.refs_8_, bf16[1024,256]{1,0:T(8,128)(2,1)} %collective-permute-done.8.refs_2_.refs_9_), custom_call_target="tpu_custom_call", output_to_operand_aliasing={{}: (0, {})} | custom-call | flops 268435456 | bytes 2097152 | tf_op jit(solution)/shard_map/gram_last/pallas_call | solution.py:101
  89.3 7.4 %all-to-all-start.1 = ((bf16[32,8,1280]{2,1,0:T(8,128)(2,1)}), bf16[32,8,1280]{2,1,0:T(8,128)(2,1)S(1)}, u32[]{:S(2)}, u32[]{:S(2)}) async-start(bf16[32,8,1280]{2,1,0:T(8,128)(2,1)} %bitcast.22), calls=%async_computation.1 | async-start | bytes 1310720 | tf_op jit(solution)/shard_map/all_to_all | solution.py:22
  96.7 12.7 %all-to-all-done.1.got_ref = bf16[32,8,1280]{2,1,0:T(8,128)(2,1)S(1)} async-done(((bf16[32,8,1280]{2,1,0:T(8,128)(2,1)}), bf16[32,8,1280]{2,1,0:T(8,128)(2,1)S(1)}, u32[]{:S(2)}, u32[]{:S(2)}) %all-to-all-start.1) | async-done | bytes 655392 | tf_op jit(solution)/shard_map/all_to_all | solution.py:22
  110.5 4.0 %all-to-all-start.2 = ((bf16[32,8,1024]{2,1,0:T(8,128)(2,1)}), bf16[32,8,1024]{2,1,0:T(8,128)(2,1)S(1)}, u32[]{:S(2)}, u32[]{:S(2)}) async-start(bf16[32,8,1024]{2,1,0:T(8,128)(2,1)} %gathered_sum.1), calls=%async_computation.2 | async-start | bytes 1048576 | tf_op jit(solution)/shard_map/all_to_all | solution.py:22
  115.3 3.2 %collective-permute-start.10 = (bf16[1024,256]{1,0:T(8,128)(2,1)}, bf16[1024,256]{1,0:T(8,128)(2,1)S(1)}, u32[]{:S(2)}, u32[]{:S(2)}) collective-permute-start(bf16[1024,256]{1,0:T(8,128)(2,1)} %collective-permute-done.7.refs_1_.refs_8_), channel_id=1, source_target_pairs={{0,1},{1,2},{2,3},{3,4},{4,5},{5,6},{6,7},{7,0},{8,15},{9,8},{10,9... | collective-permute-start | bytes 1572872 | tf_op jit(solution)/shard_map/ppermute | solution.py:339
  118.6 7.6 %all-to-all-done.2 = bf16[32,8,1024]{2,1,0:T(8,128)(2,1)S(1)} async-done(((bf16[32,8,1024]{2,1,0:T(8,128)(2,1)}), bf16[32,8,1024]{2,1,0:T(8,128)(2,1)S(1)}, u32[]{:S(2)}, u32[]{:S(2)}) %all-to-all-start.2) | async-done | bytes 524320 | tf_op jit(solution)/shard_map/all_to_all | solution.py:22
  129.4 4.2 %all-to-all-start.4 = ((bf16[8,86,256]{2,1,0:T(8,128)(2,1)}), bf16[8,86,256]{2,1,0:T(8,128)(2,1)S(1)}, u32[]{:S(2)}, u32[]{:S(2)}) async-start(bf16[8,86,256]{2,1,0:T(8,128)(2,1)} %broadcast_in_dim.10), calls=%async_computation.4 | async-start | bytes 720896 | tf_op jit(solution)/shard_map/all_to_all | solution.py:18
  133.7 2.7 %collective-permute-start.12 = (bf16[1024,256]{1,0:T(8,128)(2,1)S(1)}, bf16[1024,256]{1,0:T(8,128)(2,1)S(1)}, u32[]{:S(2)}, u32[]{:S(2)}) collective-permute-start(bf16[1024,256]{1,0:T(8,128)(2,1)S(1)} %collective-permute-done.10.refs_10_), channel_id=1, source_target_pairs={{0,1},{1,2},{2,3},{3,4},{4,5},{5,6},{6,7},{7,0},{8,15},{9,8},{10,9... | collective-permute-start | bytes 1572872 | tf_op jit(solution)/shard_map/ppermute | solution.py:339
  139.2 10.7 %collective-permute-done.12.refs_12_ = bf16[1024,256]{1,0:T(8,128)(2,1)S(1)} collective-permute-done((bf16[1024,256]{1,0:T(8,128)(2,1)S(1)}, bf16[1024,256]{1,0:T(8,128)(2,1)S(1)}, u32[]{:S(2)}, u32[]{:S(2)}) %collective-permute-start.12) | collective-permute-done | bytes 524320 | tf_op jit(solution)/shard_map/ppermute | solution.py:339
  150.8 4.7 %collective-permute-done.13.refs_13_ = bf16[1024,256]{1,0:T(8,128)(2,1)S(1)} collective-permute-done((bf16[1024,256]{1,0:T(8,128)(2,1)S(1)}, bf16[1024,256]{1,0:T(8,128)(2,1)S(1)}, u32[]{:S(2)}, u32[]{:S(2)}) %collective-permute-start.13) | collective-permute-done | bytes 524320 | tf_op jit(solution)/shard_map/ppermute | solution.py:339
  157.2 6.9 %rotated_cols.1 = (f32[2048,64]{1,0:T(8,128)}, bf16[32,64,128]{2,1,0:T(8,128)(2,1)}) custom-call(bf16[2048,2048]{1,0:T(8,128)(2,1)} %all-gather.2.cloned.1.call-done.basis_ref, bf16[8,86,256]{2,1,0:T(8,128)(2,1)} %copy-done.8, bf16[64,64]{1,0:T(8,128)(2,1)} %fusion.13.spread_ref), custom_call_target="tpu_custom_call" | custom-call | flops 536870912 | bytes 8388608 | tf_op jit(solution)/shard_map/rotated_cols/pallas_call | solution.py:174
  164.1 4.4 %all-to-all-start.5 = ((bf16[32,64,128]{2,1,0:T(8,128)(2,1)}), bf16[32,64,128]{2,1,0:T(8,128)(2,1)S(1)}, u32[]{:S(2)}, u32[]{:S(2)}) async-start(bf16[32,64,128]{2,1,0:T(8,128)(2,1)} %get-tuple-element.11), calls=%async_computation.5 | async-start | bytes 1048576 | tf_op jit(solution)/shard_map/all_to_all | solution.py:22
  170.0 8.2 %first_product.1 = (bf16[1024,2048]{1,0:T(8,128)(2,1)}, f32[1024,256]{1,0:T(8,128)}) custom-call(s32[8]{0:T(128)} %and_select_fusion.place_ref, f32[16,256]{1,0:T(8,128)} %reshape.44.told_ref, bf16[2048,256]{1,0:T(8,128)(2,1)} %whiten_ref.1, bf16[1024,256]{1,0:T(8,128)(2,1)} %refs_0_.1, bf16[1024,256]{1,0:T(8,128)(2,1)} %refs_1_.3, ...), custom_call_target="tpu_custom_call" | custom-call | flops 1073741824 | bytes 12582912 | tf_op jit(solution)/shard_map/first_product/pallas_call | solution.py:261
  178.8 2.3 %constant_dynamic-slice_fusion.refs_4_ = bf16[2048,256]{1,0:T(8,128)(2,1)} fusion(bf16[2048,2048]{1,0:T(8,128)(2,1)} %all-gather.2.cloned.1.call-done.basis_ref, s32[]{:T(128)S(6)} %select_n.42), kind=kLoop, calls=%fused_computation.35 | loop fusion | bytes 2097156 | tf_op jit(solution)/shard_map/dynamic_slice | solution.py:386
  181.9 4.6 %undone_copies.1 = bf16[32,64,256]{2,1,0:T(8,128)(2,1)} custom-call(f32[2048,64]{1,0:T(8,128)} %get-tuple-element.10.refs_0_, bf16[32,64,128]{2,1,0:T(8,128)(2,1)} %copy-done.7, f32[64,64]{1,0:T(8,128)} %pad_maximum_fusion.1.refs_2_, f32[64,2048]{1,0:T(8,128)} %divide_select_fusion.refs_3_, bf16[2048,256]{1,0:T(8,128)(2,1)} %constant_dynamic-slice_fusion.refs_4_), custom_call_target="tpu_custom_call" | custom-call | flops 134217728 | bytes 2097152 | tf_op jit(solution)/shard_map/undone_copies/pallas_call | solution.py:227
  186.4 7.4 %all-to-all-start.6 = ((bf16[32,64,256]{2,1,0:T(8,128)(2,1)}), bf16[32,64,256]{2,1,0:T(8,128)(2,1)S(1)}, u32[]{:S(2)}, u32[]{:S(2)}) async-start(bf16[32,64,256]{2,1,0:T(8,128)(2,1)} %undone_copies.1), calls=%async_computation.6 | async-start | bytes 2097152 | tf_op jit(solution)/shard_map/all_to_all | solution.py:22
  193.9 14.0 %multiply_convert_fusion.turned_ref = bf16[1024,2048]{1,0:T(8,128)(2,1)} fusion(bf16[1024,2048]{1,0:T(8,128)(2,1)} %get-tuple-element.9, bf16[2048,2048]{1,0:T(8,128)(2,1)} %all-gather.2.cloned.1.call-done.basis_ref), kind=kOutput, calls=%fused_computation | convolution fusion | flops 8594128896 | bytes 16777216 | tf_op jit(solution)/shard_map/dot_general | solution.py:26
  207.9 3.1 %all-to-all-done.6 = bf16[32,64,256]{2,1,0:T(8,128)(2,1)S(1)} async-done(((bf16[32,64,256]{2,1,0:T(8,128)(2,1)}), bf16[32,64,256]{2,1,0:T(8,128)(2,1)S(1)}, u32[]{:S(2)}, u32[]{:S(2)}) %all-to-all-start.6) | async-done | bytes 1048608 | tf_op jit(solution)/shard_map/all_to_all | solution.py:22
  211.9 6.4 %last_product.1 = bf16[1024,256]{1,0:T(8,128)(2,1)} custom-call(bf16[1024,2048]{1,0:T(8,128)(2,1)} %multiply_convert_fusion.turned_ref, bf16[2048,256]{1,0:T(8,128)(2,1)} %bitcast.23, f32[1024,256]{1,0:T(8,128)} %get-tuple-element.12.running_ref), custom_call_target="tpu_custom_call" | custom-call | flops 1073741824 | bytes 5242880 | tf_op jit(solution)/shard_map/last_product/pallas_call | solution.py:306
  (93 shorter events, 24.7 us)
Async XLA Ops:
  6.5 72.0 %copy-start = (bf16[1024,256]{1,0:T(8,128)(2,1)S(1)}, bf16[1024,256]{1,0:T(8,128)(2,1)}, u32[]{:S(2)}) copy-start(bf16[1024,256]{1,0:T(8,128)(2,1)} %refs_1_.3) | copy-start | bytes 1572868
  6.5 73.0 %copy-start.15 = (f32[2048]{0:T(1024)S(1)}, f32[2048]{0:T(1024)}, u32[]{:S(2)}) copy-start(f32[2048]{0:T(1024)} %param.8) | copy-start | bytes 24580
  6.5 150.6 %all-gather.2.cloned.1.call-start = ((), (), s32[]{:S(2)}) async-start(), calls=%async_computation.7 | async-start | bytes 8650752 | tf_op jit(solution)/shard_map/all_gather | solution.py:362
  27.5 8.6 %collective-permute-start.1 = (bf16[1024,256]{1,0:T(8,128)(2,1)}, bf16[1024,256]{1,0:T(8,128)(2,1)S(1)}, u32[]{:S(2)}, u32[]{:S(2)}) collective-permute-start(bf16[1024,256]{1,0:T(8,128)(2,1)} %refs_0_.1), channel_id=1, source_target_pairs={{0,1},{1,2},{2,3},{3,4},{4,5},{5,6},{6,7},{7,0},{8,15},{9,8},{10,9... | collective-permute-start | bytes 1572872 | tf_op jit(solution)/shard_map/ppermute | solution.py:339
  27.6 14.2 %collective-permute-start.2 = (bf16[1024,256]{1,0:T(8,128)(2,1)}, bf16[1024,256]{1,0:T(8,128)(2,1)S(1)}, u32[]{:S(2)}, u32[]{:S(2)}) collective-permute-start(bf16[1024,256]{1,0:T(8,128)(2,1)} %refs_1_.3), channel_id=1, source_target_pairs={{0,1},{1,2},{2,3},{3,4},{4,5},{5,6},{6,7},{7,0},{8,15},{9,8},{10,9... | collective-permute-start | bytes 1572872 | tf_op jit(solution)/shard_map/ppermute | solution.py:339
  36.1 45.8 %copy-start.2 = (bf16[1024,256]{1,0:T(8,128)(2,1)}, bf16[1024,256]{1,0:T(8,128)(2,1)S(1)}, u32[]{:S(2)}) copy-start(bf16[1024,256]{1,0:T(8,128)(2,1)S(1)} %collective-permute-done.1.refs_3_.refs_2_) | copy-start | bytes 1572868
  36.1 11.3 %collective-permute-start.3 = (bf16[1024,256]{1,0:T(8,128)(2,1)S(1)}, bf16[1024,256]{1,0:T(8,128)(2,1)S(1)}, u32[]{:S(2)}, u32[]{:S(2)}) collective-permute-start(bf16[1024,256]{1,0:T(8,128)(2,1)S(1)} %collective-permute-done.1.refs_3_.refs_2_), channel_id=1, source_target_pairs={{0,1},{1,2},{2,3},{3,4},{4,5},{5,6},{6,7},{7,0},{8,15},{9,8},{10,9... | collective-permute-start | bytes 1572872 | tf_op jit(solution)/shard_map/ppermute | solution.py:339
  41.9 40.1 %copy-start.3 = (bf16[1024,256]{1,0:T(8,128)(2,1)}, bf16[1024,256]{1,0:T(8,128)(2,1)S(1)}, u32[]{:S(2)}) copy-start(bf16[1024,256]{1,0:T(8,128)(2,1)S(1)} %collective-permute-done.2.refs_4_.refs_3_) | copy-start | bytes 1572868
  41.9 11.1 %collective-permute-start.4 = (bf16[1024,256]{1,0:T(8,128)(2,1)S(1)}, bf16[1024,256]{1,0:T(8,128)(2,1)S(1)}, u32[]{:S(2)}, u32[]{:S(2)}) collective-permute-start(bf16[1024,256]{1,0:T(8,128)(2,1)S(1)} %collective-permute-done.2.refs_4_.refs_3_), channel_id=1, source_target_pairs={{0,1},{1,2},{2,3},{3,4},{4,5},{5,6},{6,7},{7,0},{8,15},{9,8},{10,9... | collective-permute-start | bytes 1572872 | tf_op jit(solution)/shard_map/ppermute | solution.py:339
  47.5 34.5 %copy-start.4 = (bf16[1024,256]{1,0:T(8,128)(2,1)}, bf16[1024,256]{1,0:T(8,128)(2,1)S(1)}, u32[]{:S(2)}) copy-start(bf16[1024,256]{1,0:T(8,128)(2,1)S(1)} %collective-permute-done.3.refs_5_.refs_4_) | copy-start | bytes 1572868
  47.5 11.1 %collective-permute-start.5 = (bf16[1024,256]{1,0:T(8,128)(2,1)S(1)}, bf16[1024,256]{1,0:T(8,128)(2,1)S(1)}, u32[]{:S(2)}, u32[]{:S(2)}) collective-permute-start(bf16[1024,256]{1,0:T(8,128)(2,1)S(1)} %collective-permute-done.3.refs_5_.refs_4_), channel_id=1, source_target_pairs={{0,1},{1,2},{2,3},{3,4},{4,5},{5,6},{6,7},{7,0},{8,15},{9,8},{10,9... | collective-permute-start | bytes 1572872 | tf_op jit(solution)/shard_map/ppermute | solution.py:339
  53.0 29.0 %copy-start.5 = (bf16[1024,256]{1,0:T(8,128)(2,1)}, bf16[1024,256]{1,0:T(8,128)(2,1)S(1)}, u32[]{:S(2)}) copy-start(bf16[1024,256]{1,0:T(8,128)(2,1)S(1)} %collective-permute-done.4.refs_6_.refs_5_) | copy-start | bytes 1572868
  53.0 11.3 %collective-permute-start.6 = (bf16[1024,256]{1,0:T(8,128)(2,1)S(1)}, bf16[1024,256]{1,0:T(8,128)(2,1)}, u32[]{:S(2)}, u32[]{:S(2)}) collective-permute-start(bf16[1024,256]{1,0:T(8,128)(2,1)S(1)} %collective-permute-done.4.refs_6_.refs_5_), channel_id=1, source_target_pairs={{0,1},{1,2},{2,3},{3,4},{4,5},{5,6},{6,7},{7,0},{8,15},{9,8},{10,9... | collective-permute-start | bytes 1572872 | tf_op jit(solution)/shard_map/ppermute | solution.py:339
  58.6 28.0 %collective-permute-start.7 = (bf16[1024,256]{1,0:T(8,128)(2,1)S(1)}, bf16[1024,256]{1,0:T(8,128)(2,1)}, u32[]{:S(2)}, u32[]{:S(2)}) collective-permute-start(bf16[1024,256]{1,0:T(8,128)(2,1)S(1)} %collective-permute-done.5.refs_7_.refs_6_), channel_id=1, source_target_pairs={{0,1},{1,2},{2,3},{3,4},{4,5},{5,6},{6,7},{7,0},{8,15},{9,8},{10,9... | collective-permute-start | bytes 1572872 | tf_op jit(solution)/shard_map/ppermute | solution.py:339
  64.3 22.2 %collective-permute-start.8 = (bf16[1024,256]{1,0:T(8,128)(2,1)}, bf16[1024,256]{1,0:T(8,128)(2,1)}, u32[]{:S(2)}, u32[]{:S(2)}) collective-permute-start(bf16[1024,256]{1,0:T(8,128)(2,1)} %collective-permute-done.6.refs_8_.refs_7_), channel_id=1, source_target_pairs={{0,1},{1,2},{2,3},{3,4},{4,5},{5,6},{6,7},{7,0},{8,15},{9,8},{10,9... | collective-permute-start | bytes 1572872 | tf_op jit(solution)/shard_map/ppermute | solution.py:339
  65.9 23.4 %all-to-all-start.3 = ((f32[32,2,256]{2,1,0:T(2,128)}), f32[32,2,256]{2,1,0:T(2,128)S(1)}, u32[]{:S(2)}, u32[]{:S(2)}) async-start(f32[32,2,256]{2,1,0:T(2,128)} %broadcast_in_dim.9), calls=%async_computation.3 | async-start | bytes 131072 | tf_op jit(solution)/shard_map/all_to_all | solution.py:18
  86.6 28.5 %copy-start.14 = (f32[256,64]{0,1:T(8,128)S(1)}, f32[256,64]{0,1:T(8,128)}, u32[]{:S(2)}) copy-start(f32[256,64]{0,1:T(8,128)} %param.7) | copy-start | bytes 196612
  89.3 20.2 %all-to-all-start.1 = ((bf16[32,8,1280]{2,1,0:T(8,128)(2,1)}), bf16[32,8,1280]{2,1,0:T(8,128)(2,1)S(1)}, u32[]{:S(2)}, u32[]{:S(2)}) async-start(bf16[32,8,1280]{2,1,0:T(8,128)(2,1)} %bitcast.22), calls=%async_computation.1 | async-start | bytes 1310720 | tf_op jit(solution)/shard_map/all_to_all | solution.py:22
  110.5 15.6 %all-to-all-start.2 = ((bf16[32,8,1024]{2,1,0:T(8,128)(2,1)}), bf16[32,8,1024]{2,1,0:T(8,128)(2,1)S(1)}, u32[]{:S(2)}, u32[]{:S(2)}) async-start(bf16[32,8,1024]{2,1,0:T(8,128)(2,1)} %gathered_sum.1), calls=%async_computation.2 | async-start | bytes 1048576 | tf_op jit(solution)/shard_map/all_to_all | solution.py:22
  114.6 4.0 %collective-permute-start = (bf16[64,2048]{1,0:T(8,128)(2,1)S(1)}, bf16[64,2048]{1,0:T(8,128)(2,1)S(1)}, u32[]{:S(2)}, u32[]{:S(2)}) collective-permute-start(bf16[64,2048]{1,0:T(8,128)(2,1)S(1)} %bitcast.27), channel_id=1, source_target_pairs={{0,8},{1,9},{2,10},{3,11},{4,12},{5,13},{6,14},{7,15},{8,0},{9,1},... | collective-permute-start | bytes 786440 | tf_op jit(solution)/shard_map/ppermute | solution.py:343
  115.3 18.4 %collective-permute-start.10 = (bf16[1024,256]{1,0:T(8,128)(2,1)}, bf16[1024,256]{1,0:T(8,128)(2,1)S(1)}, u32[]{:S(2)}, u32[]{:S(2)}) collective-permute-start(bf16[1024,256]{1,0:T(8,128)(2,1)} %collective-permute-done.7.refs_1_.refs_8_), channel_id=1, source_target_pairs={{0,1},{1,2},{2,3},{3,4},{4,5},{5,6},{6,7},{7,0},{8,15},{9,8},{10,9... | collective-permute-start | bytes 1572872 | tf_op jit(solution)/shard_map/ppermute | solution.py:339
  118.5 17.9 %collective-permute-start.11 = (bf16[1024,256]{1,0:T(8,128)(2,1)}, bf16[1024,256]{1,0:T(8,128)(2,1)S(1)}, u32[]{:S(2)}, u32[]{:S(2)}) collective-permute-start(bf16[1024,256]{1,0:T(8,128)(2,1)} %collective-permute-done.8.refs_2_.refs_9_), channel_id=1, source_target_pairs={{0,1},{1,2},{2,3},{3,4},{4,5},{5,6},{6,7},{7,0},{8,15},{9,8},{10,9... | collective-permute-start | bytes 1572872 | tf_op jit(solution)/shard_map/ppermute | solution.py:339
  127.2 1.4 collective-permute-start.9
  129.4 27.0 %all-to-all-start.4 = ((bf16[8,86,256]{2,1,0:T(8,128)(2,1)}), bf16[8,86,256]{2,1,0:T(8,128)(2,1)S(1)}, u32[]{:S(2)}, u32[]{:S(2)}) async-start(bf16[8,86,256]{2,1,0:T(8,128)(2,1)} %broadcast_in_dim.10), calls=%async_computation.4 | async-start | bytes 720896 | tf_op jit(solution)/shard_map/all_to_all | solution.py:18
  133.6 30.4 %copy-start.10 = (bf16[1024,256]{1,0:T(8,128)(2,1)}, bf16[1024,256]{1,0:T(8,128)(2,1)S(1)}, u32[]{:S(2)}) copy-start(bf16[1024,256]{1,0:T(8,128)(2,1)S(1)} %collective-permute-done.10.refs_10_) | copy-start | bytes 1572868
  133.7 16.2 %collective-permute-start.12 = (bf16[1024,256]{1,0:T(8,128)(2,1)S(1)}, bf16[1024,256]{1,0:T(8,128)(2,1)S(1)}, u32[]{:S(2)}, u32[]{:S(2)}) collective-permute-start(bf16[1024,256]{1,0:T(8,128)(2,1)S(1)} %collective-permute-done.10.refs_10_), channel_id=1, source_target_pairs={{0,1},{1,2},{2,3},{3,4},{4,5},{5,6},{6,7},{7,0},{8,15},{9,8},{10,9... | collective-permute-start | bytes 1572872 | tf_op jit(solution)/shard_map/ppermute | solution.py:339
  136.4 33.5 %copy-start.11 = (bf16[1024,256]{1,0:T(8,128)(2,1)}, bf16[1024,256]{1,0:T(8,128)(2,1)S(1)}, u32[]{:S(2)}) copy-start(bf16[1024,256]{1,0:T(8,128)(2,1)S(1)} %collective-permute-done.11.refs_11_) | copy-start | bytes 1572868
  136.4 19.1 %collective-permute-start.13 = (bf16[1024,256]{1,0:T(8,128)(2,1)S(1)}, bf16[1024,256]{1,0:T(8,128)(2,1)S(1)}, u32[]{:S(2)}, u32[]{:S(2)}) collective-permute-start(bf16[1024,256]{1,0:T(8,128)(2,1)S(1)} %collective-permute-done.11.refs_11_), channel_id=1, source_target_pairs={{0,1},{1,2},{2,3},{3,4},{4,5},{5,6},{6,7},{7,0},{8,15},{9,8},{10,9... | collective-permute-start | bytes 1572872 | tf_op jit(solution)/shard_map/ppermute | solution.py:339
  149.9 20.0 %collective-permute-start.14 = (bf16[1024,256]{1,0:T(8,128)(2,1)S(1)}, bf16[1024,256]{1,0:T(8,128)(2,1)}, u32[]{:S(2)}, u32[]{:S(2)}) collective-permute-start(bf16[1024,256]{1,0:T(8,128)(2,1)S(1)} %collective-permute-done.12.refs_12_), channel_id=1, source_target_pairs={{0,1},{1,2},{2,3},{3,4},{4,5},{5,6},{6,7},{7,0},{8,15},{9,8},{10,9... | collective-permute-start | bytes 1572872 | tf_op jit(solution)/shard_map/ppermute | solution.py:339
  155.5 14.4 %collective-permute-start.15 = (bf16[1024,256]{1,0:T(8,128)(2,1)S(1)}, bf16[1024,256]{1,0:T(8,128)(2,1)}, u32[]{:S(2)}, u32[]{:S(2)}) collective-permute-start(bf16[1024,256]{1,0:T(8,128)(2,1)S(1)} %collective-permute-done.13.refs_13_), channel_id=1, source_target_pairs={{0,1},{1,2},{2,3},{3,4},{4,5},{5,6},{6,7},{7,0},{8,15},{9,8},{10,9... | collective-permute-start | bytes 1572872 | tf_op jit(solution)/shard_map/ppermute | solution.py:339
  164.1 17.0 %all-to-all-start.5 = ((bf16[32,64,128]{2,1,0:T(8,128)(2,1)}), bf16[32,64,128]{2,1,0:T(8,128)(2,1)S(1)}, u32[]{:S(2)}, u32[]{:S(2)}) async-start(bf16[32,64,128]{2,1,0:T(8,128)(2,1)} %get-tuple-element.11), calls=%async_computation.5 | async-start | bytes 1048576 | tf_op jit(solution)/shard_map/all_to_all | solution.py:22
  186.4 24.5 %all-to-all-start.6 = ((bf16[32,64,256]{2,1,0:T(8,128)(2,1)}), bf16[32,64,256]{2,1,0:T(8,128)(2,1)S(1)}, u32[]{:S(2)}, u32[]{:S(2)}) async-start(bf16[32,64,256]{2,1,0:T(8,128)(2,1)} %undone_copies.1), calls=%async_computation.6 | async-start | bytes 2097152 | tf_op jit(solution)/shard_map/all_to_all | solution.py:22
  (7 other events, 88.4 us)
Sparse Core Ops, SparseCore 0:
  27.6 56.6 all-gather.1

commit v9 on v7

--- a/solution.py
+++ b/solution.py
@@ -128,14 +128,15 @@
         value = jnp.concatenate(pair, axis=1).astype(BF16)
 
         def store(i, carry):
-            out_ref[i] = value
+            out_ref[2 * i] = value[:, : half * width]
+            out_ref[2 * i + 1] = value[:, half * width :]
             return carry
 
-        lax.fori_loop(0, groups, store, 0)
-
-    return pl.pallas_call(
-        body,
-        out_shape=jax.ShapeDtypeStruct((groups, few, 2 * half * width), BF16),
+        lax.fori_loop(0, groups // 2, store, 0)
+
+    return pl.pallas_call(
+        body,
+        out_shape=jax.ShapeDtypeStruct((groups, few, half * width), BF16),
         in_specs=[VMEM],
         out_specs=VMEM,
         compiler_params=params(SMALL),
@@ -221,7 +222,7 @@
         out_shape=jax.ShapeDtypeStruct((groups, narrow, width), BF16),
         in_specs=[VMEM] * 5,
         out_specs=VMEM,
-        compiler_params=params(),
+        compiler_params=params(SMALL),
         cost_estimate=cost(4 * dim * narrow * width, 4 * dim * width),
         name="undone_copies",
     )(rot, back, spread, kernel_t, basis)
@@ -266,28 +267,6 @@
     )(places, told, whiten, *flat)
 
 
-def last_product(turned, undone, running):
-    n, dim = turned.shape
-    width = undone.shape[1]
-    rows = 256
-
-    def body(turned_ref, undone_ref, running_ref, out_ref):
-        value = running_ref[...] + product(turned_ref[...], undone_ref[...])
-        out_ref[...] = value.astype(BF16)
-
-    part = lambda cols: pl.BlockSpec((rows, cols), lambda i: (i, 0))
-    return pl.pallas_call(
-        body,
-        out_shape=jax.ShapeDtypeStruct((n, width), BF16),
-        grid=(n // rows,),
-        in_specs=[part(dim), pl.BlockSpec((dim, width), lambda i: (0, 0)), part(width)],
-        out_specs=part(width),
-        compiler_params=params(),
-        cost_estimate=cost(2 * n * dim * width, 2 * n * dim + 2 * dim * width),
-        name="last_product",
-    )(turned, undone, running)
-
-
 def local(features, grad_out, eigvecs, eigvals, whiten):
     n, width = features.shape
     groups, planes = lax.axis_size("rows"), lax.axis_size("feat")
@@ -306,6 +285,10 @@
         ]
         return lax.ppermute(value, ("rows", "feat"), pairs)
 
+    def swap(value):
+        pairs = [(a * planes + b, (a ^ 1) * planes + b) for a in range(groups) for b in range(planes)]
+        return lax.ppermute(value, ("rows", "feat"), pairs)
+
     blocks = [(grad_out, features)]
     for _ in range(1, planes):
         grads = pass_on(blocks[-1][0])
@@ -322,6 +305,7 @@
 
     basis_rt = copy_for_each(eigvecs.astype(BF16).T, "feat")
     basis_rt = jnp.swapaxes(basis_rt, 0, 1).reshape(narrow, dim)
+    both = jnp.concatenate([basis_rt, swap(basis_rt)])
     basis_t = lax.all_gather(basis_rt, "rows", axis=0, tiled=True)
 
     own = jnp.concatenate([features.T, grad_out.T], axis=1)
@@ -330,11 +314,12 @@
 
     got = exchange(mixed.reshape(groups, width // groups, -1), "rows")
     copies = gathered_sum(got, width, half)
-    gram = exchange(copies, "rows").reshape(width, dim)
-
-    twice = jnp.concatenate([basis_rt, basis_rt], axis=1)
-    turned = lax.dynamic_slice_in_dim(twice, f * width, dim, axis=1)
-    right = contract_last(turned, gram).astype(BF16)
+    gram = exchange(copies, "rows").reshape(width, half * width)
+
+    twice = jnp.concatenate([both, both], axis=1)
+    turned = lax.dynamic_slice_in_dim(twice, f * width + (r % 2) * half * width, half * width, axis=1)
+    right = contract_last(turned, gram)
+    right = (right[:narrow] + swap(right[narrow:])).astype(BF16)
     shared = copy_for_each(jnp.concatenate([right, spread, *three_parts(means)]), "feat")
     spread = jnp.sum(shared[:, narrow : narrow + few].astype(F32), axis=0)
     spread = jnp.concatenate(
@@ -354,7 +339,7 @@
     told = jnp.sum(told, axis=1).reshape(2 * planes, width)
     centered, running = first_product(places, told, whiten, blocks)
     turned = (contract_last(centered, basis_t) * (1.0 / total)).astype(BF16)
-    return last_product(turned, undone, running)
+    return (running + product(lax.optimization_barrier(turned), undone)).astype(BF16)
 
 
 def solution(mesh):

time: 230 us -> 219 us (0.952)
  Pallas kernels: 33.3 us -> 26.1 us
  waiting for transfers between devices: 73.8 us -> 68.9 us
  matrix products: 14.6 us -> 18.7 us
  local copies, waits for them, and re-layouts: 10 us -> 7.34 us
    pallas_call x2 -> x1, Pallas kernels: 6.56 us -> 1.07 us  [gathered_sum(): pl.pallas_call(body, out_shape=jax.ShapeDtypeStruct((groups, few, half *...]
    all_to_all x4, waiting for transfers between devices: 29.2 us -> 23.7 us  [exchange(): return lax.all_to_all(parts, axis, split_axis=0, concat_axis=0, tiled=True)]
    dot_general x0 -> x1, matrix products: none -> 3.44 us  [product(): return jnp.dot(a, b, preferred_element_type=F32)]
    unnamed x34 -> x30, local copies, waits for them, and re-layouts: 4.89 us -> 3.13 us
  transfers between devices with their start and end apart: 21 -> 23, of which waited for: 11 -> 13; matrix products, arithmetic and copies ran while one was open for 13% -> 13% of each run, Pallas kernels for 10% -> 11%
where the time goes in v9:
time: 219 us; the launch traced here: 218 us
  waiting for transfers between devices  68.9 us (31%)
  starting transfers between devices  55 us (25%)
  Pallas kernels  26.1 us (12%)
  blocking collectives  19.3 us (9%)
  matrix products  18.7 us (9%)
  between operations  13.7 us (6%)
  other arithmetic  8.99 us (4%)
  local copies, waits for them, and re-layouts  7.34 us (3%)
    ppermute x14, waiting for transfers between devices, pass_on(): return lax.ppermute(value, ('rows', 'feat'), pairs)  44.3 us
    all_to_all x4, waiting for transfers between devices, exchange(): return lax.all_to_all(parts, axis, split_axis=0, concat_axis=0, tiled=True)  23.7 us
    all_to_all x4, starting transfers between devices, exchange(): return lax.all_to_all(parts, axis, split_axis=0, concat_axis=0, tiled=True)  22.8 us
    all_to_all x1, blocking collectives, copy_for_each(): return lax.all_to_all(copies, axis, split_axis=0, concat_axis=0, tiled=True)  19.3 us
    ppermute x14, starting transfers between devices, pass_on(): return lax.ppermute(value, ('rows', 'feat'), pairs)  16.4 us
    dot_general x2, matrix products, contract_last(): lax.dot_general(a, b, (((1,), (1,)), ((), ())), preferred_element_type=F32)  15 us
    all_to_all x2, starting transfers between devices, copy_for_each(): return lax.all_to_all(copies, axis, split_axis=0, concat_axis=0, tiled=True)  14.8 us
    pallas_call x1, Pallas kernels, first_product(): pl.pallas_call(body, out_shape=[jax.ShapeDtypeStruct((n, dim), BF16), jax...  8.33 us
  transfers between devices with their start and end apart: 23, of which 13 were waited for; matrix products, arithmetic and copies ran while one was open for 13% of the time, Pallas kernels for 11%

profile of v9, /device:TPU:1, one launch (start us, length us, event | category | flops | bytes accessed | tf_op | source)
XLA Modules:
  0.0 217.9 jit_solution(13866807364020239866)
XLA Ops:
  7.5 19.3 %all_to_all.35 = bf16[8,64,256]{2,1,0:T(8,128)(2,1)S(1)} all-to-all(bf16[8,64,256]{2,1,0:T(8,128)(2,1)S(1)} %broadcast_in_dim.8), channel_id=1, replica_groups=mesh['rows'=32,'feat'=8] {'feat'}, dimensions={0} | all-to-all | bytes 524288 | tf_op jit(solution)/shard_map/all_to_all | solution.py:18
  27.6 1.6 collective-permute-start.2
  29.2 6.9 %collective-permute-done.1.refs_3_.refs_2_ = bf16[1024,256]{1,0:T(8,128)(2,1)S(1)} collective-permute-done((bf16[1024,256]{1,0:T(8,128)(2,1)}, bf16[1024,256]{1,0:T(8,128)(2,1)S(1)}, u32[]{:S(2)}, u32[]{:S(2)}) %collective-permute-start.1) | collective-permute-done | bytes 524320 | tf_op jit(solution)/shard_map/ppermute | solution.py:286
  37.0 4.8 %collective-permute-done.2.refs_4_.refs_3_ = bf16[1024,256]{1,0:T(8,128)(2,1)S(1)} collective-permute-done((bf16[1024,256]{1,0:T(8,128)(2,1)}, bf16[1024,256]{1,0:T(8,128)(2,1)S(1)}, u32[]{:S(2)}, u32[]{:S(2)}) %collective-permute-start.2) | collective-permute-done | bytes 524320 | tf_op jit(solution)/shard_map/ppermute | solution.py:286
  42.7 4.8 %collective-permute-done.3.refs_5_.refs_4_ = bf16[1024,256]{1,0:T(8,128)(2,1)S(1)} collective-permute-done((bf16[1024,256]{1,0:T(8,128)(2,1)S(1)}, bf16[1024,256]{1,0:T(8,128)(2,1)S(1)}, u32[]{:S(2)}, u32[]{:S(2)}) %collective-permute-start.3) | collective-permute-done | bytes 524320 | tf_op jit(solution)/shard_map/ppermute | solution.py:286
  48.3 4.7 %collective-permute-done.4.refs_6_.refs_5_ = bf16[1024,256]{1,0:T(8,128)(2,1)S(1)} collective-permute-done((bf16[1024,256]{1,0:T(8,128)(2,1)S(1)}, bf16[1024,256]{1,0:T(8,128)(2,1)S(1)}, u32[]{:S(2)}, u32[]{:S(2)}) %collective-permute-start.4) | collective-permute-done | bytes 524320 | tf_op jit(solution)/shard_map/ppermute | solution.py:286
  53.0 1.3 collective-permute-start.6
  56.7 1.9 collective-permute-done.5.refs_7_.refs_6_
  59.5 4.8 %collective-permute-done.6.refs_8_.refs_7_ = bf16[1024,256]{1,0:T(8,128)(2,1)} collective-permute-done((bf16[1024,256]{1,0:T(8,128)(2,1)S(1)}, bf16[1024,256]{1,0:T(8,128)(2,1)}, u32[]{:S(2)}, u32[]{:S(2)}) %collective-permute-start.6) | collective-permute-done | bytes 524320 | tf_op jit(solution)/shard_map/ppermute | solution.py:286
  65.9 10.6 %all-to-all-start.3 = ((f32[32,2,256]{2,1,0:T(2,128)}), f32[32,2,256]{2,1,0:T(2,128)S(1)}, u32[]{:S(2)}, u32[]{:S(2)}) async-start(f32[32,2,256]{2,1,0:T(2,128)} %broadcast_in_dim.9), calls=%async_computation.3 | async-start | bytes 131072 | tf_op jit(solution)/shard_map/all_to_all | solution.py:18
  76.5 2.1 copy.20
  79.6 2.3 %pad_maximum_fusion.refs_0_ = bf16[256,2048]{1,0:T(8,128)(2,1)} fusion(bf16[256,1024]{1,0:T(8,128)(2,1)} %bitcast.25, bf16[256,1024]{1,0:T(8,128)(2,1)} %bitcast.26), kind=kLoop, calls=%fused_computation.6 | loop fusion | flops 2097152 | bytes 2097152 | tf_op jit(solution)/shard_map/concatenate | solution.py:311
  82.0 4.6 %gram_first.1.partial_ref = bf16[256,1280]{1,0:T(8,128)(2,1)} custom-call(bf16[256,2048]{1,0:T(8,128)(2,1)} %pad_maximum_fusion.refs_0_, bf16[1024,256]{1,0:T(8,128)(2,1)} %refs_0_.1, bf16[1024,256]{1,0:T(8,128)(2,1)} %refs_1_.3, bf16[1024,256]{1,0:T(8,128)(2,1)} %copy-done.2, bf16[1024,256]{1,0:T(8,128)(2,1)} %copy-done.3, bf16[1024,256]{1,0:T(8,128)(2,1)} %copy-done.4, ...), custom_call_target="tpu_custom_call" | custom-call | flops 1073741824 | bytes 5242880 | tf_op jit(solution)/shard_map/gram_first/pallas_call | solution.py:83
  86.6 2.7 %gram_last.1 = bf16[256,1280]{1,0:T(8,128)(2,1)} custom-call(bf16[256,1280]{1,0:T(8,128)(2,1)} %gram_first.1.partial_ref, bf16[256,2048]{1,0:T(8,128)(2,1)} %pad_maximum_fusion.refs_0_, bf16[1024,256]{1,0:T(8,128)(2,1)} %collective-permute-done.7.refs_1_.refs_8_, bf16[1024,256]{1,0:T(8,128)(2,1)} %collective-permute-done.8.refs_2_.refs_9_), custom_call_target="tpu_custom_call", output_to_operand_aliasing={{}: (0, {})} | custom-call | flops 268435456 | bytes 2097152 | tf_op jit(solution)/shard_map/gram_last/pallas_call | solution.py:101
  89.3 7.4 %all-to-all-start.1 = ((bf16[32,8,1280]{2,1,0:T(8,128)(2,1)}), bf16[32,8,1280]{2,1,0:T(8,128)(2,1)S(1)}, u32[]{:S(2)}, u32[]{:S(2)}) async-start(bf16[32,8,1280]{2,1,0:T(8,128)(2,1)} %bitcast.24), calls=%async_computation.1 | async-start | bytes 1310720 | tf_op jit(solution)/shard_map/all_to_all | solution.py:22
  96.7 12.7 %all-to-all-done.1.got_ref = bf16[32,8,1280]{2,1,0:T(8,128)(2,1)S(1)} async-done(((bf16[32,8,1280]{2,1,0:T(8,128)(2,1)}), bf16[32,8,1280]{2,1,0:T(8,128)(2,1)S(1)}, u32[]{:S(2)}, u32[]{:S(2)}) %all-to-all-start.1) | async-done | bytes 655392 | tf_op jit(solution)/shard_map/all_to_all | solution.py:22
  110.6 4.0 %all-to-all-start.2 = ((bf16[32,8,1024]{2,1,0:T(8,128)(2,1)}), bf16[32,8,1024]{2,1,0:T(8,128)(2,1)S(1)}, u32[]{:S(2)}, u32[]{:S(2)}) async-start(bf16[32,8,1024]{2,1,0:T(8,128)(2,1)} %gathered_sum.1), calls=%async_computation.2 | async-start | bytes 1048576 | tf_op jit(solution)/shard_map/all_to_all | solution.py:22
  115.3 3.2 %collective-permute-start.10 = (bf16[1024,256]{1,0:T(8,128)(2,1)}, bf16[1024,256]{1,0:T(8,128)(2,1)S(1)}, u32[]{:S(2)}, u32[]{:S(2)}) collective-permute-start(bf16[1024,256]{1,0:T(8,128)(2,1)} %collective-permute-done.7.refs_1_.refs_8_), channel_id=1, source_target_pairs={{0,1},{1,2},{2,3},{3,4},{4,5},{5,6},{6,7},{7,0},{8,15},{9,8},{10,9... | collective-permute-start | bytes 1572872 | tf_op jit(solution)/shard_map/ppermute | solution.py:286
  118.6 7.6 %all-to-all-done.2 = bf16[32,8,1024]{2,1,0:T(8,128)(2,1)S(1)} async-done(((bf16[32,8,1024]{2,1,0:T(8,128)(2,1)}), bf16[32,8,1024]{2,1,0:T(8,128)(2,1)S(1)}, u32[]{:S(2)}, u32[]{:S(2)}) %all-to-all-start.2) | async-done | bytes 524320 | tf_op jit(solution)/shard_map/all_to_all | solution.py:22
  129.4 4.2 %all-to-all-start.4 = ((bf16[8,86,256]{2,1,0:T(8,128)(2,1)}), bf16[8,86,256]{2,1,0:T(8,128)(2,1)S(1)}, u32[]{:S(2)}, u32[]{:S(2)}) async-start(bf16[8,86,256]{2,1,0:T(8,128)(2,1)} %broadcast_in_dim.10), calls=%async_computation.4 | async-start | bytes 720896 | tf_op jit(solution)/shard_map/all_to_all | solution.py:18
  133.7 2.7 %collective-permute-start.12 = (bf16[1024,256]{1,0:T(8,128)(2,1)S(1)}, bf16[1024,256]{1,0:T(8,128)(2,1)}, u32[]{:S(2)}, u32[]{:S(2)}) collective-permute-start(bf16[1024,256]{1,0:T(8,128)(2,1)S(1)} %collective-permute-done.10.refs_10_), channel_id=1, source_target_pairs={{0,1},{1,2},{2,3},{3,4},{4,5},{5,6},{6,7},{7,0},{8,15},{9,8},{10,9... | collective-permute-start | bytes 1572872 | tf_op jit(solution)/shard_map/ppermute | solution.py:286
  138.4 11.6 %collective-permute-done.12.refs_12_ = bf16[1024,256]{1,0:T(8,128)(2,1)} collective-permute-done((bf16[1024,256]{1,0:T(8,128)(2,1)S(1)}, bf16[1024,256]{1,0:T(8,128)(2,1)}, u32[]{:S(2)}, u32[]{:S(2)}) %collective-permute-start.12) | collective-permute-done | bytes 524320 | tf_op jit(solution)/shard_map/ppermute | solution.py:286
  150.9 4.7 %collective-permute-done.13.refs_13_ = bf16[1024,256]{1,0:T(8,128)(2,1)} collective-permute-done((bf16[1024,256]{1,0:T(8,128)(2,1)S(1)}, bf16[1024,256]{1,0:T(8,128)(2,1)}, u32[]{:S(2)}, u32[]{:S(2)}) %collective-permute-start.13) | collective-permute-done | bytes 524320 | tf_op jit(solution)/shard_map/ppermute | solution.py:286
  157.3 6.8 %rotated_cols.1 = (f32[2048,64]{1,0:T(8,128)}, bf16[32,64,128]{2,1,0:T(8,128)(2,1)}) custom-call(bf16[2048,2048]{1,0:T(8,128)(2,1)} %all-gather.2.cloned.1.call-done.basis_ref, bf16[8,86,256]{2,1,0:T(8,128)(2,1)} %copy-done.7, bf16[64,64]{1,0:T(8,128)(2,1)} %fusion.13.spread_ref), custom_call_target="tpu_custom_call" | custom-call | flops 536870912 | bytes 8388608 | tf_op jit(solution)/shard_map/rotated_cols/pallas_call | solution.py:174
  164.1 4.3 %all-to-all-start.5 = ((bf16[32,64,128]{2,1,0:T(8,128)(2,1)}), bf16[32,64,128]{2,1,0:T(8,128)(2,1)S(1)}, u32[]{:S(2)}, u32[]{:S(2)}) async-start(bf16[32,64,128]{2,1,0:T(8,128)(2,1)} %get-tuple-element.12), calls=%async_computation.5 | async-start | bytes 1048576 | tf_op jit(solution)/shard_map/all_to_all | solution.py:22
  169.9 8.3 %first_product.1 = (bf16[1024,2048]{1,0:T(8,128)(2,1)}, f32[1024,256]{1,0:T(8,128)}) custom-call(s32[8]{0:T(128)} %and_select_fusion.place_ref, f32[16,256]{1,0:T(8,128)} %reshape.44.told_ref, bf16[2048,256]{1,0:T(8,128)(2,1)} %whiten_ref.1, bf16[1024,256]{1,0:T(8,128)(2,1)} %refs_0_.1, bf16[1024,256]{1,0:T(8,128)(2,1)} %refs_1_.3, ...), custom_call_target="tpu_custom_call" | custom-call | flops 1073741824 | bytes 12582912 | tf_op jit(solution)/shard_map/first_product/pallas_call | solution.py:252
  178.3 1.3 constant_dynamic-slice_fusion.basis_ref
  179.9 2.6 %undone_copies.1 = bf16[32,64,256]{2,1,0:T(8,128)(2,1)} custom-call(f32[2048,64]{1,0:T(8,128)S(1)} %copy-done, bf16[32,64,128]{2,1,0:T(8,128)(2,1)S(1)} %all-to-all-done.5.back_ref, f32[64,64]{1,0:T(8,128)S(1)} %pad_maximum_fusion.1.spread_ref, f32[64,2048]{1,0:T(8,128)S(1)} %divide_select_fusion.kernel_ref, ...), custom_call_target="tpu_custom_call" | custom-call | flops 134217728 | bytes 2097152 | tf_op jit(solution)/shard_map/undone_copies/pallas_call | solution.py:220
  182.6 7.1 %all-to-all-start.6 = ((bf16[32,64,256]{2,1,0:T(8,128)(2,1)}), bf16[32,64,256]{2,1,0:T(8,128)(2,1)S(1)}, u32[]{:S(2)}, u32[]{:S(2)}) async-start(bf16[32,64,256]{2,1,0:T(8,128)(2,1)} %undone_copies.1), calls=%async_computation.6 | async-start | bytes 2097152 | tf_op jit(solution)/shard_map/all_to_all | solution.py:22
  189.6 14.0 %multiply_convert_fusion = bf16[1024,2048]{1,0:T(8,128)(2,1)} fusion(bf16[1024,2048]{1,0:T(8,128)(2,1)} %get-tuple-element.10, bf16[2048,2048]{1,0:T(8,128)(2,1)} %all-gather.2.cloned.1.call-done.basis_ref), kind=kOutput, calls=%fused_computation | convolution fusion | flops 8594128896 | bytes 16777216 | tf_op jit(solution)/shard_map/dot_general | solution.py:26
  203.6 3.1 %all-to-all-done.6 = bf16[32,64,256]{2,1,0:T(8,128)(2,1)S(1)} async-done(((bf16[32,64,256]{2,1,0:T(8,128)(2,1)}), bf16[32,64,256]{2,1,0:T(8,128)(2,1)S(1)}, u32[]{:S(2)}, u32[]{:S(2)}) %all-to-all-start.6) | async-done | bytes 1048608 | tf_op jit(solution)/shard_map/all_to_all | solution.py:22
  206.7 3.4 %fusion.16 = f32[1024,256]{1,0:T(8,128)S(1)} fusion(bf16[1024,2048]{1,0:T(8,128)(2,1)} %multiply_convert_fusion, bf16[2048,256]{1,0:T(8,128)(2,1)S(1)} %bitcast.27), kind=kOutput, calls=%fused_computation.47 | convolution fusion | flops 1073741824 | bytes 6291456 | tf_op jit(solution)/shard_map/dot_general | solution.py:30
  (90 shorter events, 22.7 us)
Async XLA Ops:
  6.5 72.0 %copy-start.1 = (bf16[1024,256]{1,0:T(8,128)(2,1)S(1)}, bf16[1024,256]{1,0:T(8,128)(2,1)}, u32[]{:S(2)}) copy-start(bf16[1024,256]{1,0:T(8,128)(2,1)} %refs_1_.3) | copy-start | bytes 1572868
  6.5 73.0 %copy-start.13 = (f32[2048]{0:T(1024)S(1)}, f32[2048]{0:T(1024)}, u32[]{:S(2)}) copy-start(f32[2048]{0:T(1024)} %param.8) | copy-start | bytes 24580
  6.5 150.7 %all-gather.2.cloned.1.call-start = ((), (), s32[]{:S(2)}) async-start(), calls=%async_computation.7 | async-start | bytes 8650752 | tf_op jit(solution)/shard_map/all_gather | solution.py:309
  27.5 8.6 %collective-permute-start.1 = (bf16[1024,256]{1,0:T(8,128)(2,1)}, bf16[1024,256]{1,0:T(8,128)(2,1)S(1)}, u32[]{:S(2)}, u32[]{:S(2)}) collective-permute-start(bf16[1024,256]{1,0:T(8,128)(2,1)} %refs_0_.1), channel_id=1, source_target_pairs={{0,1},{1,2},{2,3},{3,4},{4,5},{5,6},{6,7},{7,0},{8,15},{9,8},{10,9... | collective-permute-start | bytes 1572872 | tf_op jit(solution)/shard_map/ppermute | solution.py:286
  27.6 14.2 %collective-permute-start.2 = (bf16[1024,256]{1,0:T(8,128)(2,1)}, bf16[1024,256]{1,0:T(8,128)(2,1)S(1)}, u32[]{:S(2)}, u32[]{:S(2)}) collective-permute-start(bf16[1024,256]{1,0:T(8,128)(2,1)} %refs_1_.3), channel_id=1, source_target_pairs={{0,1},{1,2},{2,3},{3,4},{4,5},{5,6},{6,7},{7,0},{8,15},{9,8},{10,9... | collective-permute-start | bytes 1572872 | tf_op jit(solution)/shard_map/ppermute | solution.py:286
  36.1 45.8 %copy-start.2 = (bf16[1024,256]{1,0:T(8,128)(2,1)}, bf16[1024,256]{1,0:T(8,128)(2,1)S(1)}, u32[]{:S(2)}) copy-start(bf16[1024,256]{1,0:T(8,128)(2,1)S(1)} %collective-permute-done.1.refs_3_.refs_2_) | copy-start | bytes 1572868
  36.1 11.3 %collective-permute-start.3 = (bf16[1024,256]{1,0:T(8,128)(2,1)S(1)}, bf16[1024,256]{1,0:T(8,128)(2,1)S(1)}, u32[]{:S(2)}, u32[]{:S(2)}) collective-permute-start(bf16[1024,256]{1,0:T(8,128)(2,1)S(1)} %collective-permute-done.1.refs_3_.refs_2_), channel_id=1, source_target_pairs={{0,1},{1,2},{2,3},{3,4},{4,5},{5,6},{6,7},{7,0},{8,15},{9,8},{10,9... | collective-permute-start | bytes 1572872 | tf_op jit(solution)/shard_map/ppermute | solution.py:286
  41.8 40.1 %copy-start.3 = (bf16[1024,256]{1,0:T(8,128)(2,1)}, bf16[1024,256]{1,0:T(8,128)(2,1)S(1)}, u32[]{:S(2)}) copy-start(bf16[1024,256]{1,0:T(8,128)(2,1)S(1)} %collective-permute-done.2.refs_4_.refs_3_) | copy-start | bytes 1572868
  41.8 11.1 %collective-permute-start.4 = (bf16[1024,256]{1,0:T(8,128)(2,1)S(1)}, bf16[1024,256]{1,0:T(8,128)(2,1)S(1)}, u32[]{:S(2)}, u32[]{:S(2)}) collective-permute-start(bf16[1024,256]{1,0:T(8,128)(2,1)S(1)} %collective-permute-done.2.refs_4_.refs_3_), channel_id=1, source_target_pairs={{0,1},{1,2},{2,3},{3,4},{4,5},{5,6},{6,7},{7,0},{8,15},{9,8},{10,9... | collective-permute-start | bytes 1572872 | tf_op jit(solution)/shard_map/ppermute | solution.py:286
  47.5 34.5 %copy-start.4 = (bf16[1024,256]{1,0:T(8,128)(2,1)}, bf16[1024,256]{1,0:T(8,128)(2,1)S(1)}, u32[]{:S(2)}) copy-start(bf16[1024,256]{1,0:T(8,128)(2,1)S(1)} %collective-permute-done.3.refs_5_.refs_4_) | copy-start | bytes 1572868
  47.5 11.1 %collective-permute-start.5 = (bf16[1024,256]{1,0:T(8,128)(2,1)S(1)}, bf16[1024,256]{1,0:T(8,128)(2,1)S(1)}, u32[]{:S(2)}, u32[]{:S(2)}) collective-permute-start(bf16[1024,256]{1,0:T(8,128)(2,1)S(1)} %collective-permute-done.3.refs_5_.refs_4_), channel_id=1, source_target_pairs={{0,1},{1,2},{2,3},{3,4},{4,5},{5,6},{6,7},{7,0},{8,15},{9,8},{10,9... | collective-permute-start | bytes 1572872 | tf_op jit(solution)/shard_map/ppermute | solution.py:286
  53.0 29.0 %copy-start.5 = (bf16[1024,256]{1,0:T(8,128)(2,1)}, bf16[1024,256]{1,0:T(8,128)(2,1)S(1)}, u32[]{:S(2)}) copy-start(bf16[1024,256]{1,0:T(8,128)(2,1)S(1)} %collective-permute-done.4.refs_6_.refs_5_) | copy-start | bytes 1572868
  53.0 11.3 %collective-permute-start.6 = (bf16[1024,256]{1,0:T(8,128)(2,1)S(1)}, bf16[1024,256]{1,0:T(8,128)(2,1)}, u32[]{:S(2)}, u32[]{:S(2)}) collective-permute-start(bf16[1024,256]{1,0:T(8,128)(2,1)S(1)} %collective-permute-done.4.refs_6_.refs_5_), channel_id=1, source_target_pairs={{0,1},{1,2},{2,3},{3,4},{4,5},{5,6},{6,7},{7,0},{8,15},{9,8},{10,9... | collective-permute-start | bytes 1572872 | tf_op jit(solution)/shard_map/ppermute | solution.py:286
  58.6 28.0 %collective-permute-start.7 = (bf16[1024,256]{1,0:T(8,128)(2,1)S(1)}, bf16[1024,256]{1,0:T(8,128)(2,1)}, u32[]{:S(2)}, u32[]{:S(2)}) collective-permute-start(bf16[1024,256]{1,0:T(8,128)(2,1)S(1)} %collective-permute-done.5.refs_7_.refs_6_), channel_id=1, source_target_pairs={{0,1},{1,2},{2,3},{3,4},{4,5},{5,6},{6,7},{7,0},{8,15},{9,8},{10,9... | collective-permute-start | bytes 1572872 | tf_op jit(solution)/shard_map/ppermute | solution.py:286
  64.3 22.3 %collective-permute-start.8 = (bf16[1024,256]{1,0:T(8,128)(2,1)}, bf16[1024,256]{1,0:T(8,128)(2,1)}, u32[]{:S(2)}, u32[]{:S(2)}) collective-permute-start(bf16[1024,256]{1,0:T(8,128)(2,1)} %collective-permute-done.6.refs_8_.refs_7_), channel_id=1, source_target_pairs={{0,1},{1,2},{2,3},{3,4},{4,5},{5,6},{6,7},{7,0},{8,15},{9,8},{10,9... | collective-permute-start | bytes 1572872 | tf_op jit(solution)/shard_map/ppermute | solution.py:286
  65.9 23.4 %all-to-all-start.3 = ((f32[32,2,256]{2,1,0:T(2,128)}), f32[32,2,256]{2,1,0:T(2,128)S(1)}, u32[]{:S(2)}, u32[]{:S(2)}) async-start(f32[32,2,256]{2,1,0:T(2,128)} %broadcast_in_dim.9), calls=%async_computation.3 | async-start | bytes 131072 | tf_op jit(solution)/shard_map/all_to_all | solution.py:18
  86.6 28.5 %copy-start.12 = (f32[256,64]{0,1:T(8,128)S(1)}, f32[256,64]{0,1:T(8,128)}, u32[]{:S(2)}) copy-start(f32[256,64]{0,1:T(8,128)} %param.7) | copy-start | bytes 196612
  89.3 20.2 %all-to-all-start.1 = ((bf16[32,8,1280]{2,1,0:T(8,128)(2,1)}), bf16[32,8,1280]{2,1,0:T(8,128)(2,1)S(1)}, u32[]{:S(2)}, u32[]{:S(2)}) async-start(bf16[32,8,1280]{2,1,0:T(8,128)(2,1)} %bitcast.24), calls=%async_computation.1 | async-start | bytes 1310720 | tf_op jit(solution)/shard_map/all_to_all | solution.py:22
  110.6 15.6 %all-to-all-start.2 = ((bf16[32,8,1024]{2,1,0:T(8,128)(2,1)}), bf16[32,8,1024]{2,1,0:T(8,128)(2,1)S(1)}, u32[]{:S(2)}, u32[]{:S(2)}) async-start(bf16[32,8,1024]{2,1,0:T(8,128)(2,1)} %gathered_sum.1), calls=%async_computation.2 | async-start | bytes 1048576 | tf_op jit(solution)/shard_map/all_to_all | solution.py:22
  114.6 4.0 %collective-permute-start = (bf16[64,2048]{1,0:T(8,128)(2,1)S(1)}, bf16[64,2048]{1,0:T(8,128)(2,1)S(1)}, u32[]{:S(2)}, u32[]{:S(2)}) collective-permute-start(bf16[64,2048]{1,0:T(8,128)(2,1)S(1)} %bitcast.29), channel_id=1, source_target_pairs={{0,8},{1,9},{2,10},{3,11},{4,12},{5,13},{6,14},{7,15},{8,0},{9,1},... | collective-permute-start | bytes 786440 | tf_op jit(solution)/shard_map/ppermute | solution.py:290
  115.3 18.4 %collective-permute-start.10 = (bf16[1024,256]{1,0:T(8,128)(2,1)}, bf16[1024,256]{1,0:T(8,128)(2,1)S(1)}, u32[]{:S(2)}, u32[]{:S(2)}) collective-permute-start(bf16[1024,256]{1,0:T(8,128)(2,1)} %collective-permute-done.7.refs_1_.refs_8_), channel_id=1, source_target_pairs={{0,1},{1,2},{2,3},{3,4},{4,5},{5,6},{6,7},{7,0},{8,15},{9,8},{10,9... | collective-permute-start | bytes 1572872 | tf_op jit(solution)/shard_map/ppermute | solution.py:286
  118.5 17.9 %collective-permute-start.11 = (bf16[1024,256]{1,0:T(8,128)(2,1)}, bf16[1024,256]{1,0:T(8,128)(2,1)S(1)}, u32[]{:S(2)}, u32[]{:S(2)}) collective-permute-start(bf16[1024,256]{1,0:T(8,128)(2,1)} %collective-permute-done.8.refs_2_.refs_9_), channel_id=1, source_target_pairs={{0,1},{1,2},{2,3},{3,4},{4,5},{5,6},{6,7},{7,0},{8,15},{9,8},{10,9... | collective-permute-start | bytes 1572872 | tf_op jit(solution)/shard_map/ppermute | solution.py:286
  127.2 1.4 collective-permute-start.9
  129.4 27.1 %all-to-all-start.4 = ((bf16[8,86,256]{2,1,0:T(8,128)(2,1)}), bf16[8,86,256]{2,1,0:T(8,128)(2,1)S(1)}, u32[]{:S(2)}, u32[]{:S(2)}) async-start(bf16[8,86,256]{2,1,0:T(8,128)(2,1)} %broadcast_in_dim.10), calls=%async_computation.4 | async-start | bytes 720896 | tf_op jit(solution)/shard_map/all_to_all | solution.py:18
  133.7 30.5 %copy-start.10 = (bf16[1024,256]{1,0:T(8,128)(2,1)}, bf16[1024,256]{1,0:T(8,128)(2,1)S(1)}, u32[]{:S(2)}) copy-start(bf16[1024,256]{1,0:T(8,128)(2,1)S(1)} %collective-permute-done.10.refs_10_) | copy-start | bytes 1572868
  133.7 16.3 %collective-permute-start.12 = (bf16[1024,256]{1,0:T(8,128)(2,1)S(1)}, bf16[1024,256]{1,0:T(8,128)(2,1)}, u32[]{:S(2)}, u32[]{:S(2)}) collective-permute-start(bf16[1024,256]{1,0:T(8,128)(2,1)S(1)} %collective-permute-done.10.refs_10_), channel_id=1, source_target_pairs={{0,1},{1,2},{2,3},{3,4},{4,5},{5,6},{6,7},{7,0},{8,15},{9,8},{10,9... | collective-permute-start | bytes 1572872 | tf_op jit(solution)/shard_map/ppermute | solution.py:286
  136.4 33.5 %copy-start.11 = (bf16[1024,256]{1,0:T(8,128)(2,1)}, bf16[1024,256]{1,0:T(8,128)(2,1)S(1)}, u32[]{:S(2)}) copy-start(bf16[1024,256]{1,0:T(8,128)(2,1)S(1)} %collective-permute-done.11.refs_11_) | copy-start | bytes 1572868
  136.4 19.2 %collective-permute-start.13 = (bf16[1024,256]{1,0:T(8,128)(2,1)S(1)}, bf16[1024,256]{1,0:T(8,128)(2,1)}, u32[]{:S(2)}, u32[]{:S(2)}) collective-permute-start(bf16[1024,256]{1,0:T(8,128)(2,1)S(1)} %collective-permute-done.11.refs_11_), channel_id=1, source_target_pairs={{0,1},{1,2},{2,3},{3,4},{4,5},{5,6},{6,7},{7,0},{8,15},{9,8},{10,9... | collective-permute-start | bytes 1572872 | tf_op jit(solution)/shard_map/ppermute | solution.py:286
  150.0 19.9 %collective-permute-start.14 = (bf16[1024,256]{1,0:T(8,128)(2,1)}, bf16[1024,256]{1,0:T(8,128)(2,1)}, u32[]{:S(2)}, u32[]{:S(2)}) collective-permute-start(bf16[1024,256]{1,0:T(8,128)(2,1)} %collective-permute-done.12.refs_12_), channel_id=1, source_target_pairs={{0,1},{1,2},{2,3},{3,4},{4,5},{5,6},{6,7},{7,0},{8,15},{9,8},{10,9... | collective-permute-start | bytes 1572872 | tf_op jit(solution)/shard_map/ppermute | solution.py:286
  155.6 14.3 %collective-permute-start.15 = (bf16[1024,256]{1,0:T(8,128)(2,1)}, bf16[1024,256]{1,0:T(8,128)(2,1)}, u32[]{:S(2)}, u32[]{:S(2)}) collective-permute-start(bf16[1024,256]{1,0:T(8,128)(2,1)} %collective-permute-done.13.refs_13_), channel_id=1, source_target_pairs={{0,1},{1,2},{2,3},{3,4},{4,5},{5,6},{6,7},{7,0},{8,15},{9,8},{10,9... | collective-permute-start | bytes 1572872 | tf_op jit(solution)/shard_map/ppermute | solution.py:286
  164.1 15.8 %all-to-all-start.5 = ((bf16[32,64,128]{2,1,0:T(8,128)(2,1)}), bf16[32,64,128]{2,1,0:T(8,128)(2,1)S(1)}, u32[]{:S(2)}, u32[]{:S(2)}) async-start(bf16[32,64,128]{2,1,0:T(8,128)(2,1)} %get-tuple-element.12), calls=%async_computation.5 | async-start | bytes 1048576 | tf_op jit(solution)/shard_map/all_to_all | solution.py:22
  182.6 24.1 %all-to-all-start.6 = ((bf16[32,64,256]{2,1,0:T(8,128)(2,1)}), bf16[32,64,256]{2,1,0:T(8,128)(2,1)S(1)}, u32[]{:S(2)}, u32[]{:S(2)}) async-start(bf16[32,64,256]{2,1,0:T(8,128)(2,1)} %undone_copies.1), calls=%async_computation.6 | async-start | bytes 2097152 | tf_op jit(solution)/shard_map/all_to_all | solution.py:22
  (5 other events, 68.8 us)
Sparse Core Ops, SparseCore 0:
  27.6 56.6 all-gather.1
